TPU v7x, 256 devices: a whole 4x4x8 slice. The times are simulated.
256 devices in a mesh: seq: 64 (over x, z, core), var: 4 (over y).
Axes of the slice: x: 4, y: 4, z: 8, core: 2. Of those that a mesh axis runs over, the one named last changes fastest.
Arguments:
- clean_proj: bfloat16 [2048, 10240], P('seq'), may hold values from -8 to 8
- corrupt_proj: bfloat16 [2048, 10240], P('seq'), may hold values from -8 to 8
- patch_pos: int32 [4, 16], P('var'), may hold values from 0 to 2047
- patch_mode: int32 [4], P('var'), may hold values from 0 to 2
- a_log: float32 [16, 5120], replicated, may hold values from -6 to 1.5
- dt_bias: float32 [5120], replicated, may hold values from -6 to -2
- conv_weight: float32 [4, 5120], replicated, may hold values from -3 to 3
- conv_bias: float32 [5120], replicated, may hold values from -3 to 3
- x_weight: bfloat16 [5120, 192], replicated, may hold values from -0.078125 to 0.078125
- dt_weight: bfloat16 [160, 5120], replicated, may hold values from -0.5 to 0.5
- d_skip: float32 [5120], replicated, may hold values from 0.5 to 1.5
Outputs:
- patched_out: bfloat16 [4, 2048, 5120], P('var', 'seq')
- effect_peak: float32 [4, 5120], P('var')
Inputs may be any that keep to these rules, and one draw needn't show every extreme that they name: `patch_pos`: positions of one variant may repeat.
All inputs are finite; a program needn't handle non-finite values.
Results may differ from a plain program's by a relative error of at most 0.0029.
The roundings to bfloat16 on the way count: a program that leaves them out, or rounds other values in their place, can miss the bound.
Values may be sent and summed in bfloat16 or wider, within the bound.
A program may use at most 128 MiB of HBM per device.

v0:
```python
import jax
import jax.numpy as jnp
from jax import lax
from jax.sharding import Mesh
from jax.sharding import PartitionSpec as P

STATE = 16
RANK = 160
BLOCK = 8
SEQ = ("seq_0", "seq_1", "seq_2")


tiny_offset = 1e-06


def from_behind(value, axis, steps):
    count = lax.axis_size(axis)
    first, last = (max(0, -steps), min(count, count - steps))
    return lax.ppermute(value, axis, [(source, source + steps) for source in range(first, last)])


def filled_with(value, identity):
    return jax.tree.map(
        lambda part, zero: jnp.zeros_like(part) + jnp.asarray(zero, part.dtype), value, identity
    )


def gathered_once(value, axis):
    leaves = jax.tree.leaves(value)
    turns = sorted(range(len(leaves)), key=lambda k: -leaves[k].size)
    width = (1, *leaves[turns[0]].shape)[-1]
    lines = [
        jnp.pad(leaves[k].reshape(-1), (0, -leaves[k].size % width)).reshape(-1, width)
        for k in turns
    ]
    both, at, found = (lax.all_gather(jnp.concatenate(lines), axis), 0, {})
    for k, line in zip(turns, lines):
        share = both[:, at : at + len(line)].reshape(len(both), -1)
        found[k] = share[:, : leaves[k].size].reshape(-1, *leaves[k].shape)
        at += len(line)
    numbers = iter(range(len(leaves)))
    return jax.tree.map(lambda _: found[next(numbers)], value)


def carried_in(value, axes, combine, identity):
    before = start = filled_with(value, identity)
    total = value
    for axis in reversed(axes):
        size, place = (lax.axis_size(axis), lax.axis_index(axis))
        pieces = gathered_once(total, axis)
        inside, total = (start, start)
        for k in range(size):
            passed = k < place
            total = combine(total, jax.tree.map(lambda part: part[k], pieces))
            inside = jax.tree.map(lambda new, old: jnp.where(passed, new, old), total, inside)
        before = combine(inside, before)
    return before


def from_everyone(value, axis):
    size = lax.axis_size(axis)
    return lax.all_to_all(
        jnp.broadcast_to(value[None], (size, *value.shape)), axis, 0, 0, tiled=True
    )


def laid_out(parts, dim):
    parts = jnp.moveaxis(parts, 0, dim)
    lengths = parts.shape
    return parts.reshape(*lengths[:dim], lengths[dim] * lengths[dim + 1], *lengths[dim + 2 :])


def gather_directly(value, axis, dim):
    parts = from_everyone(value, axis)
    return laid_out(parts, dim)


def joined_all(value, axes, combine):
    for axis in axes:
        pieces = jax.tree.map(lambda part: lax.all_gather(part, axis), value)
        value = jax.tree.map(lambda part: part[0], pieces)
        for k in range(1, lax.axis_size(axis)):
            value = combine(value, jax.tree.map(lambda part: part[k], pieces))
    return value


def prepare(signal_rows, rim_rows, conv_weight, conv_bias, x_weight):
    row_count = signal_rows.shape[0]
    kernel = conv_weight.shape[0]
    padded = jnp.concatenate([rim_rows, signal_rows], axis=0).astype(jnp.float32)
    conv_sum = conv_bias[None, :] + conv_weight[0][None, :] * padded[0:row_count]
    for lag_index in range(1, kernel):
        conv_sum = (
            conv_sum + conv_weight[lag_index][None, :] * padded[lag_index : lag_index + row_count]
        )
    conv_act = lax.optimization_barrier(jax.nn.silu(conv_sum).astype(jnp.bfloat16))
    projected = jnp.dot(conv_act, x_weight, preferred_element_type=jnp.float32)
    low_rank = projected[:, :RANK].astype(jnp.bfloat16)
    input_map = projected[:, RANK : RANK + STATE]
    output_map = projected[:, RANK + STATE :]
    return (conv_act, low_rank, input_map, output_map)


def channels(parts, gate_rows, offset, span, a_log, dt_bias, dt_weight, d_skip):
    conv_act, low_rank, input_map, output_map = parts
    signal_f = lax.dynamic_slice_in_dim(conv_act, offset, span, 1).astype(jnp.float32)
    weight_cut = lax.dynamic_slice_in_dim(dt_weight, offset, span, 1)
    bias_cut = lax.dynamic_slice_in_dim(dt_bias, offset, span, 0)
    step_size = jax.nn.softplus(
        jnp.dot(low_rank, weight_cut, preferred_element_type=jnp.float32) + bias_cut[None, :]
    )
    decay_rates = jnp.exp(lax.dynamic_slice_in_dim(a_log, offset, span, 1))
    gate_act = jax.nn.silu(lax.dynamic_slice_in_dim(gate_rows, offset, span, 1).astype(jnp.float32))
    skip_cut = lax.dynamic_slice_in_dim(d_skip, offset, span, 0)
    return (step_size, signal_f, input_map, output_map, decay_rates, gate_act, skip_cut)


def local_pass(terms):
    step_size, signal_f, input_map, output_map, decay_rates, gate_act, skip_cut = terms
    row_count, span = step_size.shape
    blocks = row_count // BLOCK
    inflow = step_size * signal_f
    pieces = (
        step_size.reshape(blocks, BLOCK, span),
        inflow.reshape(blocks, BLOCK, span),
        input_map.reshape(blocks, BLOCK, STATE),
        output_map.reshape(blocks, BLOCK, STATE),
    )

    def advance(state, block_rows):
        steps, flows, b_rows, c_rows = block_rows
        outputs = []
        for row in range(BLOCK):
            state = (
                jnp.exp(-steps[row][None, :] * decay_rates) * state
                + flows[row][None, :] * b_rows[row][:, None]
            )
            outputs.append(jnp.sum(c_rows[row][:, None] * state, axis=0))
        return (state, jnp.stack(outputs))

    end_state, readout = lax.scan(advance, jnp.zeros((STATE, span), jnp.float32), pieces)
    running = jnp.cumsum(step_size, axis=0)
    return (readout.reshape(row_count, span), running, end_state)


def make_chain(rate_list):

    def chain(earlier, later):
        joined = ()
        for member, rates in enumerate(rate_list):
            early_first, early_state = (earlier[2 * member], earlier[2 * member + 1])
            late_first, late_state = (later[2 * member], later[2 * member + 1])
            joined = joined + (early_first * late_first, late_first * early_state + late_state)
        return joined

    return chain


def finish(terms, local_readout, running, incoming):
    step_size, signal_f, input_map, output_map, decay_rates, gate_act, skip_cut = terms
    readout = local_readout
    for entry in range(STATE):
        entering = jnp.exp(-decay_rates[entry][None, :] * running)
        readout = readout + output_map[:, entry : entry + 1] * entering * incoming[entry][None, :]
    return ((readout + skip_cut[None, :] * signal_f) * gate_act).astype(jnp.bfloat16)


def combine_stats(first_pair, second_pair):
    return (jnp.maximum(first_pair[0], second_pair[0]), first_pair[1] + second_pair[1])


def shards(
    clean_proj,
    corrupt_proj,
    patch_pos,
    patch_mode,
    a_log,
    dt_bias,
    conv_weight,
    conv_bias,
    x_weight,
    dt_weight,
    d_skip,
):
    row_count = clean_proj.shape[0]
    inner_dim = conv_weight.shape[1]
    margin = conv_weight.shape[0] - 1
    first_row = lax.axis_index(SEQ) * row_count
    positions = first_row + jnp.arange(row_count, dtype=jnp.int32)
    rim_positions = first_row - margin + jnp.arange(margin, dtype=jnp.int32)
    targets = patch_pos[0]
    chosen_mode = patch_mode[0]
    hits_here = jnp.any(positions[:, None] == targets[None, :], axis=1)
    hits_rim = jnp.any(rim_positions[:, None] == targets[None, :], axis=1)
    take_signal = hits_here & (chosen_mode != 1)
    take_gate = hits_here & (chosen_mode != 0)
    rim_signal = hits_rim & (chosen_mode != 1)
    clean_signal = clean_proj[:, :inner_dim]
    corrupt_signal = corrupt_proj[:, :inner_dim]
    clean_gate = clean_proj[:, inner_dim:]
    corrupt_gate = corrupt_proj[:, inner_dim:]
    tails = jnp.stack([clean_signal[row_count - margin :], corrupt_signal[row_count - margin :]])
    rims = from_behind(tails, SEQ, 1)
    patched_signal = jnp.where(take_signal[:, None], clean_signal, corrupt_signal)
    patched_gate = jnp.where(take_gate[:, None], clean_gate, corrupt_gate)
    patched_rim = jnp.where(rim_signal[:, None], rims[0], rims[1])
    clean_front = prepare(clean_signal, rims[0], conv_weight, conv_bias, x_weight)
    corrupt_front = prepare(corrupt_signal, rims[1], conv_weight, conv_bias, x_weight)
    patched_front = prepare(patched_signal, patched_rim, conv_weight, conv_bias, x_weight)
    span = inner_dim // lax.axis_size("var")
    offset = lax.axis_index("var") * span
    clean_terms = channels(clean_front, clean_gate, offset, span, a_log, dt_bias, dt_weight, d_skip)
    corrupt_terms = channels(
        corrupt_front, corrupt_gate, offset, span, a_log, dt_bias, dt_weight, d_skip
    )
    patched_terms = channels(
        patched_front, patched_gate, 0, inner_dim, a_log, dt_bias, dt_weight, d_skip
    )
    run_terms = (clean_terms, corrupt_terms, patched_terms)
    locals_list = []
    summaries = ()
    identity = ()
    for terms in run_terms:
        local_readout, running, end_state = local_pass(terms)
        locals_list.append((local_readout, running))
        last_total = running[running.shape[0] - 1]
        summaries = summaries + (jnp.exp(-terms[4] * last_total[None, :]), end_state)
        identity = identity + (jnp.ones_like(end_state), jnp.zeros_like(end_state))
    chain = make_chain([terms[4] for terms in run_terms])
    incoming = carried_in(summaries, SEQ, chain, identity)
    clean_cut = finish(clean_terms, locals_list[0][0], locals_list[0][1], incoming[1])
    corrupt_cut = finish(corrupt_terms, locals_list[1][0], locals_list[1][1], incoming[3])
    patched_rows = finish(patched_terms, locals_list[2][0], locals_list[2][1], incoming[5])
    corrupt_whole = gather_directly(corrupt_cut, "var", 1)
    clean_cut, corrupt_cut, corrupt_whole, patched_rows = lax.optimization_barrier(
        (clean_cut, corrupt_cut, corrupt_whole, patched_rows)
    )
    sum_squares = jnp.sum(
        (clean_cut.astype(jnp.float32) - corrupt_cut.astype(jnp.float32)) ** 2, axis=0
    )
    peak = jnp.max(
        jnp.abs(patched_rows.astype(jnp.float32) - corrupt_whole.astype(jnp.float32)), axis=0
    )
    peak_all, squares_all = joined_all((peak, sum_squares), SEQ, combine_stats)
    squares_all = gather_directly(squares_all, "var", 0)
    spread = jnp.sqrt(squares_all / (row_count * lax.axis_size(SEQ)) + tiny_offset)
    return (patched_rows[None], (peak_all / spread)[None])


def solution(mesh):
    finer = Mesh(
        mesh.devices.reshape(4, 8, 2, mesh.shape["var"]), ("seq_0", "seq_1", "seq_2", "var")
    )
    return jax.shard_map(
        shards,
        mesh=finer,
        in_specs=(
            P(SEQ, None),
            P(SEQ, None),
            P("var", None),
            P("var"),
            P(),
            P(),
            P(),
            P(),
            P(),
            P(),
            P(),
        ),
        out_specs=(P("var", SEQ, None), P("var", None)),
        check_vma=False,
    )
```

profile of v0, /device:TPU:1, one launch (start us, length us, event | category | flops | bytes accessed | tf_op | source)
XLA Modules:
  0.0 420.3 jit_solution(4457055104572301700)
XLA Ops:
  9.9 4.9 %collective-permute-start = (bf16[2,3,5120]{2,1,0:T(4,128)(2,1)}, bf16[2,3,5120]{2,1,0:T(4,128)(2,1)S(1)}, u32[]{:S(2)}, u32[]{:S(2)}) collective-permute-start(bf16[2,3,5120]{2,1,0:T(4,128)(2,1)} %pad_maximum_fusion), channel_id=1, source_target_pairs={{0,4},{4,8},{8,12},{12,16},{16,20},{20,24},{24,28},{28,32},{32,36}... | collective-permute-start | bytes 184328 | tf_op jit(solution)/shard_map/ppermute | solution.py:19
  16.8 2.2 fusion.182
  32.8 11.2 %while.41 = (s32[]{:T(128)}, f32[16,1280]{1,0:T(8,128)S(1)}, f32[4,8,1280]{2,1,0:T(8,128)}, f32[4,8,1280]{2,1,0:T(8,128)S(1)}, f32[16,1280]{1,0:T(8,128)S(1)}, /...) while((s32[]{:T(128)}, f32[16,1280]{1,0:T(8,128)S(1)}, ...), condition=%wide.region_34.35_spmd.clone, body=%wide.region_25.34_spmd.clone.sunk | while | flops 1433610 | bytes 1572960 | solution.py:141
  44.7 2.0 fusion.19
  46.7 1.7 reduce_window_sum.29
  49.2 1.8 fusion.184
  51.0 33.7 %while.40 = (s32[]{:T(128)}, f32[16,5120]{1,0:T(8,128)S(1)}, f32[4,8,5120]{2,1,0:T(8,128)}, f32[4,8,5120]{2,1,0:T(8,128)}, f32[16,5120]{1,0:T(8,128)S(1)}, /*ind...) while((s32[]{:T(128)}, f32[16,5120]{1,0:T(8,128)S(1)}, ...), condition=%wide.region_23.24_spmd.clone, body=%wide.region_14.23_spmd.clone.sunk | while | flops 5734410 | bytes 6029660 | solution.py:141
  51.0 2.4 dynamic-slice_negate_fusion.25
  55.4 2.0 multiply_reduce_fusion.37
  59.3 3.0 dynamic-slice_negate_fusion.25
  64.2 2.0 multiply_reduce_fusion.37
  68.1 2.5 dynamic-slice_negate_fusion.25
  72.6 2.0 multiply_reduce_fusion.37
  76.5 2.4 dynamic-slice_negate_fusion.25
  80.9 2.0 multiply_reduce_fusion.37
  85.4 24.8 %while.39 = (s32[]{:T(128)}, f32[16,1280]{1,0:T(8,128)S(1)}, f32[4,8,1280]{2,1,0:T(8,128)}, f32[4,8,1280]{2,1,0:T(8,128)}, f32[16,1280]{1,0:T(8,128)S(1)}, /*ind...) while((s32[]{:T(128)}, f32[16,1280]{1,0:T(8,128)S(1)}, ...), condition=%wide.region_9.10_spmd.clone, body=%wide.region_0.9_spmd.clone.sunk | while | flops 1433610 | bytes 1572960 | solution.py:141
  85.4 1.8 dynamic-slice_reduce_fusion.18
  91.6 1.7 dynamic-slice_reduce_fusion.18
  97.9 1.7 dynamic-slice_reduce_fusion.18
  104.0 1.8 dynamic-slice_reduce_fusion.18
  110.3 1.7 reduce_window_sum.28
  112.9 3.9 concatenate.21
  116.9 18.1 %all-gather.14.cloned.1.call-done = f32[96,5120]{1,0:T(8,128)} async-done(((f32[48,5120]{1,0:T(8,128)}), f32[96,5120]{1,0:T(8,128)}) %all-gather.14.cloned.1.call-update) | async-done | bytes 1966096 | tf_op jit(solution)/shard_map/all_gather | solution.py:36
  137.9 3.1 concatenate.22
  141.2 89.5 %all-gather.16.cloned.1.call-done = f32[384,5120]{1,0:T(8,128)} async-done(((f32[48,5120]{1,0:T(8,128)}), f32[384,5120]{1,0:T(8,128)}) %all-gather.16.cloned.1.call-update) | async-done | bytes 7864336 | tf_op jit(solution)/shard_map/all_gather | solution.py:36
  230.7 3.7 fusion.59
  234.4 3.0 fusion.76
  237.9 3.9 concatenate.23
  252.6 3.4 fusion.179
  267.0 2.6 fusion.180
  273.6 1.6 squeeze.485
  297.1 2.1 fusion.125
  299.2 2.1 fusion.126
  301.4 4.0 fusion.58
  307.6 1.6 add_add_fusion
  309.8 1.7 fusion.84
  312.2 4.0 all-to-all-start
  318.1 1.8 add_add_fusion.1
  320.6 4.6 %fusion.22 = bf16[32,5120]{1,0:T(8,128)(2,1)} fusion(bf16[32,5120]{1,0:T(8,128)(2,1)S(1)} %copy-done.3, f32[4,8,5120]{2,1,0:T(8,128)} %get-tuple-element.140, f32[32,5120]{1,0:T(8,128)S(1)} %copy-done.15, f32[5120]{0:T(1024)} %param.27, f32[5120]{0:T(1024)S(1)} %bitcast.924, f32[5120]{0:T(1024)S(1)} %bitcast.922, f32[32]{0:T(128)} %get-tuple-element.328, ...), kind=kLoop, calls=%fused_computation.183 | loop fusion | flops 12288000 | bytes 3299360 | tf_op jit(solution)/shard_map/convert_element_type | solution.py:165
  325.2 1.9 fusion.80
  327.3 9.7 %all-gather.3 = f32[20480]{0:T(1024)S(1)} all-gather(f32[5120]{0:T(1024)S(1)} %abs_reduce_fusion), channel_id=5, replica_groups=mesh['seq_0'=4,'seq_1'=8,'seq_2'=2,'var'=4] {'seq_0'}, dimensions={0}, use_global_device_ids=true | all-gather | bytes 102400 | tf_op jit(solution)/shard_map/all_gather | solution.py:80
  337.0 18.3 %all-gather.5 = f32[8,1,5120]{2,1,0:T(1,128)S(1)} all-gather(f32[1,1,5120]{2,1,0:T(1,128)S(1)} %bitcast.905), channel_id=1, replica_groups=mesh['seq_0'=4,'seq_1'=8,'seq_2'=2,'var'=4] {'seq_1'}, dimensions={0}, use_global_device_ids=true | all-gather | bytes 184320 | tf_op jit(solution)/shard_map/all_gather | solution.py:80
  355.3 9.5 %all-gather.7 = f32[4,1,1280]{2,1,0:T(1,128)S(1)} all-gather(f32[1,1,1280]{2,1,0:T(1,128)S(1)} %reshape.841), channel_id=6, replica_groups=mesh['seq_0'=4,'seq_1'=8,'seq_2'=2,'var'=4] {'seq_0'}, dimensions={0}, use_global_device_ids=true | all-gather | bytes 25600 | tf_op jit(solution)/shard_map/all_gather | solution.py:80
  364.8 18.4 %all-gather.8 = f32[8,1,1280]{2,1,0:T(1,128)S(1)} all-gather(f32[1,1,1280]{2,1,0:T(1,128)S(1)} %slice_add_fusion.16), channel_id=1, replica_groups=mesh['seq_0'=4,'seq_1'=8,'seq_2'=2,'var'=4] {'seq_1'}, dimensions={0}, use_global_device_ids=true | all-gather | bytes 46080 | tf_op jit(solution)/shard_map/all_gather | solution.py:80
  383.2 20.3 %all-gather.9 = f32[2,1,1280]{2,1,0:T(1,128)S(1)} all-gather(f32[1,1,1280]{2,1,0:T(1,128)S(1)} %fusion.153), channel_id=1, replica_groups=mesh['seq_0'=4,'seq_1'=8,'seq_2'=2,'var'=4] {'seq_2'}, dimensions={0}, use_global_device_ids=true | all-gather | bytes 15360 | tf_op jit(solution)/shard_map/all_gather | solution.py:80
  404.2 4.6 %all-to-all-start.1 = ((f32[4,1,1280]{2,1,0:T(1,128)}), f32[4,1,1280]{2,1,0:T(1,128)S(1)}, u32[]{:S(2)}, u32[]{:S(2)}) async-start(f32[4,1,1280]{2,1,0:T(1,128)} %broadcast_in_dim.75), calls=%async_computation.1 | async-start | bytes 40960 | tf_op jit(solution)/shard_map/all_to_all | solution.py:62
  408.9 2.1 all-gather.6
  411.0 2.0 all-to-all-done.1
  (559 shorter events, 121.7 us)
Async XLA Ops:
  7.2 15.4 %copy-start = (bf16[5120,192]{0,1:T(8,128)(2,1)S(1)}, bf16[5120,192]{0,1:T(8,128)(2,1)}, u32[]{:S(2)}) copy-start(bf16[5120,192]{0,1:T(8,128)(2,1)} %param.25) | copy-start | bytes 5898244
  7.2 11.8 %copy-start.105 = (s32[1,16]{1,0:T(1,128)S(1)}, s32[1,16]{1,0:T(1,128)}, u32[]{:S(2)}) copy-start(s32[1,16]{1,0:T(1,128)} %param.19) | copy-start | bytes 196
  7.2 12.0 %copy-start.30 = (f32[4,5120]{1,0:T(4,128)S(1)}, f32[4,5120]{1,0:T(4,128)}, u32[]{:S(2)}) copy-start(f32[4,5120]{1,0:T(4,128)} %param.23) | copy-start | bytes 245764
  7.2 127.8 %all-gather.14.cloned.1.call-start = ((), (), s32[]{:S(2)}) async-start(), calls=%async_computation.2 | async-start | bytes 2949120 | tf_op jit(solution)/shard_map/all_gather | solution.py:36
  9.9 10.9 %collective-permute-start = (bf16[2,3,5120]{2,1,0:T(4,128)(2,1)}, bf16[2,3,5120]{2,1,0:T(4,128)(2,1)S(1)}, u32[]{:S(2)}, u32[]{:S(2)}) collective-permute-start(bf16[2,3,5120]{2,1,0:T(4,128)(2,1)} %pad_maximum_fusion), channel_id=1, source_target_pairs={{0,4},{4,8},{8,12},{12,16},{16,20},{20,24},{24,28},{28,32},{32,36}... | collective-permute-start | bytes 184328 | tf_op jit(solution)/shard_map/ppermute | solution.py:19
  22.5 5.7 %copy-start.8 = (bf16[32,5120]{1,0:T(8,128)(2,1)}, bf16[32,5120]{1,0:T(8,128)(2,1)S(1)}, u32[]{:S(2)}) copy-start(bf16[32,5120]{1,0:T(8,128)(2,1)S(1)} %get-tuple-element.624) | copy-start | bytes 983044
  22.5 5.6 %copy-start.9 = (bf16[32,5120]{1,0:T(8,128)(2,1)}, bf16[32,5120]{1,0:T(8,128)(2,1)S(1)}, u32[]{:S(2)}) copy-start(bf16[32,5120]{1,0:T(8,128)(2,1)S(1)} %get-tuple-element.623) | copy-start | bytes 983044
  22.5 22.1 %copy-start.2 = (bf16[32,5120]{1,0:T(8,128)(2,1)}, bf16[32,5120]{1,0:T(8,128)(2,1)S(1)}, u32[]{:S(2)}) copy-start(bf16[32,5120]{1,0:T(8,128)(2,1)S(1)} %get-tuple-element.622) | copy-start | bytes 983044
  27.5 5.3 %copy-start.7 = (f32[32,1280]{1,0:T(8,128)}, f32[32,1280]{1,0:T(8,128)S(1)}, u32[]{:S(2)}) copy-start(f32[32,1280]{1,0:T(8,128)S(1)} %compare_select_fusion.2) | copy-start | bytes 491524
  85.4 27.5 %copy-start.19 = (f32[16,1280]{1,0:T(8,128)S(1)}, f32[16,1280]{1,0:T(8,128)}, u32[]{:S(2)}) copy-start(f32[16,1280]{1,0:T(8,128)} %get-tuple-element.439) | copy-start | bytes 245764
  85.4 27.5 %copy-start.11 = (f32[16,5120]{1,0:T(8,128)S(1)}, f32[16,5120]{1,0:T(8,128)}, u32[]{:S(2)}) copy-start(f32[16,5120]{1,0:T(8,128)} %get-tuple-element.621) | copy-start | bytes 983044
  116.8 113.9 %all-gather.16.cloned.1.call-start = ((), (), s32[]{:S(2)}) async-start(), calls=%async_computation.3 | async-start | bytes 8847360 | tf_op jit(solution)/shard_map/all_gather | solution.py:36
  136.3 4.7 %copy-start.4 = (f32[16,5120]{1,0:T(8,128)}, f32[16,5120]{1,0:T(8,128)S(1)}, u32[]{:S(2)}) copy-start(f32[16,5120]{1,0:T(8,128)S(1)} %get-tuple-element.582) | copy-start | bytes 983044
  141.0 156.1 %all-gather.18.cloned.1.call-start = ((), (), s32[]{:S(2)}) async-start(), calls=%async_computation.4 | async-start | bytes 4915200 | tf_op jit(solution)/shard_map/all_gather | solution.py:36
  230.7 6.7 %copy-start.1 = (f32[384,5120]{1,0:T(8,128)S(1)}, f32[384,5120]{1,0:T(8,128)}, u32[]{:S(2)}) copy-start(f32[384,5120]{1,0:T(8,128)} %all-gather.16.cloned.1.call-done) | copy-start | bytes 23592964
  273.6 27.7 %copy-start.5 = (f32[16,5120]{1,0:T(8,128)S(1)}, f32[16,5120]{1,0:T(8,128)}, u32[]{:S(2)}) copy-start(f32[16,5120]{1,0:T(8,128)} %copy-done.4) | copy-start | bytes 983044
  273.6 27.7 %copy-start.10 = (f32[16,5120]{1,0:T(8,128)S(1)}, f32[16,5120]{1,0:T(8,128)}, u32[]{:S(2)}) copy-start(f32[16,5120]{1,0:T(8,128)} %get-tuple-element.436) | copy-start | bytes 983044
  305.4 4.0 copy-start.22
  305.4 4.0 copy-start.24
  305.4 4.0 copy-start.70
  305.4 4.0 copy-start.72
  305.4 4.0 copy-start.73
  305.4 4.0 copy-start.74
  305.5 4.0 copy-start.75
  305.5 4.0 copy-start.76
  305.5 4.0 copy-start.77
  305.5 4.0 copy-start.78
  305.5 4.0 copy-start.79
  305.5 4.0 copy-start.80
  305.5 4.0 copy-start.81
  305.5 4.0 copy-start.82
  305.5 4.0 copy-start.83
  305.5 4.0 copy-start.84
  305.6 4.0 copy-start.85
  305.6 4.0 copy-start.86
  305.6 4.0 copy-start.88
  305.6 4.0 copy-start.89
  305.6 4.0 copy-start.90
  307.6 10.3 %copy-start.16 = (f32[16,1280]{1,0:T(8,128)S(1)}, f32[16,1280]{1,0:T(8,128)}, u32[]{:S(2)}) copy-start(f32[16,1280]{1,0:T(8,128)} %squeeze.431) | copy-start | bytes 245764
  307.6 10.2 %copy-start.17 = (f32[16,1280]{1,0:T(8,128)S(1)}, f32[16,1280]{1,0:T(8,128)}, u32[]{:S(2)}) copy-start(f32[16,1280]{1,0:T(8,128)} %squeeze.492) | copy-start | bytes 245764
  311.5 8.7 %copy-start.3 = (bf16[32,5120]{1,0:T(8,128)(2,1)S(1)}, bf16[32,5120]{1,0:T(8,128)(2,1)}, u32[]{:S(2)}) copy-start(bf16[32,5120]{1,0:T(8,128)(2,1)} %copy-done.2) | copy-start | bytes 983044
  311.5 8.7 %copy-start.12 = (bf16[32,10240]{1,0:T(8,128)(2,1)S(1)}, bf16[32,10240]{1,0:T(8,128)(2,1)}, u32[]{:S(2)}) copy-start(bf16[32,10240]{1,0:T(8,128)(2,1)} %param.18) | copy-start | bytes 1966084
  312.2 14.9 %all-to-all-start = ((bf16[4,32,1280]{2,1,0:T(8,128)(2,1)}), bf16[4,32,1280]{2,1,0:T(8,128)(2,1)S(1)}, u32[]{:S(2)}, u32[]{:S(2)}) async-start(bf16[4,32,1280]{2,1,0:T(8,128)(2,1)} %broadcast_in_dim.71), calls=%async_computation | async-start | bytes 655360 | tf_op jit(solution)/shard_map/all_to_all | solution.py:62
  320.5 4.6 %copy-start.23 = (f32[32,1280]{1,0:T(8,128)S(1)}, f32[32,1280]{1,0:T(8,128)}, u32[]{:S(2)}) copy-start(f32[32,1280]{1,0:T(8,128)} %reduce_window_sum.28) | copy-start | bytes 491524
  320.5 4.6 %copy-start.25 = (f32[4,8,1280]{2,1,0:T(8,128)S(1)}, f32[4,8,1280]{2,1,0:T(8,128)}, u32[]{:S(2)}) copy-start(f32[4,8,1280]{2,1,0:T(8,128)} %get-tuple-element.135) | copy-start | bytes 491524
  320.6 4.6 %copy-start.71 = (f32[1280]{0:T(1024)S(1)}, f32[1280]{0:T(1024)}, u32[]{:S(2)}) copy-start(f32[1280]{0:T(1024)} %get-tuple-element.295) | copy-start | bytes 15364
  325.1 30.2 %copy-start.21 = (bf16[32,1280]{1,0:T(8,128)(2,1)S(1)}, bf16[32,1280]{1,0:T(8,128)(2,1)}, u32[]{:S(2)}) copy-start(bf16[32,1280]{1,0:T(8,128)(2,1)} %copy-done.20) | copy-start | bytes 245764
  404.2 8.9 %all-to-all-start.1 = ((f32[4,1,1280]{2,1,0:T(1,128)}), f32[4,1,1280]{2,1,0:T(1,128)S(1)}, u32[]{:S(2)}, u32[]{:S(2)}) async-start(f32[4,1,1280]{2,1,0:T(1,128)} %broadcast_in_dim.75), calls=%async_computation.1 | async-start | bytes 40960 | tf_op jit(solution)/shard_map/all_to_all | solution.py:62
  (91 other events, 220.0 us)
Sparse Core Ops, SparseCore 0:
  116.9 17.9 all-gather.13
  141.1 89.5 all-gather.15
  241.9 47.1 all-gather.17
where the time goes:
time: 424 us; the launch traced here: 420 us
  waiting for transfers between devices  110 us (26%)
  local copies, waits for them, and re-layouts  104 us (25%)
  other arithmetic  92.6 us (22%)
  blocking collectives  78.3 us (18%)
  between operations  16.1 us (4%)
  starting transfers between devices  13.9 us (3%)
    all_gather x3, waiting for transfers between devices, gathered_once(): both, at, found = (lax.all_gather(jnp.concatenate(lines), axis), 0, {})  108 us
    all_gather x6, blocking collectives, joined_all(): pieces = jax.tree.map(lambda part: lax.all_gather(part, axis), value)  78.3 us
    squeeze x40, local copies, waits for them, and re-layouts, carried_in(): total = combine(total, jax.tree.map(lambda part: part[k], pieces))  41.9 us
    reduce_sum x36, other arithmetic, advance(): outputs.append(jnp.sum(c_rows[row][:, None] * state, axis=0))  20.3 us
    add x8, other arithmetic, chain(): late_first * early_state + late_state  14.5 us
    slice x8, other arithmetic, advance(): flows[row][None, :] * b_rows[row][:, None]  12.8 us
    concatenate x3, local copies, waits for them, and re-layouts, gathered_once(): both, at, found = (lax.all_gather(jnp.concatenate(lines), axis), 0, {})  10.8 us
    neg x4, other arithmetic, advance(): -steps[row][None, :] * decay_rates  10.4 us
  transfers between devices with their start and end apart: 6, of which 3 were waited for; matrix products, arithmetic and copies ran while one was open for 17% of the time, Pallas kernels for 0%

commit v1 on v0

v1 whole, which is shorter than its diff:
```python
import functools

import jax
import jax.numpy as jnp
from jax import lax
from jax.experimental import pallas as pl
from jax.experimental.pallas import tpu as pltpu
from jax.sharding import PartitionSpec as P

STATE = 16
RANK = 160
ROWS = 32
INNER = 5120
SPAN = 1280
TAPS = 4
LANES = 128
CHUNKS = 64
SHARDS = 64
VARS = 4
TILES = INNER // LANES
CUT_TILES = SPAN // LANES
GROUPS = CHUNKS // 8
MESH = pl.DeviceIdType.MESH
LOG2E = 1.4426950408889634
TINY = 1e-06
F32 = jnp.float32
BF16 = jnp.bfloat16
LINK = jnp.float32
CLEAN, CORRUPT, PATCHED = 0, 1, 2


def cut_slot(run, tile):
    if tile < 8:
        return TILES + 8 * run + tile
    return 56 + 2 * run + (tile - 8)


def hit_rows(pos_ref, first, count):
    rows = first + lax.broadcasted_iota(jnp.int32, (count, LANES), 0)
    hits = rows == pos_ref[0, 0]
    for k in range(1, pos_ref.shape[1]):
        hits = hits | (rows == pos_ref[0, k])
    return hits


def silu(value):
    return value / (1.0 + jnp.exp(-value))


def softplus(value):
    return jnp.maximum(value, 0.0) + jnp.log1p(jnp.exp(-jnp.abs(value)))


def row_of(ref, row):
    return jnp.broadcast_to(ref[pl.ds(row, 1), :], (8, LANES))


def scan_group(dts, us, rate, group, state, drive, readout, out):
    def step(t, carry):
        row = pl.multiple_of(t * CHUNKS + group * 8, 8)
        steps = dts[pl.ds(row, 8), :]
        flow = us[pl.ds(row, 8), :]
        entries = []
        total = None
        for n in range(STATE):
            decay = jnp.exp2(steps * rate[n])
            entry = decay * carry[n] + flow * drive(t, n)
            entries.append(entry)
            if readout is not None:
                term = readout(t, n) * entry
                total = term if total is None else total + term
        if readout is not None:
            out[pl.ds(row, 8), :] = total
            return tuple(entries)
        return (*entries, carry[STATE] + steps)

    return lax.fori_loop(0, ROWS, step, state)


def splat_reader(ref, base):
    return lambda t, n: row_of(ref, base + t * STATE + n)


def mixed_reader(ref):
    first = lax.broadcasted_iota(jnp.int32, (8, LANES), 0) < 2

    def read(t, n):
        return jnp.where(
            first,
            row_of(ref, CLEAN * ROWS * STATE + t * STATE + n),
            row_of(ref, CORRUPT * ROWS * STATE + t * STATE + n),
        )

    return read


def front_kernel(
    pos, mode, clean, corrupt, rims, conv_w, conv_b, x_w, dt_w, dt_b, a_log,
    ends, totals, rates, dts, us, bs, cs, acts, pad, low,
):
    v = lax.axis_index("var")
    first = lax.axis_index("seq") * ROWS
    take = hit_rows(pos, first, ROWS)[:, :1] & (mode[0] != 1)
    take_rim = hit_rows(pos, first - 8, 8)[:, :1] & (mode[0] != 1)

    width = 512

    def conv(i, _):
        cols = pl.ds(pl.multiple_of(i * width, width), width)
        sig_clean = clean[:, cols].astype(F32)
        sig_corrupt = corrupt[:, cols].astype(F32)
        rim_clean = rims[0, :, cols].astype(F32)
        rim_corrupt = rims[1, :, cols].astype(F32)
        pieces = (
            (rim_clean, sig_clean),
            (rim_corrupt, sig_corrupt),
            (
                jnp.where(take_rim, rim_clean, rim_corrupt),
                jnp.where(take, sig_clean, sig_corrupt),
            ),
        )
        bias = conv_b[:, cols]
        for run, (rim, sig) in enumerate(pieces):
            pad[run, 0:8, :] = rim
            pad[run, 8:, :] = sig
            total = bias + conv_w[0:1, cols] * pad[run, 5 : 5 + ROWS, :]
            for k in range(1, TAPS):
                total = total + conv_w[k : k + 1, cols] * pad[run, 5 + k : 5 + k + ROWS, :]
            acts[run * ROWS : (run + 1) * ROWS, cols] = silu(total).astype(BF16)
        return 0

    lax.fori_loop(0, INNER // width, conv, 0)

    projected = jnp.dot(acts[...], x_w[...], preferred_element_type=F32)
    low[...] = projected[:, :RANK].astype(BF16)
    for run in range(3):
        mine = projected[run * ROWS : (run + 1) * ROWS]
        for n in range(STATE):
            at = run * ROWS * STATE + n
            bs[pl.ds(at, ROWS, stride=STATE), :] = jnp.broadcast_to(
                mine[:, RANK + n : RANK + n + 1], (ROWS, LANES)
            )
            cs[pl.ds(at, ROWS, stride=STATE), :] = jnp.broadcast_to(
                mine[:, RANK + STATE + n : RANK + STATE + n + 1], (ROWS, LANES)
            )

    def place(slot, steps, act, log_rate):
        dts[pl.ds(slot, ROWS, stride=CHUNKS), :] = steps
        us[pl.ds(slot, ROWS, stride=CHUNKS), :] = steps * act
        at = (slot // 8) * (STATE * 8) + slot % 8
        rates[pl.ds(at, STATE, stride=8), :] = jnp.exp(log_rate) * (-LOG2E)

    wide = 640

    def patched_steps(i, _):
        start = pl.multiple_of(i * wide, wide)
        cols = pl.ds(start, wide)
        raw = jnp.dot(low[2 * ROWS :, :], dt_w[:, cols], preferred_element_type=F32)
        steps = softplus(raw + dt_b[:, cols])
        act = acts[2 * ROWS :, cols].astype(F32)
        logs = a_log[:, cols]
        for k in range(wide // LANES):
            part = slice(k * LANES, (k + 1) * LANES)
            place(i * (wide // LANES) + k, steps[:, part], act[:, part], logs[:, part])
        return 0

    lax.fori_loop(0, INNER // wide, patched_steps, 0)

    cols = pl.ds(pl.multiple_of(v * SPAN, LANES), SPAN)
    raw = jnp.dot(low[: 2 * ROWS, :], dt_w[:, cols], preferred_element_type=F32)
    steps = softplus(raw + dt_b[:, cols])
    act = acts[: 2 * ROWS, cols].astype(F32)
    logs = a_log[:, cols]
    for run in (CLEAN, CORRUPT):
        rows = slice(run * ROWS, (run + 1) * ROWS)
        for tile in range(CUT_TILES):
            part = slice(tile * LANES, (tile + 1) * LANES)
            place(cut_slot(run, tile), steps[rows, part], act[rows, part], logs[:, part])
    blank = jnp.zeros((ROWS, LANES), F32)
    for slot in range(60, CHUNKS):
        place(slot, blank, blank, jnp.zeros((STATE, LANES), F32))

    zero = jnp.zeros((8, LANES), F32)

    def one_group(group, drive):
        base = group * (STATE * 8)
        rate = [rates[pl.ds(pl.multiple_of(base + n * 8, 8), 8), :] for n in range(STATE)]
        found = scan_group(dts, us, rate, group, (zero,) * (STATE + 1), drive, None, None)
        for n in range(STATE):
            ends[pl.ds(base + n, 8, stride=STATE), :] = found[n]
        totals[pl.ds(pl.multiple_of(group * 8, 8), 8), :] = found[STATE]

    def plain(group, _):
        run = jnp.where(group < 5, PATCHED, group - 5)
        one_group(group, splat_reader(bs, run * (ROWS * STATE)))
        return 0

    lax.fori_loop(0, GROUPS - 1, plain, 0)
    one_group(GROUPS - 1, mixed_reader(bs))


def wait_for(ref, sem):
    pltpu.make_async_copy(ref, ref, sem).wait()


def exchange_kernel(
    ends, totals, rate, incoming,
    got_ends, got_totals, leaving, landed, send_a, send_b, send_c, recv_a, recv_b, recv_c,
):
    me = lax.axis_index("seq")
    v = lax.axis_index("var")

    barrier = pltpu.get_barrier_semaphore()

    def greet(k, _):
        peer = lax.rem(me + k, SHARDS)
        pl.semaphore_signal(barrier, inc=1, device_id=(peer, v), device_id_type=MESH)
        return 0

    lax.fori_loop(1, SHARDS, greet, 0)
    own_a = pltpu.make_async_copy(ends.at[me], got_ends.at[me], recv_a)
    own_b = pltpu.make_async_copy(totals.at[me], got_totals.at[me], recv_b)
    own_a.start()
    own_b.start()
    pl.semaphore_wait(barrier, SHARDS - 1)

    def send(k, _):
        peer = lax.rem(me + k, SHARDS)
        pltpu.make_async_remote_copy(
            src_ref=ends.at[peer], dst_ref=got_ends.at[me], send_sem=send_a, recv_sem=recv_a,
            device_id=(peer, v), device_id_type=MESH,
        ).start()
        pltpu.make_async_remote_copy(
            src_ref=totals.at[peer], dst_ref=got_totals.at[me], send_sem=send_b, recv_sem=recv_b,
            device_id=(peer, v), device_id_type=MESH,
        ).start()
        return 0

    lax.fori_loop(1, SHARDS, send, 0)
    wait_for(got_totals, recv_b)
    wait_for(got_ends, recv_a)

    def chain(s, state):
        leaving[s] = state.astype(LINK)
        return jnp.exp2(rate[...] * got_totals[s]) * state + got_ends[s].astype(F32)

    lax.fori_loop(0, SHARDS, chain, jnp.zeros((STATE, LANES), F32), unroll=4)

    own_c = pltpu.make_async_copy(leaving.at[me], landed.at[me], recv_c)
    own_c.start()

    def give(k, _):
        peer = lax.rem(me + k, SHARDS)
        pltpu.make_async_remote_copy(
            src_ref=leaving.at[peer], dst_ref=landed.at[me], send_sem=send_c, recv_sem=recv_c,
            device_id=(peer, v), device_id_type=MESH,
        ).start()
        return 0

    lax.fori_loop(1, SHARDS, give, 0)
    others = pl.ds(0, SHARDS - 1)
    wait_for(ends.at[others], send_a)
    wait_for(totals.at[others], send_b)
    wait_for(leaving.at[others], send_c)
    wait_for(landed, recv_c)
    incoming[...] = landed[...]


def back_kernel(
    pos, mode, clean_gate, corrupt_gate, d_skip, incoming, rates, dts, us, bs, cs, acts,
    patched, cut, squares, start, ys,
):
    v = lax.axis_index("var")
    first = lax.axis_index("seq") * ROWS
    take = hit_rows(pos, first, ROWS)[:, :1] & (mode[0] != 0)

    def widen(c, _):
        start[pl.ds(pl.multiple_of(c * STATE, STATE), STATE), :] = incoming[c].astype(F32)
        return 0

    lax.fori_loop(0, CHUNKS, widen, 0, unroll=4)

    def one_group(group, drive, readout):
        base = group * (STATE * 8)
        rate = [rates[pl.ds(pl.multiple_of(base + n * 8, 8), 8), :] for n in range(STATE)]
        state = tuple(start[pl.ds(base + n, 8, stride=STATE), :] for n in range(STATE))
        scan_group(dts, us, rate, group, state, drive, readout, ys)

    def plain(group, _):
        run = jnp.where(group < 5, PATCHED, group - 5) * (ROWS * STATE)
        one_group(group, splat_reader(bs, run), splat_reader(cs, run))
        return 0

    lax.fori_loop(0, GROUPS - 1, plain, 0)
    one_group(GROUPS - 1, mixed_reader(bs), mixed_reader(cs))

    def result(slot, act, skip, gate):
        y = ys[pl.ds(slot, ROWS, stride=CHUNKS), :]
        return ((y + skip * act) * silu(gate)).astype(BF16)

    for tile in range(CUT_TILES):
        cols = pl.ds(pl.multiple_of(v * SPAN + tile * LANES, LANES), LANES)
        skip = d_skip[:, cols]
        clean_out = result(
            cut_slot(CLEAN, tile), acts[:ROWS, cols].astype(F32), skip,
            clean_gate[:, cols].astype(F32),
        )
        corrupt_out = result(
            cut_slot(CORRUPT, tile), acts[ROWS : 2 * ROWS, cols].astype(F32), skip,
            corrupt_gate[:, cols].astype(F32),
        )
        cut[:, tile * LANES : (tile + 1) * LANES] = corrupt_out
        gap = clean_out.astype(F32) - corrupt_out.astype(F32)
        squares[tile] = jnp.sum(gap * gap, axis=0, keepdims=True)

    def patched_tile(tile, _):
        cols = pl.ds(pl.multiple_of(tile * LANES, LANES), LANES)
        gate = jnp.where(take, clean_gate[:, cols].astype(F32), corrupt_gate[:, cols].astype(F32))
        patched[:, cols] = result(tile, acts[2 * ROWS :, cols].astype(F32), d_skip[:, cols], gate)
        return 0

    lax.fori_loop(0, TILES, patched_tile, 0, unroll=2)


def tail_kernel(
    cut, patched, squares, effect,
    whole, peaks, got_squares, spread, got_peaks, answer, answers,
    send_cut, send_sq, send_pk, send_sp, send_an, recv_cut, recv_sq, recv_pk, recv_sp, recv_an,
):
    me = lax.axis_index("seq")
    v = lax.axis_index("var")
    barrier = pltpu.get_barrier_semaphore()

    def greet(k, _):
        peer = lax.rem(me + k, SHARDS)
        pl.semaphore_signal(barrier, inc=1, device_id=(peer, v), device_id_type=MESH)
        return 0

    lax.fori_loop(1, SHARDS, greet, 0)
    for k in range(1, VARS):
        pl.semaphore_signal(
            barrier, inc=1, device_id=(me, lax.rem(v + k, VARS)), device_id_type=MESH
        )
    pl.semaphore_wait(barrier, SHARDS - 1 + VARS - 1)

    def to_variant(k, src, dst, send_sem, recv_sem):
        return pltpu.make_async_remote_copy(
            src_ref=src, dst_ref=dst, send_sem=send_sem, recv_sem=recv_sem,
            device_id=(me, lax.rem(v + k, VARS)), device_id_type=MESH,
        )

    def to_shard(peer, src, dst, send_sem, recv_sem):
        return pltpu.make_async_remote_copy(
            src_ref=src, dst_ref=dst, send_sem=send_sem, recv_sem=recv_sem,
            device_id=(peer, v), device_id_type=MESH,
        )

    for k in range(1, VARS):
        to_variant(k, cut, whole.at[v], send_cut.at[k], recv_cut.at[k]).start()

    def send_square(i, _):
        peer = v * CUT_TILES + i

        @pl.when(peer != me)
        def _():
            to_shard(
                peer, squares.at[i], got_squares.at[me], send_sq.at[i], recv_sq
            ).start()

        @pl.when(peer == me)
        def _():
            pltpu.make_async_copy(squares.at[i], got_squares.at[me], recv_sq).start()

        return 0

    lax.fori_loop(0, CUT_TILES, send_square, 0)
    whole[v] = cut[...]
    for k in range(1, VARS):
        to_variant(k, cut, whole.at[lax.rem(v + VARS - k, VARS)], send_cut.at[k], recv_cut.at[k]).wait()

    for w in range(VARS):
        def peak_tile(i, _):
            here = pl.ds(pl.multiple_of(i * LANES, LANES), LANES)
            there = pl.ds(pl.multiple_of(w * SPAN + i * LANES, LANES), LANES)
            gap = jnp.abs(patched[:, there].astype(F32) - whole[w, :, here].astype(F32))
            peaks[w * CUT_TILES + i] = jnp.max(gap, axis=0, keepdims=True)
            return 0

        lax.fori_loop(0, CUT_TILES, peak_tile, 0, unroll=2)

    def send_peak(c, _):
        @pl.when(c != me)
        def _():
            to_shard(c, peaks.at[c], got_peaks.at[me], send_pk.at[c], recv_pk).start()

        @pl.when(c == me)
        def _():
            pltpu.make_async_copy(peaks.at[c], got_peaks.at[me], recv_pk).start()

        return 0

    lax.fori_loop(0, TILES, send_peak, 0)

    owner = lax.div(me, CUT_TILES)

    @pl.when(owner == v)
    def _():
        wait_for(got_squares, recv_sq)
        total = jnp.sum(got_squares[...], axis=0)
        spread[...] = jnp.sqrt(total / (SHARDS * ROWS) + TINY)
        for k in range(1, VARS):
            to_variant(k, spread, spread, send_sp.at[k], recv_sp).start()

    @pl.when((owner != v) & (me < TILES))
    def _():
        wait_for(spread, recv_sp)

    @pl.when(me < TILES)
    def _():
        wait_for(got_peaks, recv_pk)
        answer[...] = jnp.max(got_peaks[...], axis=0) / spread[...]
        pltpu.make_async_copy(answer, answers.at[me], recv_an).start()

        def share(k, _):
            peer = lax.rem(me + k, SHARDS)
            to_shard(peer, answer, answers.at[me], send_an.at[k], recv_an).start()
            return 0

        lax.fori_loop(1, SHARDS, share, 0)

    wait_for(answers, recv_an)
    for c in range(TILES):
        effect[:, c * LANES : (c + 1) * LANES] = answers[c]

    @pl.when(me < TILES)
    def _():
        def done(k, _):
            peer = lax.rem(me + k, SHARDS)
            to_shard(peer, answer, answers.at[me], send_an.at[k], recv_an).wait_send()
            return 0

        lax.fori_loop(1, SHARDS, done, 0)

    @pl.when(owner == v)
    def _():
        for k in range(1, VARS):
            to_variant(k, spread, spread, send_sp.at[k], recv_sp).wait_send()

    def sent_peak(c, _):
        @pl.when(c != me)
        def _():
            to_shard(c, peaks.at[c], got_peaks.at[me], send_pk.at[c], recv_pk).wait_send()

        return 0

    lax.fori_loop(0, TILES, sent_peak, 0)

    def sent_square(i, _):
        peer = v * CUT_TILES + i

        @pl.when(peer != me)
        def _():
            to_shard(
                peer, squares.at[i], got_squares.at[me], send_sq.at[i], recv_sq
            ).wait_send()

        return 0

    lax.fori_loop(0, CUT_TILES, sent_square, 0)


VMEM = pl.BlockSpec(memory_space=pltpu.VMEM)
SMEM = pl.BlockSpec(memory_space=pltpu.SMEM)
DMA = pltpu.SemaphoreType.DMA
LIMIT = 40 * 1024 * 1024


def shape(dims, kind):
    return jax.ShapeDtypeStruct(dims, kind)


def half(which):
    return pl.BlockSpec((ROWS, INNER), lambda i: (0, which))


def shards(
    clean_proj, corrupt_proj, patch_pos, patch_mode, a_log, dt_bias,
    conv_weight, conv_bias, x_weight, dt_weight, d_skip,
):
    me = lax.axis_index("seq")
    v = lax.axis_index("var")
    tails = jnp.stack([clean_proj[ROWS - 8 :, :INNER], corrupt_proj[ROWS - 8 :, :INNER]])
    rims = lax.ppermute(tails, "seq", [(s, s + 1) for s in range(SHARDS - 1)])

    ends, totals, rates, dts, us, bs, cs, acts = pl.pallas_call(
        front_kernel,
        out_shape=(
            shape((CHUNKS * STATE, LANES), F32),
            shape((CHUNKS, LANES), F32),
            shape((GROUPS * STATE * 8, LANES), F32),
            shape((ROWS * CHUNKS, LANES), F32),
            shape((ROWS * CHUNKS, LANES), F32),
            shape((3 * ROWS * STATE, LANES), F32),
            shape((3 * ROWS * STATE, LANES), F32),
            shape((3 * ROWS, INNER), BF16),
        ),
        grid=(1,),
        in_specs=[SMEM, SMEM, half(0), half(0)] + [VMEM] * 7,
        out_specs=(VMEM,) * 8,
        scratch_shapes=[
            pltpu.VMEM((3, 8 + ROWS, 512), F32),
            pltpu.VMEM((3 * ROWS, RANK), BF16),
        ],
        compiler_params=pltpu.CompilerParams(vmem_limit_bytes=LIMIT),
        name="front",
    )(
        patch_pos, patch_mode, clean_proj, corrupt_proj, rims, conv_weight,
        conv_bias[None], x_weight, dt_weight, dt_bias[None], a_log,
    )

    ends = ends.reshape(CHUNKS, STATE, LANES).astype(LINK)
    totals = totals.reshape(CHUNKS, 1, LANES)
    place = jnp.where(me < 56, me - 8 * (me >= 48) - 40, jnp.where(me < 58, me - 48, me - 50))
    tile = jnp.where(me < TILES, me, jnp.where(me < 60, v * CUT_TILES + place, 0))
    rate = jnp.exp(lax.dynamic_slice_in_dim(a_log, tile * LANES, LANES, 1)) * (-LOG2E)
    incoming = pl.pallas_call(
        exchange_kernel,
        out_shape=shape((CHUNKS, STATE, LANES), LINK),
        in_specs=[VMEM] * 3,
        out_specs=VMEM,
        scratch_shapes=[
            pltpu.VMEM((SHARDS, STATE, LANES), LINK),
            pltpu.VMEM((SHARDS, 1, LANES), F32),
            pltpu.VMEM((SHARDS, STATE, LANES), LINK),
            pltpu.VMEM((CHUNKS, STATE, LANES), LINK),
        ]
        + [DMA] * 6,
        compiler_params=pltpu.CompilerParams(
            collective_id=0, has_side_effects=True, vmem_limit_bytes=16 * 1024 * 1024
        ),
        name="exchange",
    )(ends, totals, rate)

    patched, cut, squares = pl.pallas_call(
        back_kernel,
        out_shape=(
            shape((ROWS, INNER), BF16),
            shape((ROWS, SPAN), BF16),
            shape((CUT_TILES, 1, LANES), F32),
        ),
        grid=(1,),
        in_specs=[SMEM, SMEM, half(1), half(1)] + [VMEM] * 8,
        out_specs=(VMEM,) * 3,
        scratch_shapes=[
            pltpu.VMEM((CHUNKS * STATE, LANES), F32),
            pltpu.VMEM((ROWS * CHUNKS, LANES), F32),
        ],
        compiler_params=pltpu.CompilerParams(vmem_limit_bytes=LIMIT),
        name="back",
    )(
        patch_pos, patch_mode, clean_proj, corrupt_proj, d_skip[None], incoming, rates,
        dts, us, bs, cs, acts,
    )

    effect = pl.pallas_call(
        tail_kernel,
        out_shape=shape((1, INNER), F32),
        in_specs=[VMEM] * 3,
        out_specs=VMEM,
        scratch_shapes=[
            pltpu.VMEM((VARS, ROWS, SPAN), BF16),
            pltpu.VMEM((TILES, 1, LANES), F32),
            pltpu.VMEM((SHARDS, 1, LANES), F32),
            pltpu.VMEM((1, LANES), F32),
            pltpu.VMEM((SHARDS, 1, LANES), F32),
            pltpu.VMEM((1, LANES), F32),
            pltpu.VMEM((TILES, 1, LANES), F32),
            DMA((VARS,)),
            DMA((CUT_TILES,)),
            DMA((TILES,)),
            DMA((VARS,)),
            DMA((SHARDS,)),
            DMA((VARS,)),
            DMA,
            DMA,
            DMA,
            DMA,
        ],
        compiler_params=pltpu.CompilerParams(
            collective_id=1, has_side_effects=True, vmem_limit_bytes=16 * 1024 * 1024
        ),
        name="tail",
    )(cut, patched, squares)
    return (patched[None], effect)


def solution(mesh):
    return jax.shard_map(
        shards,
        mesh=mesh,
        in_specs=(
            P("seq", None), P("seq", None), P("var", None), P("var"),
            P(), P(), P(), P(), P(), P(), P(),
        ),
        out_specs=(P("var", "seq", None), P("var", None)),
        check_vma=False,
    )
```

time: 424 us -> 106 us (0.25)
  waiting for transfers between devices: 110 us -> 0.01 us
  local copies, waits for them, and re-layouts: 104 us -> 9.67 us
  other arithmetic: 92.6 us -> 1.39 us
  Pallas kernels: 0 us -> 88.6 us
  blocking collectives: 78.3 us -> 0 us
  between operations: 16.1 us -> 1.44 us
  starting transfers between devices: 13.9 us -> 4.91 us
    all_gather x3 -> x0, waiting for transfers between devices: 108 us -> none  [gathered_once(): both, at, found = (lax.all_gather(jnp.concatenate(lines), axis), 0, {})]
    pallas_call x0 -> x4, Pallas kernels: none -> 88.6 us  [the longest x1 38.9 us: shards(): pl.pallas_call(exchange_kernel, out_shape=shape((CHUNKS, STATE, LANES), L...]
    all_gather x6 -> x0, blocking collectives: 78.3 us -> none  [joined_all(): pieces = jax.tree.map(lambda part: lax.all_gather(part, axis), value)]
    squeeze x41 -> x0, local copies, waits for them, and re-layouts: 42 us -> none  [the longest x40 41.9 us: carried_in(): total = combine(total, jax.tree.map(lambda part: part[k], pieces))]
    reduce_sum x37 -> x0, other arithmetic: 20.4 us -> none  [the longest x36 20.3 us: advance(): outputs.append(jnp.sum(c_rows[row][:, None] * state, axis=0))]
    slice x9 -> x0, other arithmetic: 15 us -> none  [the longest x8 12.8 us: advance(): flows[row][None, :] * b_rows[row][:, None]]
    add x12 -> x0, other arithmetic: 14.5 us -> none  [the longest x8 14.5 us: chain(): late_first * early_state + late_state]
    slice x13 -> x0, local copies, waits for them, and re-layouts: 14.3 us -> none  [the longest x3 7.52 us: carried_in(): total = combine(total, jax.tree.map(lambda part: part[k], pieces))]
  transfers between devices with their start and end apart: 6 -> 1, of which waited for: 3 -> 0; matrix products, arithmetic and copies ran while one was open for 17% -> 3% of each run, Pallas kernels for 0% -> 0%
where the time goes in v1:
time: 106 us
  Pallas kernels  88.6 us (84%)
  local copies, waits for them, and re-layouts  9.67 us (9%)
  starting transfers between devices  4.91 us (5%)
  between operations  1.44 us (1%)
  other arithmetic  1.39 us (1%)
    pallas_call x1, Pallas kernels, shards(): pl.pallas_call(exchange_kernel, out_shape=shape((CHUNKS, STATE, LANES), L...  38.9 us
    pallas_call x1, Pallas kernels, shards(): pl.pallas_call(tail_kernel, out_shape=shape((1, INNER), F32), in_specs=[V...  27 us
    pallas_call x1, Pallas kernels, shards(): pl.pallas_call(front_kernel, out_shape=(shape((CHUNKS * STATE, LANES), F3...  12.8 us
    pallas_call x1, Pallas kernels, shards(): pl.pallas_call(back_kernel, out_shape=(shape((ROWS, INNER), BF16), shape(...  9.95 us
    unnamed x22, local copies, waits for them, and re-layouts  8.73 us
    ppermute x1, starting transfers between devices, shards(): rims = lax.ppermute(tails, 'seq', [(s, s + 1) for s in range(SHARDS - 1)])  4.91 us
  transfers between devices with their start and end apart: 1, of which 0 were waited for; matrix products, arithmetic and copies ran while one was open for 3% of the time, Pallas kernels for 0%

profile of v1, /device:TPU:1, one launch (start us, length us, event | category | flops | bytes accessed | tf_op | source)
XLA Modules:
  0.0 106.0 jit_solution(761522191642731732)
XLA Ops:
  0.6 0.9 slice_bitcast_fusion
  1.6 0.7 pad_maximum_fusion
  2.3 4.9 %collective-permute-start = (bf16[2,8,5120]{2,1,0:T(8,128)(2,1)}, bf16[2,8,5120]{2,1,0:T(8,128)(2,1)S(1)}, u32[]{:S(2)}, u32[]{:S(2)}) collective-permute-start(bf16[2,8,5120]{2,1,0:T(8,128)(2,1)} %pad_maximum_fusion), channel_id=1, source_target_pairs={{0,4},{4,8},{8,12},{12,16},{16,20},{20,24},{24,28},{28,32},{32,36}... | collective-permute-start | bytes 491528 | tf_op jit(solution)/shard_map/ppermute | solution.py:493
  7.8 0.0 copy-start
  7.8 0.0 copy-start.5
  7.9 0.0 copy-start.6
  7.9 0.0 copy-start.9
  7.9 2.9 %copy.13.x_w = bf16[5120,192]{1,0:T(8,128)(2,1)S(1)} copy(bf16[5120,192]{0,1:T(8,128)(2,1)} %param.19) | data formatting | bytes 3932160 | tf_op args[8]
  10.8 0.7 exponential_multiply_fusion.rate
  11.5 0.0 collective-permute-done.rims
  11.5 0.0 copy-done
  11.5 0.0 copy-done.5
  11.5 0.0 copy-done.6
  11.6 0.0 copy-done.9
  11.6 0.0 copy-start.1
  11.6 1.1 %copy-done.1 = bf16[32,10240]{1,0:T(8,128)(2,1)S(1)} copy-done((bf16[32,10240]{1,0:T(8,128)(2,1)S(1)}, bf16[32,10240]{1,0:T(8,128)(2,1)}, u32[]{:S(2)}) %copy-start.1) | copy-done | bytes 655384
  12.7 0.0 copy-start.2
  12.7 1.4 %copy-done.2 = bf16[160,5120]{1,0:T(8,128)(2,1)S(1)} copy-done((bf16[160,5120]{1,0:T(8,128)(2,1)S(1)}, bf16[160,5120]{1,0:T(8,128)(2,1)}, u32[]{:S(2)}) %copy-start.2) | copy-done | bytes 1638424
  14.1 0.0 copy-start.3
  14.1 1.0 copy-done.3
  15.1 0.0 copy-start.7
  15.1 0.7 copy-done.7
  15.8 0.0 copy-start.8
  15.8 12.8 %front.1 = (f32[1024,128]{1,0:T(8,128)S(1)}, f32[64,128]{1,0:T(8,128)S(1)}, f32[1024,128]{1,0:T(8,128)S(1)}, f32[2048,128]{1,0:T(8,128)S(1)}, f32[2048,128]{1,0:...) custom-call(s32[1,16]{1,0:T(1,128)S(1)} %copy-done.9, ...), custom_call_target="tpu_custom_call" | custom-call | tf_op jit(solution)/shard_map/front/pallas_call | solution.py:495
  28.6 38.9 %exchange.1.incoming = f32[64,16,128]{2,1,0:T(8,128)S(1)} custom-call(f32[64,16,128]{2,1,0:T(8,128)S(1)} %bitcast.10, f32[64,1,128]{2,1,0:T(1,128)S(1)} %bitcast.12, f32[16,128]{1,0:T(8,128)S(1)} %exponential_multiply_fusion.rate), custom_call_target="tpu_custom_call" | custom-call | tf_op jit(solution)/shard_map/exchange/pallas_call | solution.py:526
  67.5 0.0 copy-done.8
  67.5 9.9 %back.1 = (bf16[32,5120]{1,0:T(8,128)(2,1)}, bf16[32,1280]{1,0:T(8,128)(2,1)S(1)}, f32[10,1,128]{2,1,0:T(1,128)S(1)}) custom-call(s32[1,16]{1,0:T(1,128)S(1)} %copy-done.9, s32[1]{0:T(128)S(6)} %copy.15.mode, bf16[32,10240]{1,0:T(8,128)(2,1)S(1)} %copy-done, bf16[32,10240]{1,0:T(8,128)(2,1)S(1)} %copy-done.1, f32[1,5120]{1,0:T(1,128)S(1)} %bitcast.15, ...), custom_call_target="tpu_custom_call" | custom-call | tf_op jit(solution)/shard_map/back/pallas_call | solution.py:544
  77.5 0.0 copy-start.4
  77.5 1.0 copy-done.4
  78.4 27.0 %tail.1 = f32[1,5120]{1,0:T(1,128)S(1)} custom-call(bf16[32,1280]{1,0:T(8,128)(2,1)S(1)} %get-tuple-element.22.cut, bf16[32,5120]{1,0:T(8,128)(2,1)S(1)} %copy-done.4, f32[10,1,128]{2,1,0:T(1,128)S(1)} %get-tuple-element.23.squares), custom_call_target="tpu_custom_call" | custom-call | tf_op jit(solution)/shard_map/tail/pallas_call | solution.py:565
  105.4 0.6 copy.16
Async XLA Ops:
  2.3 9.3 %collective-permute-start = (bf16[2,8,5120]{2,1,0:T(8,128)(2,1)}, bf16[2,8,5120]{2,1,0:T(8,128)(2,1)S(1)}, u32[]{:S(2)}, u32[]{:S(2)}) collective-permute-start(bf16[2,8,5120]{2,1,0:T(8,128)(2,1)} %pad_maximum_fusion), channel_id=1, source_target_pairs={{0,4},{4,8},{8,12},{12,16},{16,20},{20,24},{24,28},{28,32},{32,36}... | collective-permute-start | bytes 491528 | tf_op jit(solution)/shard_map/ppermute | solution.py:493
  7.8 3.7 %copy-start = (bf16[32,10240]{1,0:T(8,128)(2,1)S(1)}, bf16[32,10240]{1,0:T(8,128)(2,1)}, u32[]{:S(2)}) copy-start(bf16[32,10240]{1,0:T(8,128)(2,1)} %clean_gate.1) | copy-start | bytes 1966084
  7.8 3.7 %copy-start.5 = (f32[4,5120]{1,0:T(4,128)S(1)}, f32[4,5120]{1,0:T(4,128)}, u32[]{:S(2)}) copy-start(f32[4,5120]{1,0:T(4,128)} %conv_w.1) | copy-start | bytes 245764
  7.9 3.7 %copy-start.6 = (f32[5120]{0:T(1024)S(1)}, f32[5120]{0:T(1024)}, u32[]{:S(2)}) copy-start(f32[5120]{0:T(1024)} %param.18) | copy-start | bytes 61444
  7.9 3.7 %copy-start.9 = (s32[1,16]{1,0:T(1,128)S(1)}, s32[1,16]{1,0:T(1,128)}, u32[]{:S(2)}) copy-start(s32[1,16]{1,0:T(1,128)} %pos.3) | copy-start | bytes 196
  11.6 1.1 %copy-start.1 = (bf16[32,10240]{1,0:T(8,128)(2,1)S(1)}, bf16[32,10240]{1,0:T(8,128)(2,1)}, u32[]{:S(2)}) copy-start(bf16[32,10240]{1,0:T(8,128)(2,1)} %corrupt_gate.1) | copy-start | bytes 1966084
  12.7 1.4 %copy-start.2 = (bf16[160,5120]{1,0:T(8,128)(2,1)S(1)}, bf16[160,5120]{1,0:T(8,128)(2,1)}, u32[]{:S(2)}) copy-start(bf16[160,5120]{1,0:T(8,128)(2,1)} %dt_w.1) | copy-start | bytes 4915204
  14.1 1.0 copy-start.3
  15.1 0.7 copy-start.7
  15.8 51.7 %copy-start.8 = (f32[5120]{0:T(1024)S(1)}, f32[5120]{0:T(1024)}, u32[]{:S(2)}) copy-start(f32[5120]{0:T(1024)} %param.21) | copy-start | bytes 61444
  77.5 1.0 copy-start.4

commit v2 on v1

v2 whole, which is shorter than its diff:
```python
import functools

import jax
import jax.numpy as jnp
from jax import lax
from jax.experimental import pallas as pl
from jax.experimental.pallas import tpu as pltpu
from jax.sharding import PartitionSpec as P

STATE = 16
RANK = 160
ROWS = 32
INNER = 5120
SPAN = 1280
TAPS = 4
LANES = 128
CHUNKS = 64
SHARDS = 64
VARS = 4
TILES = INNER // LANES
CUT_TILES = SPAN // LANES
GROUPS = CHUNKS // 8
HALF = CHUNKS // 2
CHIPS = SHARDS // 2
PITCH = 72
SPLAT = 17
MESH = pl.DeviceIdType.MESH
LOG2E = 1.4426950408889634
TINY = 1e-06
F32 = jnp.float32
BF16 = jnp.bfloat16
UNROLL = 4
CLEAN, CORRUPT, PATCHED = 0, 1, 2


def cut_slot(run, tile):
    if tile < 8:
        return TILES + 8 * run + tile
    return 56 + 2 * run + (tile - 8)


def hit_rows(pos_ref, first, count):
    rows = first + lax.broadcasted_iota(jnp.int32, (count, LANES), 0)
    hits = rows == pos_ref[0, 0]
    for k in range(1, pos_ref.shape[1]):
        hits = hits | (rows == pos_ref[0, k])
    return hits


def silu(value):
    return value / (1.0 + jnp.exp(-value))


def softplus(value):
    return jnp.maximum(value, 0.0) + jnp.log1p(jnp.exp(-jnp.abs(value)))


def row_of(ref, row):
    return jnp.broadcast_to(ref[pl.ds(row, 1), :], (8, LANES))


def scan_group(dts, us, rate, group, state, drive, readout, out):
    def step(t, carry):
        row = pl.multiple_of(t * PITCH + group * 8, 8)
        steps = dts[pl.ds(row, 8), :]
        flow = us[pl.ds(row, 8), :]
        entries = []
        total = None
        for n in range(STATE):
            decay = jnp.exp2(steps * rate[n])
            entry = decay * carry[n] + flow * drive(t, n)
            entries.append(entry)
            if readout is not None:
                term = readout(t, n) * entry
                total = term if total is None else total + term
        if readout is not None:
            out[pl.ds(row, 8), :] = total
        return tuple(entries)

    return lax.fori_loop(0, ROWS, step, state, unroll=UNROLL)


def splat_reader(ref, base):
    return lambda t, n: row_of(ref, base + t * SPLAT + n)


def mixed_reader(ref):
    first = lax.broadcasted_iota(jnp.int32, (8, LANES), 0) < 2

    def read(t, n):
        return jnp.where(
            first,
            row_of(ref, CLEAN * ROWS * SPLAT + t * SPLAT + n),
            row_of(ref, CORRUPT * ROWS * SPLAT + t * SPLAT + n),
        )

    return read


def wait_for(ref, sem):
    pltpu.make_async_copy(ref, ref, sem).wait()


def kernel(
    pos, mode, clean_in, corrupt_in, rims_in, conv_w_in, conv_b_in, x_w_in, dt_w_in, dt_b_in,
    a_log_in, d_skip_in,
    patched, effect,
    clean, corrupt, rims, conv_w, conv_b, x_w, dt_w, dt_b, a_log, d_skip,
    pad, acts, low, dts, us, bs, cs, rates, ends, totals,
    pair_ends, pair_totals, chip_ends, chip_totals, got_ends, got_totals,
    leaving, landed, across, start, ys,
    cut, squares, whole, peaks, got_squares, spread, got_peaks, answer, answers,
    load_sem, send_pt, recv_pt, send_pe, recv_pe, send_ct, recv_ct, send_ce, recv_ce,
    send_in, recv_in, send_st, recv_st,
    send_cut, send_sq, send_pk, send_sp, send_an, recv_cut, recv_sq, recv_pk, recv_sp, recv_an,
):
    me = lax.axis_index("seq")
    v = lax.axis_index("var")
    chip = lax.div(me, 2)
    core = lax.rem(me, 2)
    mate = me + 1 - 2 * core
    mine = core * HALF
    theirs = HALF - mine
    barrier = pltpu.get_barrier_semaphore()

    loads = [
        pltpu.make_async_copy(src, dst, load_sem.at[i])
        for i, (src, dst) in enumerate(
            (
                (clean_in, clean), (corrupt_in, corrupt), (rims_in, rims), (conv_w_in, conv_w),
                (conv_b_in, conv_b), (x_w_in, x_w), (dt_w_in, dt_w), (dt_b_in, dt_b),
                (a_log_in, a_log), (d_skip_in, d_skip),
            )
        )
    ]
    for load in loads:
        load.start()

    def greet(k, _):
        peer = lax.rem(me + k, SHARDS)
        pl.semaphore_signal(barrier, inc=1, device_id=(peer, v), device_id_type=MESH)
        return 0

    lax.fori_loop(1, SHARDS, greet, 0)
    for k in range(1, VARS):
        pl.semaphore_signal(
            barrier, inc=1, device_id=(me, lax.rem(v + k, VARS)), device_id_type=MESH
        )

    def to_variant(k, src, dst, send_sem, recv_sem):
        return pltpu.make_async_remote_copy(
            src_ref=src, dst_ref=dst, send_sem=send_sem, recv_sem=recv_sem,
            device_id=(me, lax.rem(v + k, VARS)), device_id_type=MESH,
        )

    def to_shard(peer, src, dst, send_sem, recv_sem):
        return pltpu.make_async_remote_copy(
            src_ref=src, dst_ref=dst, send_sem=send_sem, recv_sem=recv_sem,
            device_id=(peer, v), device_id_type=MESH,
        )

    first = me * ROWS
    hits = hit_rows(pos, first, ROWS)[:, :1]
    take = hits & (mode[0] != 1)
    take_gate = hits & (mode[0] != 0)
    take_rim = hit_rows(pos, first - 8, 8)[:, :1] & (mode[0] != 1)

    for load in loads[:5]:
        load.wait()
    width = 512

    def conv(i, _):
        cols = pl.ds(pl.multiple_of(i * width, width), width)
        sig_clean = clean[:, cols].astype(F32)
        sig_corrupt = corrupt[:, cols].astype(F32)
        rim_clean = rims[0:8, cols].astype(F32)
        rim_corrupt = rims[8:16, cols].astype(F32)
        pieces = (
            (rim_clean, sig_clean),
            (rim_corrupt, sig_corrupt),
            (
                jnp.where(take_rim, rim_clean, rim_corrupt),
                jnp.where(take, sig_clean, sig_corrupt),
            ),
        )
        bias = conv_b[:, cols]
        for run, (rim, sig) in enumerate(pieces):
            pad[run, 0:8, :] = rim
            pad[run, 8:, :] = sig
            total = bias + conv_w[0:1, cols] * pad[run, 5 : 5 + ROWS, :]
            for k in range(1, TAPS):
                total = total + conv_w[k : k + 1, cols] * pad[run, 5 + k : 5 + k + ROWS, :]
            acts[run * ROWS : (run + 1) * ROWS, cols] = silu(total).astype(BF16)
        return 0

    lax.fori_loop(0, INNER // width, conv, 0)

    loads[5].wait()
    projected = lax.dot_general(
        acts[...], x_w[...], (((1,), (1,)), ((), ())), preferred_element_type=F32
    )
    low[...] = projected[:, :RANK].astype(BF16)
    for run in range(3):
        part = projected[run * ROWS : (run + 1) * ROWS]
        for n in range(STATE):
            at = run * ROWS * SPLAT + n
            bs[pl.ds(at, ROWS, stride=SPLAT), :] = jnp.broadcast_to(
                part[:, RANK + n : RANK + n + 1], (ROWS, LANES)
            )
            cs[pl.ds(at, ROWS, stride=SPLAT), :] = jnp.broadcast_to(
                part[:, RANK + STATE + n : RANK + STATE + n + 1], (ROWS, LANES)
            )

    for load in loads[6:9]:
        load.wait()

    def rate_at(slot):
        return pl.ds(lax.div(slot, 8) * (STATE * 8) + lax.rem(slot, 8), STATE, stride=8)

    def place(slot, steps, act, log_rate):
        dts[pl.ds(slot, ROWS, stride=PITCH), :] = steps
        us[pl.ds(slot, ROWS, stride=PITCH), :] = steps * act
        totals[slot] = jnp.sum(steps, axis=0, keepdims=True)
        rates[rate_at(slot), :] = jnp.exp(log_rate) * (-LOG2E)

    wide = 640

    def patched_steps(i, _):
        cols = pl.ds(pl.multiple_of(i * wide, wide), wide)
        raw = jnp.dot(low[2 * ROWS :, :], dt_w[:, cols], preferred_element_type=F32)
        steps = softplus(raw + dt_b[:, cols])
        act = acts[2 * ROWS :, cols].astype(F32)
        logs = a_log[:, cols]
        for k in range(wide // LANES):
            part = slice(k * LANES, (k + 1) * LANES)
            place(i * (wide // LANES) + k, steps[:, part], act[:, part], logs[:, part])
        return 0

    lax.fori_loop(0, INNER // wide, patched_steps, 0)

    cols = pl.ds(pl.multiple_of(v * SPAN, LANES), SPAN)
    raw = jnp.dot(low[: 2 * ROWS, :], dt_w[:, cols], preferred_element_type=F32)
    steps = softplus(raw + dt_b[:, cols])
    act = acts[: 2 * ROWS, cols].astype(F32)
    logs = a_log[:, cols]
    for run in (CLEAN, CORRUPT):
        rows = slice(run * ROWS, (run + 1) * ROWS)
        for tile in range(CUT_TILES):
            part = slice(tile * LANES, (tile + 1) * LANES)
            place(cut_slot(run, tile), steps[rows, part], act[rows, part], logs[:, part])
    blank = jnp.zeros((ROWS, LANES), F32)
    for slot in range(60, CHUNKS):
        place(slot, blank, blank, jnp.zeros((STATE, LANES), F32))

    pl.semaphore_wait(barrier, SHARDS - 1 + VARS - 1)
    theirs_3 = pl.ds(theirs, HALF)
    swap_totals = to_shard(mate, totals.at[theirs_3], pair_totals, send_pt, recv_pt)
    swap_totals.start()

    zero = jnp.zeros((8, LANES), F32)

    def rates_of(group):
        base = group * (STATE * 8)
        return [rates[pl.ds(pl.multiple_of(base + n * 8, 8), 8), :] for n in range(STATE)]

    def run_base(group):
        return jnp.where(group < 5, PATCHED, group - 5) * (ROWS * SPLAT)

    def local_group(group, drive):
        found = scan_group(
            dts, us, rates_of(group), group, (zero,) * STATE, drive, None, None
        )
        for n in range(STATE):
            ends[pl.ds(group * (STATE * 8) + n, 8, stride=STATE), :] = found[n]

    def local_pass(offset):
        def body(i, _):
            group = offset + i

            @pl.when(group < GROUPS - 1)
            def _():
                local_group(group, splat_reader(bs, run_base(group)))

            @pl.when(group == GROUPS - 1)
            def _():
                local_group(group, mixed_reader(bs))

            return 0

        lax.fori_loop(0, GROUPS // 2, body, 0)

    local_pass(lax.div(theirs, 8))
    theirs_2 = pl.ds(pl.multiple_of(theirs * STATE, 8), HALF * STATE)
    swap_ends = to_shard(mate, ends.at[theirs_2], pair_ends, send_pe, recv_pe)
    swap_ends.start()
    local_pass(lax.div(mine, 8))
    swap_totals.wait()
    leads = core == 0

    def my_summary(k):
        own = ends[pl.ds(pl.multiple_of((mine + k) * STATE, 8), STATE), :]
        return own, totals[mine + k]

    def pair_of(k):
        own_end, own_total = my_summary(k)
        other_end = pair_ends[pl.ds(pl.multiple_of(k * STATE, 8), STATE), :]
        other_total = pair_totals[k]
        return (
            jnp.where(leads, own_end, other_end), jnp.where(leads, own_total, other_total),
            jnp.where(leads, other_end, own_end), jnp.where(leads, other_total, own_total),
        )

    def chip_total(k, _):
        chip_totals[k] = totals[mine + k] + pair_totals[k]
        return 0

    lax.fori_loop(0, HALF, chip_total, 0, unroll=4)
    swap_ends.wait()

    def chip_end(k, _):
        end_a, total_a, end_b, total_b = pair_of(k)
        chip_ends[k] = jnp.exp2(rates[rate_at(mine + k), :] * total_b) * end_a + end_b
        return 0

    lax.fori_loop(0, HALF, chip_end, 0, unroll=4)
    pltpu.make_async_copy(chip_totals.at[chip], got_totals.at[chip], recv_ct).start()
    pltpu.make_async_copy(chip_ends.at[chip], got_ends.at[chip], recv_ce).start()

    def spread_out(k, _):
        peer = lax.rem(chip + k, CHIPS)
        target = 2 * peer + core
        to_shard(target, chip_ends.at[peer], got_ends.at[chip], send_ce, recv_ce).start()
        to_shard(target, chip_totals.at[peer], got_totals.at[chip], send_ct, recv_ct).start()
        return 0

    lax.fori_loop(1, CHIPS, spread_out, 0)
    my_rate = rates[rate_at(mine + chip), :]
    wait_for(got_totals, recv_ct)
    wait_for(got_ends, recv_ce)

    def chain(s, state):
        leaving[s] = state
        return jnp.exp2(my_rate * got_totals[s]) * state + got_ends[s]

    lax.fori_loop(0, CHIPS, chain, jnp.zeros((STATE, LANES), F32), unroll=4)
    pltpu.make_async_copy(leaving.at[chip], landed.at[chip], recv_in).start()

    def give(k, _):
        peer = lax.rem(chip + k, CHIPS)
        to_shard(2 * peer + core, leaving.at[peer], landed.at[chip], send_in, recv_in).start()
        return 0

    lax.fori_loop(1, CHIPS, give, 0)
    wait_for(landed, recv_in)

    def enter(k, _):
        end_a, total_a, _, _ = pair_of(k)
        before = landed[k]
        after = jnp.exp2(rates[rate_at(mine + k), :] * total_a) * before + end_a
        at = pl.ds(pl.multiple_of((mine + k) * STATE, 8), STATE)
        start[at, :] = jnp.where(leads, before, after)
        across[pl.ds(pl.multiple_of(k * STATE, 8), STATE), :] = jnp.where(leads, after, before)
        return 0

    lax.fori_loop(0, HALF, enter, 0, unroll=4)
    mine_2 = pl.ds(pl.multiple_of(mine * STATE, 8), HALF * STATE)
    swap_start = to_shard(mate, across, start.at[mine_2], send_st, recv_st)
    swap_start.start()
    loads[9].wait()
    swap_start.wait()

    def final_group(group, drive, readout):
        base = group * (STATE * 8)
        state = tuple(start[pl.ds(base + n, 8, stride=STATE), :] for n in range(STATE))
        scan_group(dts, us, rates_of(group), group, state, drive, readout, ys)

    def final_plain(group, _):
        base = run_base(group)
        final_group(group, splat_reader(bs, base), splat_reader(cs, base))
        return 0

    def result(slot, act, skip, gate):
        y = ys[pl.ds(slot, ROWS, stride=PITCH), :]
        return ((y + skip * act) * silu(gate)).astype(BF16)

    lax.fori_loop(5, GROUPS - 1, final_plain, 0)
    final_group(GROUPS - 1, mixed_reader(bs), mixed_reader(cs))
    for tile in range(CUT_TILES):
        at = v * SPAN + tile * LANES
        cols = pl.ds(pl.multiple_of(at, LANES), LANES)
        gate_cols = pl.ds(pl.multiple_of(INNER + at, LANES), LANES)
        skip = d_skip[:, cols]
        clean_out = result(
            cut_slot(CLEAN, tile), acts[:ROWS, cols].astype(F32), skip,
            clean[:, gate_cols].astype(F32),
        )
        corrupt_out = result(
            cut_slot(CORRUPT, tile), acts[ROWS : 2 * ROWS, cols].astype(F32), skip,
            corrupt[:, gate_cols].astype(F32),
        )
        cut[:, tile * LANES : (tile + 1) * LANES] = corrupt_out
        gap = clean_out.astype(F32) - corrupt_out.astype(F32)
        squares[tile] = jnp.sum(gap * gap, axis=0, keepdims=True)

    for k in range(1, VARS):
        to_variant(k, cut, whole.at[v], send_cut.at[k], recv_cut.at[k]).start()

    def send_square(i, _):
        peer = v * CUT_TILES + i

        @pl.when(peer != me)
        def _():
            to_shard(
                peer, squares.at[i], got_squares.at[me], send_sq.at[i], recv_sq
            ).start()

        @pl.when(peer == me)
        def _():
            pltpu.make_async_copy(squares.at[i], got_squares.at[me], recv_sq).start()

        return 0

    lax.fori_loop(0, CUT_TILES, send_square, 0)
    whole[v] = cut[...]

    lax.fori_loop(0, 5, final_plain, 0)

    def patched_tile(tile, _):
        cols = pl.ds(pl.multiple_of(tile * LANES, LANES), LANES)
        gate_cols = pl.ds(pl.multiple_of(INNER + tile * LANES, LANES), LANES)
        gate = jnp.where(
            take_gate, clean[:, gate_cols].astype(F32), corrupt[:, gate_cols].astype(F32)
        )
        patched[:, cols] = result(tile, acts[2 * ROWS :, cols].astype(F32), d_skip[:, cols], gate)
        return 0

    lax.fori_loop(0, TILES, patched_tile, 0, unroll=2)

    for k in range(1, VARS):
        to_variant(
            k, cut, whole.at[lax.rem(v + VARS - k, VARS)], send_cut.at[k], recv_cut.at[k]
        ).wait()

    for w in range(VARS):
        def peak_tile(i, _):
            here = pl.ds(pl.multiple_of(i * LANES, LANES), LANES)
            there = pl.ds(pl.multiple_of(w * SPAN + i * LANES, LANES), LANES)
            gap = jnp.abs(patched[:, there].astype(F32) - whole[w, :, here].astype(F32))
            peaks[w * CUT_TILES + i] = jnp.max(gap, axis=0, keepdims=True)
            return 0

        lax.fori_loop(0, CUT_TILES, peak_tile, 0, unroll=2)

    def send_peak(c, _):
        @pl.when(c != me)
        def _():
            to_shard(c, peaks.at[c], got_peaks.at[me], send_pk.at[c], recv_pk).start()

        @pl.when(c == me)
        def _():
            pltpu.make_async_copy(peaks.at[c], got_peaks.at[me], recv_pk).start()

        return 0

    lax.fori_loop(0, TILES, send_peak, 0)

    owner = lax.div(me, CUT_TILES)

    @pl.when(owner == v)
    def _():
        wait_for(got_squares, recv_sq)
        total = jnp.sum(got_squares[...], axis=0)
        spread[...] = jnp.sqrt(total / (SHARDS * ROWS) + TINY)
        for k in range(1, VARS):
            to_variant(k, spread, spread, send_sp.at[k], recv_sp).start()

    @pl.when((owner != v) & (me < TILES))
    def _():
        wait_for(spread, recv_sp)

    @pl.when(me < TILES)
    def _():
        wait_for(got_peaks, recv_pk)
        answer[...] = jnp.max(got_peaks[...], axis=0) / spread[...]
        pltpu.make_async_copy(answer, answers.at[me], recv_an).start()

        def share(k, _):
            peer = lax.rem(me + k, SHARDS)
            to_shard(peer, answer, answers.at[me], send_an.at[k], recv_an).start()
            return 0

        lax.fori_loop(1, SHARDS, share, 0)

    wait_for(answers, recv_an)
    for c in range(TILES):
        effect[:, c * LANES : (c + 1) * LANES] = answers[c]

    @pl.when(me < TILES)
    def _():
        def done(k, _):
            peer = lax.rem(me + k, SHARDS)
            to_shard(peer, answer, answers.at[me], send_an.at[k], recv_an).wait_send()
            return 0

        lax.fori_loop(1, SHARDS, done, 0)

    @pl.when(owner == v)
    def _():
        for k in range(1, VARS):
            to_variant(k, spread, spread, send_sp.at[k], recv_sp).wait_send()

    def sent_peak(c, _):
        @pl.when(c != me)
        def _():
            to_shard(c, peaks.at[c], got_peaks.at[me], send_pk.at[c], recv_pk).wait_send()

        return 0

    lax.fori_loop(0, TILES, sent_peak, 0)

    def sent_square(i, _):
        peer = v * CUT_TILES + i

        @pl.when(peer != me)
        def _():
            to_shard(
                peer, squares.at[i], got_squares.at[me], send_sq.at[i], recv_sq
            ).wait_send()

        return 0

    lax.fori_loop(0, CUT_TILES, sent_square, 0)
    others = pl.ds(0, CHIPS - 1)
    wait_for(chip_totals.at[others], send_ct)
    wait_for(chip_ends.at[others], send_ce)
    wait_for(leaving.at[others], send_in)


SMEM = pl.BlockSpec(memory_space=pltpu.SMEM)
HBM = pl.BlockSpec(memory_space=pltpu.HBM)
VMEM = pl.BlockSpec(memory_space=pltpu.VMEM)
DMA = pltpu.SemaphoreType.DMA


def shards(
    clean_proj, corrupt_proj, patch_pos, patch_mode, a_log, dt_bias,
    conv_weight, conv_bias, x_weight, dt_weight, d_skip,
):
    tails = jnp.concatenate([clean_proj[ROWS - 8 :, :INNER], corrupt_proj[ROWS - 8 :, :INNER]])
    rims = lax.ppermute(tails, "seq", [(s, s + 1) for s in range(SHARDS - 1)])
    row = (1, LANES)
    tile = (STATE, LANES)
    patched, effect = pl.pallas_call(
        kernel,
        out_shape=(
            jax.ShapeDtypeStruct((ROWS, INNER), BF16),
            jax.ShapeDtypeStruct((1, INNER), F32),
        ),
        in_specs=[SMEM, SMEM] + [HBM] * 10,
        out_specs=(VMEM, VMEM),
        scratch_shapes=[
            pltpu.VMEM((ROWS, 2 * INNER), BF16),
            pltpu.VMEM((ROWS, 2 * INNER), BF16),
            pltpu.VMEM((16, INNER), BF16),
            pltpu.VMEM((TAPS, INNER), F32),
            pltpu.VMEM((1, INNER), F32),
            pltpu.VMEM((RANK + 2 * STATE, INNER), BF16),
            pltpu.VMEM((RANK, INNER), BF16),
            pltpu.VMEM((1, INNER), F32),
            pltpu.VMEM((STATE, INNER), F32),
            pltpu.VMEM((1, INNER), F32),
            pltpu.VMEM((3, 8 + ROWS, 512), F32),
            pltpu.VMEM((3 * ROWS, INNER), BF16),
            pltpu.VMEM((3 * ROWS, RANK), BF16),
            pltpu.VMEM((ROWS * PITCH, LANES), F32),
            pltpu.VMEM((ROWS * PITCH, LANES), F32),
            pltpu.VMEM((3 * ROWS * SPLAT + 8, LANES), F32),
            pltpu.VMEM((3 * ROWS * SPLAT + 8, LANES), F32),
            pltpu.VMEM((CHUNKS * STATE, LANES), F32),
            pltpu.VMEM((CHUNKS * STATE, LANES), F32),
            pltpu.VMEM((CHUNKS, *row), F32),
            pltpu.VMEM((HALF * STATE, LANES), F32),
            pltpu.VMEM((HALF, *row), F32),
            pltpu.VMEM((HALF, *tile), F32),
            pltpu.VMEM((HALF, *row), F32),
            pltpu.VMEM((CHIPS, *tile), F32),
            pltpu.VMEM((CHIPS, *row), F32),
            pltpu.VMEM((CHIPS, *tile), F32),
            pltpu.VMEM((HALF, *tile), F32),
            pltpu.VMEM((HALF * STATE, LANES), F32),
            pltpu.VMEM((CHUNKS * STATE, LANES), F32),
            pltpu.VMEM((ROWS * PITCH, LANES), F32),
            pltpu.VMEM((ROWS, SPAN), BF16),
            pltpu.VMEM((CUT_TILES, *row), F32),
            pltpu.VMEM((VARS, ROWS, SPAN), BF16),
            pltpu.VMEM((TILES, *row), F32),
            pltpu.VMEM((SHARDS, *row), F32),
            pltpu.VMEM(row, F32),
            pltpu.VMEM((SHARDS, *row), F32),
            pltpu.VMEM(row, F32),
            pltpu.VMEM((TILES, *row), F32),
            DMA((10,)),
        ]
        + [DMA] * 12
        + [
            DMA((VARS,)), DMA((CUT_TILES,)), DMA((TILES,)), DMA((VARS,)), DMA((SHARDS,)),
            DMA((VARS,)), DMA, DMA, DMA, DMA,
        ],
        compiler_params=pltpu.CompilerParams(
            collective_id=0, has_side_effects=True, vmem_limit_bytes=48 * 1024 * 1024
        ),
        name="mixer",
    )(
        patch_pos, patch_mode, clean_proj, corrupt_proj, rims, conv_weight, conv_bias[None],
        x_weight.T, dt_weight, dt_bias[None], a_log, d_skip[None],
    )
    return (patched[None], effect)


def solution(mesh):
    return jax.shard_map(
        shards,
        mesh=mesh,
        in_specs=(
            P("seq", None), P("seq", None), P("var", None), P("var"),
            P(), P(), P(), P(), P(), P(), P(),
        ),
        out_specs=(P("var", "seq", None), P("var", None)),
        check_vma=False,
    )
```

time: 106 us -> 83.8 us (0.79)
  Pallas kernels: 88.6 us -> 62.4 us
  local copies, waits for them, and re-layouts: 9.67 us -> 13 us
  waiting for transfers between devices: 0.01 us -> 1.59 us
  other arithmetic: 1.39 us -> 0.01 us
    pallas_call x4 -> x1, Pallas kernels: 88.6 us -> 62.4 us  [shards(): pl.pallas_call(kernel, out_shape=(jax.ShapeDtypeStruct((ROWS, INNER), BF1...]
    unnamed x22, local copies, waits for them, and re-layouts: 8.73 us -> 11.2 us
    slice x0 -> x2, local copies, waits for them, and re-layouts: none -> 1.79 us  [the longest x1 0.9 us: shards(): clean_proj[ROWS - 8:, :INNER]]
    ppermute x1, waiting for transfers between devices: 0.01 us -> 1.59 us  [shards(): rims = lax.ppermute(tails, 'seq', [(s, s + 1) for s in range(SHARDS - 1)])]
  transfers between devices with their start and end apart: 1 -> 1, of which waited for: 0 -> 1; matrix products, arithmetic and copies ran while one was open for 3% -> 0% of each run, Pallas kernels for 0% -> 0%
where the time goes in v2:
time: 83.8 us; the launch traced here: 83.2 us
  Pallas kernels  62.4 us (74%)
  local copies, waits for them, and re-layouts  13 us (16%)
  starting transfers between devices  4.92 us (6%)
  waiting for transfers between devices  1.59 us (2%)
  between operations  1.31 us (2%)
    pallas_call x1, Pallas kernels, shards(): pl.pallas_call(kernel, out_shape=(jax.ShapeDtypeStruct((ROWS, INNER), BF1...  62.4 us
    unnamed x22, local copies, waits for them, and re-layouts  11.2 us
    ppermute x1, starting transfers between devices, shards(): rims = lax.ppermute(tails, 'seq', [(s, s + 1) for s in range(SHARDS - 1)])  4.92 us
  transfers between devices with their start and end apart: 1, of which 1 were waited for; matrix products, arithmetic and copies ran while one was open for 0% of the time, Pallas kernels for 0%

profile of v2, /device:TPU:1, one launch (start us, length us, event | category | flops | bytes accessed | tf_op | source)
XLA Modules:
  0.0 83.2 jit_solution(5472673682055738504)
XLA Ops:
  0.6 0.9 %slice.6 = bf16[8,5120]{1,0:T(8,128)(2,1)S(1)} slice(bf16[32,10240]{1,0:T(8,128)(2,1)} %clean_in.1), slice={[24:32], [0:5120]} | slice | bytes 163840 | tf_op jit(solution)/shard_map/slice | solution.py:549
  1.5 0.9 %slice.7 = bf16[8,5120]{1,0:T(8,128)(2,1)S(1)} slice(bf16[32,10240]{1,0:T(8,128)(2,1)} %corrupt_in.1), slice={[24:32], [0:5120]} | slice | bytes 163840 | tf_op jit(solution)/shard_map/slice | solution.py:549
  2.4 4.9 %collective-permute-start = (bf16[16,5120]{1,0:T(8,128)(2,1)S(1)}, bf16[16,5120]{1,0:T(8,128)(2,1)S(1)}, u32[]{:S(2)}, u32[]{:S(2)}) collective-permute-start(bf16[16,5120]{1,0:T(8,128)(2,1)S(1)} %pad_maximum_fusion), channel_id=1, source_target_pairs={{0,4},{4,8},{8,12},{12,16},{16,20},{20,24},{24,28},{28,32},{32,36}... | collective-permute-start | bytes 491528 | tf_op jit(solution)/shard_map/ppermute | solution.py:550
  8.0 1.6 %collective-permute-done.rims_in = bf16[16,5120]{1,0:T(8,128)(2,1)S(1)} collective-permute-done((bf16[16,5120]{1,0:T(8,128)(2,1)S(1)}, bf16[16,5120]{1,0:T(8,128)(2,1)S(1)}, u32[]{:S(2)}, u32[]{:S(2)}) %collective-permute-start) | collective-permute-done | bytes 163872 | tf_op jit(solution)/shard_map/ppermute | solution.py:550
  9.6 0.0 copy-start
  9.6 1.5 %copy-done = bf16[5120,192]{0,1:T(8,128)(2,1)S(1)} copy-done((bf16[5120,192]{0,1:T(8,128)(2,1)S(1)}, bf16[5120,192]{0,1:T(8,128)(2,1)}, u32[]{:S(2)}) %copy-start) | copy-done | bytes 1966104
  11.2 0.0 copy-start.1
  11.2 1.4 %copy-done.1 = bf16[160,5120]{1,0:T(8,128)(2,1)S(1)} copy-done((bf16[160,5120]{1,0:T(8,128)(2,1)S(1)}, bf16[160,5120]{1,0:T(8,128)(2,1)}, u32[]{:S(2)}) %copy-start.1) | copy-done | bytes 1638424
  12.6 0.0 copy-start.2
  12.6 1.1 %copy-done.2 = bf16[32,10240]{1,0:T(8,128)(2,1)S(1)} copy-done((bf16[32,10240]{1,0:T(8,128)(2,1)S(1)}, bf16[32,10240]{1,0:T(8,128)(2,1)}, u32[]{:S(2)}) %copy-start.2) | copy-done | bytes 655384
  13.7 0.0 copy-start.3
  13.7 1.1 %copy-done.3 = bf16[32,10240]{1,0:T(8,128)(2,1)S(1)} copy-done((bf16[32,10240]{1,0:T(8,128)(2,1)S(1)}, bf16[32,10240]{1,0:T(8,128)(2,1)}, u32[]{:S(2)}) %copy-start.3) | copy-done | bytes 655384
  14.8 0.0 copy-start.4
  14.8 1.0 %copy-done.4 = f32[16,5120]{1,0:T(8,128)S(1)} copy-done((f32[16,5120]{1,0:T(8,128)S(1)}, f32[16,5120]{1,0:T(8,128)}, u32[]{:S(2)}) %copy-start.4) | copy-done | bytes 327704
  15.7 0.0 copy-start.5
  15.7 0.9 %copy-done.5 = f32[4,5120]{1,0:T(4,128)S(1)} copy-done((f32[4,5120]{1,0:T(4,128)S(1)}, f32[4,5120]{1,0:T(4,128)}, u32[]{:S(2)}) %copy-start.5) | copy-done | bytes 81944
  16.6 0.0 copy-start.6
  16.6 0.7 copy-done.6
  17.3 0.0 copy-start.7
  17.3 0.7 copy-done.7
  18.1 0.0 copy-start.8
  18.1 0.7 copy-done.8
  18.8 0.0 copy-start.9
  18.8 0.7 copy-done.9
  19.5 62.4 %mixer.1 = (bf16[32,5120]{1,0:T(8,128)(2,1)S(1)}, f32[1,5120]{1,0:T(1,128)S(1)}) custom-call(s32[1,16]{1,0:T(1,128)S(1)} %copy-done.9, s32[1]{0:T(128)S(6)} %copy.15.mode, bf16[32,10240]{1,0:T(8,128)(2,1)S(1)} %copy-done.2, bf16[32,10240]{1,0:T(8,128)(2,1)S(1)} %copy-done.3, bf16[16,5120]{1,0:T(8,128)(2,1)S(1)} %collective-permute-done.rims_in, ...), custom_call_target="tpu_custom_call" | custom-call | tf_op jit(solution)/shard_map/mixer/pallas_call | solution.py:553
  81.9 0.7 copy.16
  82.6 0.6 copy.17
  (1 shorter events, 0.0 us)
Async XLA Ops:
  2.4 7.2 %collective-permute-start = (bf16[16,5120]{1,0:T(8,128)(2,1)S(1)}, bf16[16,5120]{1,0:T(8,128)(2,1)S(1)}, u32[]{:S(2)}, u32[]{:S(2)}) collective-permute-start(bf16[16,5120]{1,0:T(8,128)(2,1)S(1)} %pad_maximum_fusion), channel_id=1, source_target_pairs={{0,4},{4,8},{8,12},{12,16},{16,20},{20,24},{24,28},{28,32},{32,36}... | collective-permute-start | bytes 491528 | tf_op jit(solution)/shard_map/ppermute | solution.py:550
  9.6 1.5 %copy-start = (bf16[5120,192]{0,1:T(8,128)(2,1)S(1)}, bf16[5120,192]{0,1:T(8,128)(2,1)}, u32[]{:S(2)}) copy-start(bf16[5120,192]{0,1:T(8,128)(2,1)} %param.19) | copy-start | bytes 5898244
  11.2 1.4 %copy-start.1 = (bf16[160,5120]{1,0:T(8,128)(2,1)S(1)}, bf16[160,5120]{1,0:T(8,128)(2,1)}, u32[]{:S(2)}) copy-start(bf16[160,5120]{1,0:T(8,128)(2,1)} %dt_w_in.1) | copy-start | bytes 4915204
  12.6 1.1 %copy-start.2 = (bf16[32,10240]{1,0:T(8,128)(2,1)S(1)}, bf16[32,10240]{1,0:T(8,128)(2,1)}, u32[]{:S(2)}) copy-start(bf16[32,10240]{1,0:T(8,128)(2,1)} %clean_in.1) | copy-start | bytes 1966084
  13.7 1.1 %copy-start.3 = (bf16[32,10240]{1,0:T(8,128)(2,1)S(1)}, bf16[32,10240]{1,0:T(8,128)(2,1)}, u32[]{:S(2)}) copy-start(bf16[32,10240]{1,0:T(8,128)(2,1)} %corrupt_in.1) | copy-start | bytes 1966084
  14.8 1.0 %copy-start.4 = (f32[16,5120]{1,0:T(8,128)S(1)}, f32[16,5120]{1,0:T(8,128)}, u32[]{:S(2)}) copy-start(f32[16,5120]{1,0:T(8,128)} %a_log_in.1) | copy-start | bytes 983044
  15.7 0.9 %copy-start.5 = (f32[4,5120]{1,0:T(4,128)S(1)}, f32[4,5120]{1,0:T(4,128)}, u32[]{:S(2)}) copy-start(f32[4,5120]{1,0:T(4,128)} %conv_w_in.1) | copy-start | bytes 245764
  16.6 0.7 copy-start.6
  17.3 0.7 copy-start.7
  18.1 0.7 copy-start.8
  18.8 0.7 copy-start.9

commit v3 on v2

--- a/solution.py
+++ b/solution.py
@@ -29,8 +29,12 @@
 TINY = 1e-06
 F32 = jnp.float32
 BF16 = jnp.bfloat16
-UNROLL = 4
+UNROLL = 8
 CLEAN, CORRUPT, PATCHED = 0, 1, 2
+STEPS = sorted(
+    ((dx, dz) for dx in range(4) for dz in range(8) if dx or dz),
+    key=lambda step: -(min(step[0], 4 - step[0]) + min(step[1], 8 - step[1])),
+)
 
 
 def cut_slot(run, tile):
@@ -101,18 +105,64 @@
     pltpu.make_async_copy(ref, ref, sem).wait()
 
 
+def halo_kernel(clean, corrupt, rims, send_sem, recv_sem):
+    me = lax.axis_index("seq")
+    v = lax.axis_index("var")
+    after = lax.rem(me + 1, SHARDS)
+    barrier = pltpu.get_barrier_semaphore()
+    for peer in (after, lax.rem(me + SHARDS - 1, SHARDS)):
+        pl.semaphore_signal(barrier, inc=1, device_id=(peer, v), device_id_type=MESH)
+    pl.semaphore_wait(barrier, 2)
+    copies = [
+        pltpu.make_async_remote_copy(
+            src_ref=src.at[ROWS - 8 :, :INNER], dst_ref=rims.at[i], send_sem=send_sem.at[i],
+            recv_sem=recv_sem.at[i], device_id=(after, v), device_id_type=MESH,
+        )
+        for i, src in enumerate((clean, corrupt))
+    ]
+    for copy in copies:
+        copy.start()
+    for copy in copies:
+        copy.wait()
+
+
+def emit_kernel(patched_in, effect_in, patched_out, effect_out, patched, effect, sems_in, sems_out):
+    cut = ROWS // 2
+    pieces = [
+        (patched_in.at[i * cut : (i + 1) * cut], patched.at[i * cut : (i + 1) * cut],
+         patched_out.at[i * cut : (i + 1) * cut])
+        for i in range(2)
+    ]
+    pieces.append((effect_in, effect, effect_out))
+    arrivals = [
+        pltpu.make_async_copy(src, here, sems_in.at[i]) for i, (src, here, _) in enumerate(pieces)
+    ]
+    departures = [
+        pltpu.make_async_copy(here, dst, sems_out.at[i]) for i, (_, here, dst) in enumerate(pieces)
+    ]
+    for arrival in arrivals:
+        arrival.start()
+    for arrival, departure in zip(arrivals, departures):
+        arrival.wait()
+        departure.start()
+    for departure in departures:
+        departure.wait()
+
+
 def kernel(
     pos, mode, clean_in, corrupt_in, rims_in, conv_w_in, conv_b_in, x_w_in, dt_w_in, dt_b_in,
     a_log_in, d_skip_in,
-    patched, effect,
-    clean, corrupt, rims, conv_w, conv_b, x_w, dt_w, dt_b, a_log, d_skip,
+    patched_out, effect,
+    patched, clean, corrupt, rims, conv_w, conv_b, x_w, dt_w, dt_b, a_log, d_skip,
     pad, acts, low, dts, us, bs, cs, rates, ends, totals,
     pair_ends, pair_totals, chip_ends, chip_totals, got_ends, got_totals,
     leaving, landed, across, start, ys,
-    cut, squares, whole, peaks, got_squares, spread, got_peaks, answer, answers,
+    cut, squares, whole, peaks, squares_z, line_squares, squares_x, spreads,
+    peaks_z, line_peaks, peaks_x,
     load_sem, send_pt, recv_pt, send_pe, recv_pe, send_ct, recv_ct, send_ce, recv_ce,
     send_in, recv_in, send_st, recv_st,
-    send_cut, send_sq, send_pk, send_sp, send_an, recv_cut, recv_sq, recv_pk, recv_sp, recv_an,
+    send_cut, recv_cut, send_sz, recv_sz, send_sx, recv_sx, send_sp, recv_sp,
+    send_pz, recv_pz, send_px, recv_px,
 ):
     me = lax.axis_index("seq")
     v = lax.axis_index("var")
@@ -136,16 +186,19 @@
     for load in loads:
         load.start()
 
+    def signal(peer, variant):
+        pl.semaphore_signal(barrier, inc=1, device_id=(peer, variant), device_id_type=MESH)
+
     def greet(k, _):
-        peer = lax.rem(me + k, SHARDS)
-        pl.semaphore_signal(barrier, inc=1, device_id=(peer, v), device_id_type=MESH)
-        return 0
-
-    lax.fori_loop(1, SHARDS, greet, 0)
+        signal(2 * lax.rem(chip + k, CHIPS) + core, v)
+        return 0
+
+    lax.fori_loop(1, CHIPS, greet, 0)
+    signal(mate, v)
+    for k in range(1, 4):
+        signal(lax.rem(mate + 16 * k, SHARDS), v)
     for k in range(1, VARS):
-        pl.semaphore_signal(
-            barrier, inc=1, device_id=(me, lax.rem(v + k, VARS)), device_id_type=MESH
-        )
+        signal(me, lax.rem(v + k, VARS))
 
     def to_variant(k, src, dst, send_sem, recv_sem):
         return pltpu.make_async_remote_copy(
@@ -160,6 +213,7 @@
         )
 
     first = me * ROWS
+    inside = me > 0
     hits = hit_rows(pos, first, ROWS)[:, :1]
     take = hits & (mode[0] != 1)
     take_gate = hits & (mode[0] != 0)
@@ -173,8 +227,8 @@
         cols = pl.ds(pl.multiple_of(i * width, width), width)
         sig_clean = clean[:, cols].astype(F32)
         sig_corrupt = corrupt[:, cols].astype(F32)
-        rim_clean = rims[0:8, cols].astype(F32)
-        rim_corrupt = rims[8:16, cols].astype(F32)
+        rim_clean = jnp.where(inside, rims[0, :, cols].astype(F32), 0.0)
+        rim_corrupt = jnp.where(inside, rims[1, :, cols].astype(F32), 0.0)
         pieces = (
             (rim_clean, sig_clean),
             (rim_corrupt, sig_corrupt),
@@ -252,7 +306,7 @@
     for slot in range(60, CHUNKS):
         place(slot, blank, blank, jnp.zeros((STATE, LANES), F32))
 
-    pl.semaphore_wait(barrier, SHARDS - 1 + VARS - 1)
+    pl.semaphore_wait(barrier, CHIPS - 1 + 1 + 3 + VARS - 1)
     theirs_3 = pl.ds(theirs, HALF)
     swap_totals = to_shard(mate, totals.at[theirs_3], pair_totals, send_pt, recv_pt)
     swap_totals.start()
@@ -293,8 +347,20 @@
     theirs_2 = pl.ds(pl.multiple_of(theirs * STATE, 8), HALF * STATE)
     swap_ends = to_shard(mate, ends.at[theirs_2], pair_ends, send_pe, recv_pe)
     swap_ends.start()
+    swap_totals.wait()
+
+    def chip_total(k, _):
+        chip_totals[k] = totals[mine + k] + pair_totals[k]
+        return 0
+
+    lax.fori_loop(0, HALF, chip_total, 0, unroll=4)
+    row_x, line_z = lax.div(chip, 8), lax.rem(chip, 8)
+    peers = [8 * lax.rem(row_x + dx, 4) + lax.rem(line_z + dz, 8) for dx, dz in STEPS]
+    pltpu.make_async_copy(chip_totals.at[chip], got_totals.at[chip], recv_ct).start()
+    for peer in peers:
+        target = 2 * peer + core
+        to_shard(target, chip_totals.at[peer], got_totals.at[chip], send_ct, recv_ct).start()
     local_pass(lax.div(mine, 8))
-    swap_totals.wait()
     leads = core == 0
 
     def my_summary(k):
@@ -310,11 +376,6 @@
             jnp.where(leads, other_end, own_end), jnp.where(leads, other_total, own_total),
         )
 
-    def chip_total(k, _):
-        chip_totals[k] = totals[mine + k] + pair_totals[k]
-        return 0
-
-    lax.fori_loop(0, HALF, chip_total, 0, unroll=4)
     swap_ends.wait()
 
     def chip_end(k, _):
@@ -323,17 +384,11 @@
         return 0
 
     lax.fori_loop(0, HALF, chip_end, 0, unroll=4)
-    pltpu.make_async_copy(chip_totals.at[chip], got_totals.at[chip], recv_ct).start()
     pltpu.make_async_copy(chip_ends.at[chip], got_ends.at[chip], recv_ce).start()
 
-    def spread_out(k, _):
-        peer = lax.rem(chip + k, CHIPS)
+    for peer in peers:
         target = 2 * peer + core
         to_shard(target, chip_ends.at[peer], got_ends.at[chip], send_ce, recv_ce).start()
-        to_shard(target, chip_totals.at[peer], got_totals.at[chip], send_ct, recv_ct).start()
-        return 0
-
-    lax.fori_loop(1, CHIPS, spread_out, 0)
     my_rate = rates[rate_at(mine + chip), :]
     wait_for(got_totals, recv_ct)
     wait_for(got_ends, recv_ce)
@@ -345,12 +400,8 @@
     lax.fori_loop(0, CHIPS, chain, jnp.zeros((STATE, LANES), F32), unroll=4)
     pltpu.make_async_copy(leaving.at[chip], landed.at[chip], recv_in).start()
 
-    def give(k, _):
-        peer = lax.rem(chip + k, CHIPS)
+    for peer in peers:
         to_shard(2 * peer + core, leaving.at[peer], landed.at[chip], send_in, recv_in).start()
-        return 0
-
-    lax.fori_loop(1, CHIPS, give, 0)
     wait_for(landed, recv_in)
 
     def enter(k, _):
@@ -385,6 +436,7 @@
 
     lax.fori_loop(5, GROUPS - 1, final_plain, 0)
     final_group(GROUPS - 1, mixed_reader(bs), mixed_reader(cs))
+    squares[...] = jnp.zeros_like(squares)
     for tile in range(CUT_TILES):
         at = v * SPAN + tile * LANES
         cols = pl.ds(pl.multiple_of(at, LANES), LANES)
@@ -400,27 +452,27 @@
         )
         cut[:, tile * LANES : (tile + 1) * LANES] = corrupt_out
         gap = clean_out.astype(F32) - corrupt_out.astype(F32)
-        squares[tile] = jnp.sum(gap * gap, axis=0, keepdims=True)
+        squares[tile : tile + 1, :] = jnp.sum(gap * gap, axis=0, keepdims=True)
 
     for k in range(1, VARS):
         to_variant(k, cut, whole.at[v], send_cut.at[k], recv_cut.at[k]).start()
 
-    def send_square(i, _):
-        peer = v * CUT_TILES + i
-
-        @pl.when(peer != me)
-        def _():
-            to_shard(
-                peer, squares.at[i], got_squares.at[me], send_sq.at[i], recv_sq
-            ).start()
-
-        @pl.when(peer == me)
-        def _():
-            pltpu.make_async_copy(squares.at[i], got_squares.at[me], recv_sq).start()
-
-        return 0
-
-    lax.fori_loop(0, CUT_TILES, send_square, 0)
+    plane_xc = 2 * lax.div(chip, 8) + core
+
+    def along_z(k):
+        return 16 * lax.div(chip, 8) + 2 * lax.rem(line_z + k, 8) + core
+
+    def across_xc(k):
+        other = lax.rem(plane_xc + k, 8)
+        return 16 * lax.div(other, 2) + 2 * line_z + lax.rem(other, 2)
+
+    def share(peer_of, slot, src, dst, send_sem, recv_sem):
+        for k in range(1, 8):
+            to_shard(peer_of(k), src, dst.at[slot], send_sem, recv_sem).start()
+        dst[slot] = src[...]
+
+    seven = pl.ds(0, 7)
+    share(along_z, line_z, squares, squares_z, send_sz, recv_sz)
     whole[v] = cut[...]
 
     lax.fori_loop(0, 5, final_plain, 0)
@@ -436,6 +488,8 @@
 
     lax.fori_loop(0, TILES, patched_tile, 0, unroll=2)
 
+    save = pltpu.make_async_copy(patched, patched_out, load_sem.at[0])
+    save.start()
     for k in range(1, VARS):
         to_variant(
             k, cut, whole.at[lax.rem(v + VARS - k, VARS)], send_cut.at[k], recv_cut.at[k]
@@ -446,90 +500,35 @@
             here = pl.ds(pl.multiple_of(i * LANES, LANES), LANES)
             there = pl.ds(pl.multiple_of(w * SPAN + i * LANES, LANES), LANES)
             gap = jnp.abs(patched[:, there].astype(F32) - whole[w, :, here].astype(F32))
-            peaks[w * CUT_TILES + i] = jnp.max(gap, axis=0, keepdims=True)
+            peaks[pl.ds(w * CUT_TILES + i, 1), :] = jnp.max(gap, axis=0, keepdims=True)
             return 0
 
         lax.fori_loop(0, CUT_TILES, peak_tile, 0, unroll=2)
 
-    def send_peak(c, _):
-        @pl.when(c != me)
-        def _():
-            to_shard(c, peaks.at[c], got_peaks.at[me], send_pk.at[c], recv_pk).start()
-
-        @pl.when(c == me)
-        def _():
-            pltpu.make_async_copy(peaks.at[c], got_peaks.at[me], recv_pk).start()
-
-        return 0
-
-    lax.fori_loop(0, TILES, send_peak, 0)
-
-    owner = lax.div(me, CUT_TILES)
-
-    @pl.when(owner == v)
-    def _():
-        wait_for(got_squares, recv_sq)
-        total = jnp.sum(got_squares[...], axis=0)
-        spread[...] = jnp.sqrt(total / (SHARDS * ROWS) + TINY)
-        for k in range(1, VARS):
-            to_variant(k, spread, spread, send_sp.at[k], recv_sp).start()
-
-    @pl.when((owner != v) & (me < TILES))
-    def _():
-        wait_for(spread, recv_sp)
-
-    @pl.when(me < TILES)
-    def _():
-        wait_for(got_peaks, recv_pk)
-        answer[...] = jnp.max(got_peaks[...], axis=0) / spread[...]
-        pltpu.make_async_copy(answer, answers.at[me], recv_an).start()
-
-        def share(k, _):
-            peer = lax.rem(me + k, SHARDS)
-            to_shard(peer, answer, answers.at[me], send_an.at[k], recv_an).start()
-            return 0
-
-        lax.fori_loop(1, SHARDS, share, 0)
-
-    wait_for(answers, recv_an)
-    for c in range(TILES):
-        effect[:, c * LANES : (c + 1) * LANES] = answers[c]
-
-    @pl.when(me < TILES)
-    def _():
-        def done(k, _):
-            peer = lax.rem(me + k, SHARDS)
-            to_shard(peer, answer, answers.at[me], send_an.at[k], recv_an).wait_send()
-            return 0
-
-        lax.fori_loop(1, SHARDS, done, 0)
-
-    @pl.when(owner == v)
-    def _():
-        for k in range(1, VARS):
-            to_variant(k, spread, spread, send_sp.at[k], recv_sp).wait_send()
-
-    def sent_peak(c, _):
-        @pl.when(c != me)
-        def _():
-            to_shard(c, peaks.at[c], got_peaks.at[me], send_pk.at[c], recv_pk).wait_send()
-
-        return 0
-
-    lax.fori_loop(0, TILES, sent_peak, 0)
-
-    def sent_square(i, _):
-        peer = v * CUT_TILES + i
-
-        @pl.when(peer != me)
-        def _():
-            to_shard(
-                peer, squares.at[i], got_squares.at[me], send_sq.at[i], recv_sq
-            ).wait_send()
-
-        return 0
-
-    lax.fori_loop(0, CUT_TILES, sent_square, 0)
+    share(along_z, line_z, peaks, peaks_z, send_pz, recv_pz)
+    wait_for(squares_z.at[seven], recv_sz)
+    line_squares[...] = jnp.sum(squares_z[...], axis=0)
+    share(across_xc, plane_xc, line_squares, squares_x, send_sx, recv_sx)
+    wait_for(peaks_z.at[seven], recv_pz)
+    line_peaks[...] = jnp.max(peaks_z[...], axis=0)
+    share(across_xc, plane_xc, line_peaks, peaks_x, send_px, recv_px)
+    wait_for(squares_x.at[seven], recv_sx)
+    spreads[v] = jnp.sqrt(jnp.sum(squares_x[...], axis=0) / (SHARDS * ROWS) + TINY)
+    for k in range(1, VARS):
+        to_variant(k, spreads.at[v], spreads.at[v], send_sp.at[k], recv_sp.at[k]).start()
+    wait_for(peaks_x.at[seven], recv_px)
+    for k in range(1, VARS):
+        there = spreads.at[lax.rem(v + VARS - k, VARS)]
+        to_variant(k, there, there, send_sp.at[k], recv_sp.at[k]).wait()
+    peak = jnp.max(peaks_x[...], axis=0)
+    for w in range(VARS):
+        rows = slice(w * CUT_TILES, (w + 1) * CUT_TILES)
+        effect[rows, :] = peak[rows, :] / spreads[w, :CUT_TILES, :]
+    save.wait()
+    wait_for(squares_z.at[seven], send_sz)
+    wait_for(squares_x.at[seven], send_sx)
+    wait_for(peaks_z.at[seven], send_pz)
+    wait_for(peaks_x.at[seven], send_px)
     others = pl.ds(0, CHIPS - 1)
     wait_for(chip_totals.at[others], send_ct)
     wait_for(chip_ends.at[others], send_ce)
@@ -546,22 +545,32 @@
     clean_proj, corrupt_proj, patch_pos, patch_mode, a_log, dt_bias,
     conv_weight, conv_bias, x_weight, dt_weight, d_skip,
 ):
-    tails = jnp.concatenate([clean_proj[ROWS - 8 :, :INNER], corrupt_proj[ROWS - 8 :, :INNER]])
-    rims = lax.ppermute(tails, "seq", [(s, s + 1) for s in range(SHARDS - 1)])
+    rims = pl.pallas_call(
+        halo_kernel,
+        out_shape=jax.ShapeDtypeStruct((2, 8, INNER), BF16),
+        in_specs=[HBM, HBM],
+        out_specs=HBM,
+        scratch_shapes=[DMA((2,)), DMA((2,))],
+        compiler_params=pltpu.CompilerParams(
+            collective_id=1, has_side_effects=True, vmem_limit_bytes=67_043_328
+        ),
+        name="halo",
+    )(clean_proj, corrupt_proj)
     row = (1, LANES)
     tile = (STATE, LANES)
     patched, effect = pl.pallas_call(
         kernel,
         out_shape=(
             jax.ShapeDtypeStruct((ROWS, INNER), BF16),
-            jax.ShapeDtypeStruct((1, INNER), F32),
+            jax.ShapeDtypeStruct((TILES, LANES), F32),
         ),
         in_specs=[SMEM, SMEM] + [HBM] * 10,
-        out_specs=(VMEM, VMEM),
+        out_specs=(HBM, VMEM),
         scratch_shapes=[
+            pltpu.VMEM((ROWS, INNER), BF16),
             pltpu.VMEM((ROWS, 2 * INNER), BF16),
             pltpu.VMEM((ROWS, 2 * INNER), BF16),
-            pltpu.VMEM((16, INNER), BF16),
+            pltpu.VMEM((2, 8, INNER), BF16),
             pltpu.VMEM((TAPS, INNER), F32),
             pltpu.VMEM((1, INNER), F32),
             pltpu.VMEM((RANK + 2 * STATE, INNER), BF16),
@@ -591,30 +600,46 @@
             pltpu.VMEM((CHUNKS * STATE, LANES), F32),
             pltpu.VMEM((ROWS * PITCH, LANES), F32),
             pltpu.VMEM((ROWS, SPAN), BF16),
-            pltpu.VMEM((CUT_TILES, *row), F32),
+            pltpu.VMEM((STATE, LANES), F32),
             pltpu.VMEM((VARS, ROWS, SPAN), BF16),
-            pltpu.VMEM((TILES, *row), F32),
-            pltpu.VMEM((SHARDS, *row), F32),
-            pltpu.VMEM(row, F32),
-            pltpu.VMEM((SHARDS, *row), F32),
-            pltpu.VMEM(row, F32),
-            pltpu.VMEM((TILES, *row), F32),
+            pltpu.VMEM((TILES, LANES), F32),
+            pltpu.VMEM((8, STATE, LANES), F32),
+            pltpu.VMEM((STATE, LANES), F32),
+            pltpu.VMEM((8, STATE, LANES), F32),
+            pltpu.VMEM((VARS, STATE, LANES), F32),
+            pltpu.VMEM((8, TILES, LANES), F32),
+            pltpu.VMEM((TILES, LANES), F32),
+            pltpu.VMEM((8, TILES, LANES), F32),
             DMA((10,)),
         ]
         + [DMA] * 12
-        + [
-            DMA((VARS,)), DMA((CUT_TILES,)), DMA((TILES,)), DMA((VARS,)), DMA((SHARDS,)),
-            DMA((VARS,)), DMA, DMA, DMA, DMA,
-        ],
+        + [DMA((VARS,)), DMA((VARS,))]
+        + [DMA] * 4
+        + [DMA((VARS,)), DMA((VARS,))]
+        + [DMA] * 4,
         compiler_params=pltpu.CompilerParams(
-            collective_id=0, has_side_effects=True, vmem_limit_bytes=48 * 1024 * 1024
+            collective_id=0, has_side_effects=True, vmem_limit_bytes=67_043_328
         ),
         name="mixer",
     )(
         patch_pos, patch_mode, clean_proj, corrupt_proj, rims, conv_weight, conv_bias[None],
         x_weight.T, dt_weight, dt_bias[None], a_log, d_skip[None],
     )
-    return (patched[None], effect)
+    patched, effect = pl.pallas_call(
+        emit_kernel,
+        out_shape=(
+            jax.ShapeDtypeStruct((ROWS, INNER), BF16),
+            jax.ShapeDtypeStruct((TILES, LANES), F32),
+        ),
+        in_specs=[HBM, HBM],
+        out_specs=(HBM, HBM),
+        scratch_shapes=[
+            pltpu.VMEM((ROWS, INNER), BF16), pltpu.VMEM((TILES, LANES), F32), DMA((3,)), DMA((3,)),
+        ],
+        compiler_params=pltpu.CompilerParams(vmem_limit_bytes=67_043_328),
+        name="emit",
+    )(patched, effect)
+    return (patched[None], effect.reshape(1, INNER))
 
 
 def solution(mesh):

time: 83.8 us -> 67.3 us (0.80)
  local copies, waits for them, and re-layouts: 13 us -> 0 us
  starting transfers between devices: 4.92 us -> 0 us
  Pallas kernels: 62.4 us -> 65.9 us
  waiting for transfers between devices: 1.59 us -> 0 us
    pallas_call x0 -> x2, Pallas kernels: none -> 12.1 us  [the longest x1 10.4 us: shards(): pl.pallas_call(halo_kernel, out_shape=jax.ShapeDtypeStruct((2, 8, INNER),...]
    unnamed x22 -> x0, local copies, waits for them, and re-layouts: 11.2 us -> none
    pallas_call x1, Pallas kernels: 62.4 us -> 53.8 us  [shards(): pl.pallas_call(kernel, out_shape=(jax.ShapeDtypeStruct((ROWS, INNER), BF1...]
    ppermute x1 -> x0, starting transfers between devices: 4.92 us -> none  [shards(): rims = lax.ppermute(tails, 'seq', [(s, s + 1) for s in range(SHARDS - 1)])]
    slice x2 -> x0, local copies, waits for them, and re-layouts: 1.79 us -> none  [the longest x1 0.9 us: shards(): clean_proj[ROWS - 8:, :INNER]]
    ppermute x1 -> x0, waiting for transfers between devices: 1.59 us -> none  [shards(): rims = lax.ppermute(tails, 'seq', [(s, s + 1) for s in range(SHARDS - 1)])]
  transfers between devices with their start and end apart: 1 -> 0, of which waited for: 1 -> 0; matrix products, arithmetic and copies ran while one was open for 0% -> 0% of each run, Pallas kernels for 0% -> 0%
where the time goes in v3:
time: 67.3 us; the launch traced here: 67.2 us
  Pallas kernels  65.9 us (98%)
  between operations  1.29 us (2%)
    pallas_call x1, Pallas kernels, shards(): pl.pallas_call(kernel, out_shape=(jax.ShapeDtypeStruct((ROWS, INNER), BF1...  53.8 us
    pallas_call x1, Pallas kernels, shards(): pl.pallas_call(halo_kernel, out_shape=jax.ShapeDtypeStruct((2, 8, INNER),...  10.4 us
    pallas_call x1, Pallas kernels, shards(): pl.pallas_call(emit_kernel, out_shape=(jax.ShapeDtypeStruct((ROWS, INNER)...  1.71 us

profile of v3, /device:TPU:1, one launch (start us, length us, event | category | flops | bytes accessed | tf_op | source)
XLA Modules:
  0.0 67.2 jit_solution(13544630482235949479)
XLA Ops:
  1.3 10.4 %halo.1.rims_in = bf16[2,8,5120]{2,1,0:T(8,128)(2,1)} custom-call(bf16[32,10240]{1,0:T(8,128)(2,1)} %clean_in.1, bf16[32,10240]{1,0:T(8,128)(2,1)} %corrupt_in.1), custom_call_target="tpu_custom_call" | custom-call | tf_op jit(solution)/shard_map/halo/pallas_call | solution.py:548
  11.7 53.8 %mixer.1 = (bf16[32,5120]{1,0:T(8,128)(2,1)}, f32[40,128]{1,0:T(8,128)}) custom-call(s32[1,16]{1,0:T(1,128)} %pos.1, s32[1]{0:T(128)S(6)} %copy.13.mode, bf16[32,10240]{1,0:T(8,128)(2,1)} %clean_in.1, bf16[32,10240]{1,0:T(8,128)(2,1)} %corrupt_in.1, bf16[2,8,5120]{2,1,0:T(8,128)(2,1)} %halo.1.rims_in, f32[4,5120]{1,0:T(4,128)} %conv_w_in.1, ...), custom_call_target="tpu_custom_call" | custom-call | tf_op jit(solution)/shard_map/mixer/pallas_call | solution.py:561
  65.5 1.7 %emit.1 = (bf16[32,5120]{1,0:T(8,128)(2,1)}, f32[40,128]{1,0:T(8,128)}) custom-call(bf16[32,5120]{1,0:T(8,128)(2,1)} %get-tuple-element.6.patched_in, f32[40,128]{1,0:T(8,128)} %get-tuple-element.7.effect_in), custom_call_target="tpu_custom_call" | custom-call | tf_op jit(solution)/shard_map/emit/pallas_call | solution.py:628

commit v4 on v3

--- a/solution.py
+++ b/solution.py
@@ -153,8 +153,8 @@
     pos, mode, clean_in, corrupt_in, rims_in, conv_w_in, conv_b_in, x_w_in, dt_w_in, dt_b_in,
     a_log_in, d_skip_in,
     patched_out, effect,
-    patched, clean, corrupt, rims, conv_w, conv_b, x_w, dt_w, dt_b, a_log, d_skip,
-    pad, acts, low, dts, us, bs, cs, rates, ends, totals,
+    patched, clean, corrupt, clean_gate, corrupt_gate, rims, conv_w, conv_b, x_w, dt_w, dt_b, a_log, d_skip,
+    pad, acts, low, maps, weights, base, gates, dts, us, bs, cs, rates, ends, totals,
     pair_ends, pair_totals, chip_ends, chip_totals, got_ends, got_totals,
     leaving, landed, across, start, ys,
     cut, squares, whole, peaks, squares_z, line_squares, squares_x, spreads,
@@ -177,9 +177,11 @@
         pltpu.make_async_copy(src, dst, load_sem.at[i])
         for i, (src, dst) in enumerate(
             (
-                (clean_in, clean), (corrupt_in, corrupt), (rims_in, rims), (conv_w_in, conv_w),
+                (clean_in.at[:, :INNER], clean), (corrupt_in.at[:, :INNER], corrupt),
+                (rims_in, rims), (conv_w_in, conv_w),
                 (conv_b_in, conv_b), (x_w_in, x_w), (dt_w_in, dt_w), (dt_b_in, dt_b),
                 (a_log_in, a_log), (d_skip_in, d_skip),
+                (clean_in.at[:, INNER:], clean_gate), (corrupt_in.at[:, INNER:], corrupt_gate),
             )
         )
     ]
@@ -223,7 +225,10 @@
         load.wait()
     width = 512
 
-    def conv(i, _):
+    width = 512
+    span = 8 + ROWS
+
+    def fill(i, _):
         cols = pl.ds(pl.multiple_of(i * width, width), width)
         sig_clean = clean[:, cols].astype(F32)
         sig_corrupt = corrupt[:, cols].astype(F32)
@@ -237,23 +242,35 @@
                 jnp.where(take, sig_clean, sig_corrupt),
             ),
         )
+        for run, (rim, sig) in enumerate(pieces):
+            for k in range(width // LANES):
+                part = slice(k * LANES, (k + 1) * LANES)
+                at = pl.multiple_of((run * TILES + i * (width // LANES) + k) * span, 8)
+                pad[pl.ds(at, 8), :] = rim[:, part]
+                pad[pl.ds(at + 8, ROWS), :] = sig[:, part]
+        return 0
+
+    lax.fori_loop(0, INNER // width, fill, 0)
+
+    def conv(tile, _):
+        cols = pl.ds(pl.multiple_of(tile * LANES, LANES), LANES)
         bias = conv_b[:, cols]
-        for run, (rim, sig) in enumerate(pieces):
-            pad[run, 0:8, :] = rim
-            pad[run, 8:, :] = sig
-            total = bias + conv_w[0:1, cols] * pad[run, 5 : 5 + ROWS, :]
+        for run in range(3):
+            at = (run * TILES + tile) * span + 8 - (TAPS - 1)
+            total = bias + conv_w[0:1, cols] * pad[pl.ds(at, ROWS), :]
             for k in range(1, TAPS):
-                total = total + conv_w[k : k + 1, cols] * pad[run, 5 + k : 5 + k + ROWS, :]
+                total = total + conv_w[k : k + 1, cols] * pad[pl.ds(at + k, ROWS), :]
             acts[run * ROWS : (run + 1) * ROWS, cols] = silu(total).astype(BF16)
         return 0
 
-    lax.fori_loop(0, INNER // width, conv, 0)
+    lax.fori_loop(0, TILES, conv, 0, unroll=4)
 
     loads[5].wait()
     projected = lax.dot_general(
         acts[...], x_w[...], (((1,), (1,)), ((), ())), preferred_element_type=F32
     )
     low[...] = projected[:, :RANK].astype(BF16)
+    maps[...] = projected[:, RANK + STATE :]
     for run in range(3):
         part = projected[run * ROWS : (run + 1) * ROWS]
         for n in range(STATE):
@@ -261,9 +278,6 @@
             bs[pl.ds(at, ROWS, stride=SPLAT), :] = jnp.broadcast_to(
                 part[:, RANK + n : RANK + n + 1], (ROWS, LANES)
             )
-            cs[pl.ds(at, ROWS, stride=SPLAT), :] = jnp.broadcast_to(
-                part[:, RANK + STATE + n : RANK + STATE + n + 1], (ROWS, LANES)
-            )
 
     for load in loads[6:9]:
         load.wait()
@@ -277,7 +291,7 @@
         totals[slot] = jnp.sum(steps, axis=0, keepdims=True)
         rates[rate_at(slot), :] = jnp.exp(log_rate) * (-LOG2E)
 
-    wide = 640
+    wide = 1280
 
     def patched_steps(i, _):
         cols = pl.ds(pl.multiple_of(i * wide, wide), wide)
@@ -390,6 +404,22 @@
         target = 2 * peer + core
         to_shard(target, chip_ends.at[peer], got_ends.at[chip], send_ce, recv_ce).start()
     my_rate = rates[rate_at(mine + chip), :]
+    for run in range(3):
+        for n in range(STATE):
+            cs[pl.ds(run * ROWS * SPLAT + n, ROWS, stride=SPLAT), :] = jnp.broadcast_to(
+                maps[run * ROWS : (run + 1) * ROWS, n : n + 1], (ROWS, LANES)
+            )
+
+    def local_readout(group, drive, read):
+        scan_group(dts, us, rates_of(group), group, (zero,) * STATE, drive, read, ys)
+
+    def plain_readout(group, _):
+        at = run_base(group)
+        local_readout(group, splat_reader(bs, at), splat_reader(cs, at))
+        return 0
+
+    lax.fori_loop(0, GROUPS - 1, plain_readout, 0)
+    local_readout(GROUPS - 1, mixed_reader(bs), mixed_reader(cs))
     wait_for(got_totals, recv_ct)
     wait_for(got_ends, recv_ce)
 
@@ -402,6 +432,50 @@
 
     for peer in peers:
         to_shard(2 * peer + core, leaving.at[peer], landed.at[chip], send_in, recv_in).start()
+    def entry_weights(group, read):
+        rate = rates_of(group)
+
+        def step(t, run_total):
+            row = pl.multiple_of(t * PITCH + group * 8, 8)
+            run_total = run_total + dts[pl.ds(row, 8), :]
+            at = (group * ROWS + t) * (STATE * 8)
+            for n in range(STATE):
+                weights[pl.ds(pl.multiple_of(at + n * 8, 8), 8), :] = read(t, n) * jnp.exp2(
+                    run_total * rate[n]
+                )
+            return run_total
+
+        lax.fori_loop(0, ROWS, step, zero, unroll=4)
+
+    def plain_weights(group, _):
+        entry_weights(group, splat_reader(cs, run_base(group)))
+        return 0
+
+    lax.fori_loop(0, GROUPS - 1, plain_weights, 0)
+    entry_weights(GROUPS - 1, mixed_reader(cs))
+    for load in loads[9:]:
+        load.wait()
+
+    def prepare(slot, act, skip, gate):
+        rows = pl.ds(pl.multiple_of(slot * ROWS, 8), ROWS)
+        base[rows, :] = ys[pl.ds(slot, ROWS, stride=PITCH), :] + skip * act
+        gates[rows, :] = silu(gate)
+
+    for run, gate_rows in ((CLEAN, clean_gate), (CORRUPT, corrupt_gate)):
+        for tile in range(CUT_TILES):
+            cols = pl.ds(pl.multiple_of(v * SPAN + tile * LANES, LANES), LANES)
+            act = acts[run * ROWS : (run + 1) * ROWS, cols].astype(F32)
+            prepare(cut_slot(run, tile), act, d_skip[:, cols], gate_rows[:, cols].astype(F32))
+
+    def prepare_patched(tile, _):
+        cols = pl.ds(pl.multiple_of(tile * LANES, LANES), LANES)
+        gate = jnp.where(
+            take_gate, clean_gate[:, cols].astype(F32), corrupt_gate[:, cols].astype(F32)
+        )
+        prepare(tile, acts[2 * ROWS :, cols].astype(F32), d_skip[:, cols], gate)
+        return 0
+
+    lax.fori_loop(0, TILES, prepare_patched, 0, unroll=2)
     wait_for(landed, recv_in)
 
     def enter(k, _):
@@ -417,45 +491,55 @@
     mine_2 = pl.ds(pl.multiple_of(mine * STATE, 8), HALF * STATE)
     swap_start = to_shard(mate, across, start.at[mine_2], send_st, recv_st)
     swap_start.start()
-    loads[9].wait()
     swap_start.wait()
 
-    def final_group(group, drive, readout):
-        base = group * (STATE * 8)
-        state = tuple(start[pl.ds(base + n, 8, stride=STATE), :] for n in range(STATE))
-        scan_group(dts, us, rates_of(group), group, state, drive, readout, ys)
-
-    def final_plain(group, _):
-        base = run_base(group)
-        final_group(group, splat_reader(bs, base), splat_reader(cs, base))
-        return 0
-
-    def result(slot, act, skip, gate):
+    def final_group(group, _):
+        at = group * (STATE * 8)
+        state = [start[pl.ds(at + n, 8, stride=STATE), :] for n in range(STATE)]
+
+        def step(t, _):
+            at = (group * ROWS + t) * (STATE * 8)
+            total = None
+            for n in range(STATE):
+                term = weights[pl.ds(pl.multiple_of(at + n * 8, 8), 8), :] * state[n]
+                total = term if total is None else total + term
+            ys[pl.ds(pl.multiple_of(t * PITCH + group * 8, 8), 8), :] = total
+            return 0
+
+        lax.fori_loop(0, ROWS, step, 0, unroll=8)
+        return 0
+
+    def result(slot):
+        rows = pl.ds(pl.multiple_of(slot * ROWS, 8), ROWS)
         y = ys[pl.ds(slot, ROWS, stride=PITCH), :]
-        return ((y + skip * act) * silu(gate)).astype(BF16)
-
-    lax.fori_loop(5, GROUPS - 1, final_plain, 0)
-    final_group(GROUPS - 1, mixed_reader(bs), mixed_reader(cs))
+        return ((y + base[rows, :]) * gates[rows, :]).astype(BF16)
+
+    lax.fori_loop(6, GROUPS, final_group, 0)
+
+    for tile in range(CUT_TILES):
+        cut[:, tile * LANES : (tile + 1) * LANES] = result(cut_slot(CORRUPT, tile))
+    before, after = lax.rem(v + VARS - 1, VARS), lax.rem(v + 1, VARS)
+    half = ROWS // 2
+    upper, lower = pl.ds(0, half), pl.ds(half, half)
+
+    def send_rows(k, i, slot, rows, src):
+        dst = whole.at[slot, rows]
+        return to_variant(k, src if src is not None else dst, dst, send_cut.at[i], recv_cut.at[i])
+
+    directs = [
+        send_rows(k, i, v, rows, cut.at[rows])
+        for i, (k, rows) in enumerate(
+            ((1, upper), (VARS - 1, lower), (1, lower), (VARS - 1, upper))
+        )
+    ]
+    for direct in directs:
+        direct.start()
+    final_group(5, 0)
     squares[...] = jnp.zeros_like(squares)
     for tile in range(CUT_TILES):
-        at = v * SPAN + tile * LANES
-        cols = pl.ds(pl.multiple_of(at, LANES), LANES)
-        gate_cols = pl.ds(pl.multiple_of(INNER + at, LANES), LANES)
-        skip = d_skip[:, cols]
-        clean_out = result(
-            cut_slot(CLEAN, tile), acts[:ROWS, cols].astype(F32), skip,
-            clean[:, gate_cols].astype(F32),
-        )
-        corrupt_out = result(
-            cut_slot(CORRUPT, tile), acts[ROWS : 2 * ROWS, cols].astype(F32), skip,
-            corrupt[:, gate_cols].astype(F32),
-        )
-        cut[:, tile * LANES : (tile + 1) * LANES] = corrupt_out
-        gap = clean_out.astype(F32) - corrupt_out.astype(F32)
+        gap = result(cut_slot(CLEAN, tile)).astype(F32)
+        gap = gap - cut[:, tile * LANES : (tile + 1) * LANES].astype(F32)
         squares[tile : tile + 1, :] = jnp.sum(gap * gap, axis=0, keepdims=True)
-
-    for k in range(1, VARS):
-        to_variant(k, cut, whole.at[v], send_cut.at[k], recv_cut.at[k]).start()
 
     plane_xc = 2 * lax.div(chip, 8) + core
 
@@ -475,25 +559,28 @@
     share(along_z, line_z, squares, squares_z, send_sz, recv_sz)
     whole[v] = cut[...]
 
-    lax.fori_loop(0, 5, final_plain, 0)
-
+    lax.fori_loop(0, 5, final_group, 0)
     def patched_tile(tile, _):
         cols = pl.ds(pl.multiple_of(tile * LANES, LANES), LANES)
-        gate_cols = pl.ds(pl.multiple_of(INNER + tile * LANES, LANES), LANES)
-        gate = jnp.where(
-            take_gate, clean[:, gate_cols].astype(F32), corrupt[:, gate_cols].astype(F32)
-        )
-        patched[:, cols] = result(tile, acts[2 * ROWS :, cols].astype(F32), d_skip[:, cols], gate)
-        return 0
-
-    lax.fori_loop(0, TILES, patched_tile, 0, unroll=2)
+        patched[:, cols] = result(tile)
+        return 0
+
+    lax.fori_loop(0, TILES, patched_tile, 0, unroll=4)
 
     save = pltpu.make_async_copy(patched, patched_out, load_sem.at[0])
     save.start()
-    for k in range(1, VARS):
-        to_variant(
-            k, cut, whole.at[lax.rem(v + VARS - k, VARS)], send_cut.at[k], recv_cut.at[k]
-        ).wait()
+    relays = [
+        send_rows(1, 4, before, upper, None), send_rows(VARS - 1, 5, after, lower, None)
+    ]
+    for direct, relay in zip(directs, relays):
+        direct.wait_recv()
+        relay.start()
+    for direct in directs[2:]:
+        direct.wait_recv()
+    for direct in directs:
+        direct.wait_send()
+    for relay in relays:
+        relay.wait()
 
     for w in range(VARS):
         def peak_tile(i, _):
@@ -568,8 +655,10 @@
         out_specs=(HBM, VMEM),
         scratch_shapes=[
             pltpu.VMEM((ROWS, INNER), BF16),
-            pltpu.VMEM((ROWS, 2 * INNER), BF16),
-            pltpu.VMEM((ROWS, 2 * INNER), BF16),
+            pltpu.VMEM((ROWS, INNER), BF16),
+            pltpu.VMEM((ROWS, INNER), BF16),
+            pltpu.VMEM((ROWS, INNER), BF16),
+            pltpu.VMEM((ROWS, INNER), BF16),
             pltpu.VMEM((2, 8, INNER), BF16),
             pltpu.VMEM((TAPS, INNER), F32),
             pltpu.VMEM((1, INNER), F32),
@@ -578,9 +667,13 @@
             pltpu.VMEM((1, INNER), F32),
             pltpu.VMEM((STATE, INNER), F32),
             pltpu.VMEM((1, INNER), F32),
-            pltpu.VMEM((3, 8 + ROWS, 512), F32),
+            pltpu.VMEM((3 * TILES * (8 + ROWS), LANES), F32),
             pltpu.VMEM((3 * ROWS, INNER), BF16),
             pltpu.VMEM((3 * ROWS, RANK), BF16),
+            pltpu.VMEM((3 * ROWS, STATE), F32),
+            pltpu.VMEM((GROUPS * ROWS * STATE * 8, LANES), F32),
+            pltpu.VMEM((CHUNKS * ROWS, LANES), F32),
+            pltpu.VMEM((CHUNKS * ROWS, LANES), F32),
             pltpu.VMEM((ROWS * PITCH, LANES), F32),
             pltpu.VMEM((ROWS * PITCH, LANES), F32),
             pltpu.VMEM((3 * ROWS * SPLAT + 8, LANES), F32),
@@ -610,10 +703,10 @@
             pltpu.VMEM((8, TILES, LANES), F32),
             pltpu.VMEM((TILES, LANES), F32),
             pltpu.VMEM((8, TILES, LANES), F32),
-            DMA((10,)),
+            DMA((12,)),
         ]
         + [DMA] * 12
-        + [DMA((VARS,)), DMA((VARS,))]
+        + [DMA((6,)), DMA((6,))]
         + [DMA] * 4
         + [DMA((VARS,)), DMA((VARS,))]
         + [DMA] * 4,

time: 67.3 us -> 62.9 us (0.935)
  Pallas kernels: 65.9 us -> 61.5 us
    pallas_call x1, Pallas kernels: 53.8 us -> 49.3 us  [shards(): pl.pallas_call(kernel, out_shape=(jax.ShapeDtypeStruct((ROWS, INNER), BF1...]
where the time goes in v4:
time: 62.9 us; the launch traced here: 62.8 us
  Pallas kernels  61.5 us (98%)
  between operations  1.29 us (2%)
    pallas_call x1, Pallas kernels, shards(): pl.pallas_call(kernel, out_shape=(jax.ShapeDtypeStruct((ROWS, INNER), BF1...  49.3 us
    pallas_call x1, Pallas kernels, shards(): pl.pallas_call(halo_kernel, out_shape=jax.ShapeDtypeStruct((2, 8, INNER),...  10.4 us
    pallas_call x1, Pallas kernels, shards(): pl.pallas_call(emit_kernel, out_shape=(jax.ShapeDtypeStruct((ROWS, INNER)...  1.71 us

profile of v4, /device:TPU:1, one launch (start us, length us, event | category | flops | bytes accessed | tf_op | source)
XLA Modules:
  0.0 62.8 jit_solution(16723668780520450668)
XLA Ops:
  1.3 10.4 %halo.1.rims_in = bf16[2,8,5120]{2,1,0:T(8,128)(2,1)} custom-call(bf16[32,10240]{1,0:T(8,128)(2,1)} %clean_in.1, bf16[32,10240]{1,0:T(8,128)(2,1)} %corrupt_in.1), custom_call_target="tpu_custom_call" | custom-call | tf_op jit(solution)/shard_map/halo/pallas_call | solution.py:635
  11.7 49.3 %mixer.1 = (bf16[32,5120]{1,0:T(8,128)(2,1)}, f32[40,128]{1,0:T(8,128)}) custom-call(s32[1,16]{1,0:T(1,128)} %pos.1, s32[1]{0:T(128)S(6)} %copy.13.mode, bf16[32,10240]{1,0:T(8,128)(2,1)} %clean_in.1, bf16[32,10240]{1,0:T(8,128)(2,1)} %corrupt_in.1, bf16[2,8,5120]{2,1,0:T(8,128)(2,1)} %halo.1.rims_in, f32[4,5120]{1,0:T(4,128)} %conv_w_in.1, ...), custom_call_target="tpu_custom_call" | custom-call | tf_op jit(solution)/shard_map/mixer/pallas_call | solution.py:648
  61.0 1.7 %emit.1 = (bf16[32,5120]{1,0:T(8,128)(2,1)}, f32[40,128]{1,0:T(8,128)}) custom-call(bf16[32,5120]{1,0:T(8,128)(2,1)} %get-tuple-element.6.patched_in, f32[40,128]{1,0:T(8,128)} %get-tuple-element.7.effect_in), custom_call_target="tpu_custom_call" | custom-call | tf_op jit(solution)/shard_map/emit/pallas_call | solution.py:721

commit v5 on v4

--- a/solution.py
+++ b/solution.py
@@ -105,25 +105,52 @@
     pltpu.make_async_copy(ref, ref, sem).wait()
 
 
-def halo_kernel(clean, corrupt, rims, send_sem, recv_sem):
+def halo_kernel(clean, corrupt, rims, ends, wide, packed, load_sem, send_sem, recv_sem):
     me = lax.axis_index("seq")
     v = lax.axis_index("var")
-    after = lax.rem(me + 1, SHARDS)
+    after = lax.min(me + 1, SHARDS - 1)
     barrier = pltpu.get_barrier_semaphore()
-    for peer in (after, lax.rem(me + SHARDS - 1, SHARDS)):
-        pl.semaphore_signal(barrier, inc=1, device_id=(peer, v), device_id_type=MESH)
-    pl.semaphore_wait(barrier, 2)
-    copies = [
-        pltpu.make_async_remote_copy(
-            src_ref=src.at[ROWS - 8 :, :INNER], dst_ref=rims.at[i], send_sem=send_sem.at[i],
-            recv_sem=recv_sem.at[i], device_id=(after, v), device_id_type=MESH,
-        )
+    loads = [
+        pltpu.make_async_copy(src.at[ROWS - 8 :, :INNER], ends.at[i], load_sem.at[i])
         for i, src in enumerate((clean, corrupt))
     ]
-    for copy in copies:
+    for load in loads:
+        load.start()
+    has_next, has_last = me < SHARDS - 1, me > 0
+
+    def signal(peer):
+        pl.semaphore_signal(barrier, inc=1, device_id=(peer, v), device_id_type=MESH)
+
+    @pl.when(has_next)
+    def _():
+        signal(me + 1)
+
+    @pl.when(has_last)
+    def _():
+        signal(me - 1)
+
+    for load in loads:
+        load.wait()
+    margin = TAPS - 1
+    wide[...] = jnp.zeros_like(wide)
+    for i in range(2):
+        wide[i * margin : (i + 1) * margin, :] = ends[i].astype(F32)[8 - margin :, :]
+    packed[...] = wide[...].astype(BF16)
+
+    pl.semaphore_wait(barrier, lax.min(me, 1) + lax.min(SHARDS - 1 - me, 1))
+    copy = pltpu.make_async_remote_copy(
+        src_ref=packed, dst_ref=rims, send_sem=send_sem, recv_sem=recv_sem,
+        device_id=(after, v), device_id_type=MESH,
+    )
+
+    @pl.when(has_next)
+    def _():
         copy.start()
-    for copy in copies:
-        copy.wait()
+        copy.wait_send()
+
+    @pl.when(has_last)
+    def _():
+        copy.wait_recv()
 
 
 def emit_kernel(patched_in, effect_in, patched_out, effect_out, patched, effect, sems_in, sems_out):
@@ -158,11 +185,11 @@
     pair_ends, pair_totals, chip_ends, chip_totals, got_ends, got_totals,
     leaving, landed, across, start, ys,
     cut, squares, whole, peaks, squares_z, line_squares, squares_x, spreads,
-    peaks_z, line_peaks, peaks_x,
+    peaks_z, line_peaks, peaks_x, pair_squares, chip_squares, pair_peaks, chip_peaks, answer,
     load_sem, send_pt, recv_pt, send_pe, recv_pe, send_ct, recv_ct, send_ce, recv_ce,
     send_in, recv_in, send_st, recv_st,
     send_cut, recv_cut, send_sz, recv_sz, send_sx, recv_sx, send_sp, recv_sp,
-    send_pz, recv_pz, send_px, recv_px,
+    send_pz, recv_pz, send_px, recv_px, send_qq, recv_qq, send_pp, recv_pp, send_an, recv_an,
 ):
     me = lax.axis_index("seq")
     v = lax.axis_index("var")
@@ -197,8 +224,6 @@
 
     lax.fori_loop(1, CHIPS, greet, 0)
     signal(mate, v)
-    for k in range(1, 4):
-        signal(lax.rem(mate + 16 * k, SHARDS), v)
     for k in range(1, VARS):
         signal(me, lax.rem(v + k, VARS))
 
@@ -215,11 +240,12 @@
         )
 
     first = me * ROWS
+    margin = TAPS - 1
     inside = me > 0
     hits = hit_rows(pos, first, ROWS)[:, :1]
     take = hits & (mode[0] != 1)
     take_gate = hits & (mode[0] != 0)
-    take_rim = hit_rows(pos, first - 8, 8)[:, :1] & (mode[0] != 1)
+    take_rim = hit_rows(pos, first - margin, margin)[:, :1] & (mode[0] != 1)
 
     for load in loads[:5]:
         load.wait()
@@ -232,8 +258,8 @@
         cols = pl.ds(pl.multiple_of(i * width, width), width)
         sig_clean = clean[:, cols].astype(F32)
         sig_corrupt = corrupt[:, cols].astype(F32)
-        rim_clean = jnp.where(inside, rims[0, :, cols].astype(F32), 0.0)
-        rim_corrupt = jnp.where(inside, rims[1, :, cols].astype(F32), 0.0)
+        rim = jnp.where(inside, rims[:, cols].astype(F32), 0.0)
+        rim_clean, rim_corrupt = rim[:margin], rim[margin : 2 * margin]
         pieces = (
             (rim_clean, sig_clean),
             (rim_corrupt, sig_corrupt),
@@ -246,7 +272,7 @@
             for k in range(width // LANES):
                 part = slice(k * LANES, (k + 1) * LANES)
                 at = pl.multiple_of((run * TILES + i * (width // LANES) + k) * span, 8)
-                pad[pl.ds(at, 8), :] = rim[:, part]
+                pad[pl.ds(at + 8 - margin, margin), :] = rim[:, part]
                 pad[pl.ds(at + 8, ROWS), :] = sig[:, part]
         return 0
 
@@ -320,7 +346,7 @@
     for slot in range(60, CHUNKS):
         place(slot, blank, blank, jnp.zeros((STATE, LANES), F32))
 
-    pl.semaphore_wait(barrier, CHIPS - 1 + 1 + 3 + VARS - 1)
+    pl.semaphore_wait(barrier, CHIPS - 1 + 1 + VARS - 1)
     theirs_3 = pl.ds(theirs, HALF)
     swap_totals = to_shard(mate, totals.at[theirs_3], pair_totals, send_pt, recv_pt)
     swap_totals.start()
@@ -476,8 +502,6 @@
         return 0
 
     lax.fori_loop(0, TILES, prepare_patched, 0, unroll=2)
-    wait_for(landed, recv_in)
-
     def enter(k, _):
         end_a, total_a, _, _ = pair_of(k)
         before = landed[k]
@@ -487,11 +511,23 @@
         across[pl.ds(pl.multiple_of(k * STATE, 8), STATE), :] = jnp.where(leads, after, before)
         return 0
 
-    lax.fori_loop(0, HALF, enter, 0, unroll=4)
-    mine_2 = pl.ds(pl.multiple_of(mine * STATE, 8), HALF * STATE)
-    swap_start = to_shard(mate, across, start.at[mine_2], send_st, recv_st)
-    swap_start.start()
-    swap_start.wait()
+    swap_start = to_shard(
+        mate, across, start.at[pl.ds(pl.multiple_of(mine * STATE, 8), HALF * STATE)],
+        send_st, recv_st,
+    )
+
+    def enter_half():
+        wait_for(landed, recv_in)
+        lax.fori_loop(0, HALF, enter, 0, unroll=4)
+        swap_start.start()
+
+    @pl.when(core == 1)
+    def _():
+        enter_half()
+
+    @pl.when(core == 0)
+    def _():
+        swap_start.wait_recv()
 
     def final_group(group, _):
         at = group * (STATE * 8)
@@ -518,22 +554,19 @@
 
     for tile in range(CUT_TILES):
         cut[:, tile * LANES : (tile + 1) * LANES] = result(cut_slot(CORRUPT, tile))
-    before, after = lax.rem(v + VARS - 1, VARS), lax.rem(v + 1, VARS)
-    half = ROWS // 2
-    upper, lower = pl.ds(0, half), pl.ds(half, half)
-
-    def send_rows(k, i, slot, rows, src):
-        dst = whole.at[slot, rows]
-        return to_variant(k, src if src is not None else dst, dst, send_cut.at[i], recv_cut.at[i])
-
     directs = [
-        send_rows(k, i, v, rows, cut.at[rows])
-        for i, (k, rows) in enumerate(
-            ((1, upper), (VARS - 1, lower), (1, lower), (VARS - 1, upper))
-        )
+        to_variant(k, cut, whole.at[v], send_cut.at[k], recv_cut.at[k]) for k in (2, 1, VARS - 1)
     ]
     for direct in directs:
         direct.start()
+    @pl.when(core == 0)
+    def _():
+        enter_half()
+
+    @pl.when(core == 1)
+    def _():
+        swap_start.wait_recv()
+
     final_group(5, 0)
     squares[...] = jnp.zeros_like(squares)
     for tile in range(CUT_TILES):
@@ -541,22 +574,24 @@
         gap = gap - cut[:, tile * LANES : (tile + 1) * LANES].astype(F32)
         squares[tile : tile + 1, :] = jnp.sum(gap * gap, axis=0, keepdims=True)
 
-    plane_xc = 2 * lax.div(chip, 8) + core
-
     def along_z(k):
-        return 16 * lax.div(chip, 8) + 2 * lax.rem(line_z + k, 8) + core
-
-    def across_xc(k):
-        other = lax.rem(plane_xc + k, 8)
-        return 16 * lax.div(other, 2) + 2 * line_z + lax.rem(other, 2)
-
-    def share(peer_of, slot, src, dst, send_sem, recv_sem):
-        for k in range(1, 8):
+        return 16 * row_x + 2 * lax.rem(line_z + k, 8) + 1
+
+    def along_x(k):
+        return 16 * lax.rem(row_x + k, 4) + 2 * line_z + 1
+
+    def share(peer_of, count, slot, src, dst, send_sem, recv_sem):
+        for k in range(1, count):
             to_shard(peer_of(k), src, dst.at[slot], send_sem, recv_sem).start()
         dst[slot] = src[...]
 
-    seven = pl.ds(0, 7)
-    share(along_z, line_z, squares, squares_z, send_sz, recv_sz)
+    seven, three = pl.ds(0, 7), pl.ds(0, 3)
+    squares_over = to_shard(mate, squares, pair_squares, send_qq, recv_qq)
+
+    @pl.when(core == 0)
+    def _():
+        squares_over.start()
+
     whole[v] = cut[...]
 
     lax.fori_loop(0, 5, final_group, 0)
@@ -569,18 +604,15 @@
 
     save = pltpu.make_async_copy(patched, patched_out, load_sem.at[0])
     save.start()
-    relays = [
-        send_rows(1, 4, before, upper, None), send_rows(VARS - 1, 5, after, lower, None)
-    ]
-    for direct, relay in zip(directs, relays):
-        direct.wait_recv()
-        relay.start()
-    for direct in directs[2:]:
-        direct.wait_recv()
+
+    @pl.when(core == 1)
+    def _():
+        squares_over.wait_recv()
+        chip_squares[...] = squares[...] + pair_squares[...]
+        share(along_z, 8, line_z, chip_squares, squares_z, send_sz, recv_sz)
+
     for direct in directs:
-        direct.wait_send()
-    for relay in relays:
-        relay.wait()
+        direct.wait()
 
     for w in range(VARS):
         def peak_tile(i, _):
@@ -592,34 +624,57 @@
 
         lax.fori_loop(0, CUT_TILES, peak_tile, 0, unroll=2)
 
-    share(along_z, line_z, peaks, peaks_z, send_pz, recv_pz)
-    wait_for(squares_z.at[seven], recv_sz)
-    line_squares[...] = jnp.sum(squares_z[...], axis=0)
-    share(across_xc, plane_xc, line_squares, squares_x, send_sx, recv_sx)
-    wait_for(peaks_z.at[seven], recv_pz)
-    line_peaks[...] = jnp.max(peaks_z[...], axis=0)
-    share(across_xc, plane_xc, line_peaks, peaks_x, send_px, recv_px)
-    wait_for(squares_x.at[seven], recv_sx)
-    spreads[v] = jnp.sqrt(jnp.sum(squares_x[...], axis=0) / (SHARDS * ROWS) + TINY)
-    for k in range(1, VARS):
-        to_variant(k, spreads.at[v], spreads.at[v], send_sp.at[k], recv_sp.at[k]).start()
-    wait_for(peaks_x.at[seven], recv_px)
-    for k in range(1, VARS):
-        there = spreads.at[lax.rem(v + VARS - k, VARS)]
-        to_variant(k, there, there, send_sp.at[k], recv_sp.at[k]).wait()
-    peak = jnp.max(peaks_x[...], axis=0)
-    for w in range(VARS):
-        rows = slice(w * CUT_TILES, (w + 1) * CUT_TILES)
-        effect[rows, :] = peak[rows, :] / spreads[w, :CUT_TILES, :]
+    peaks_over = to_shard(mate, peaks, pair_peaks, send_pp, recv_pp)
+    answer_over = to_shard(mate, answer, answer, send_an, recv_an)
+
+    @pl.when(core == 0)
+    def _():
+        peaks_over.start()
+
+    @pl.when(core == 1)
+    def _():
+        wait_for(squares_z.at[seven], recv_sz)
+        line_squares[...] = jnp.sum(squares_z[...], axis=0)
+        share(along_x, 4, row_x, line_squares, squares_x, send_sx, recv_sx)
+        peaks_over.wait_recv()
+        chip_peaks[...] = jnp.maximum(peaks[...], pair_peaks[...])
+        share(along_z, 8, line_z, chip_peaks, peaks_z, send_pz, recv_pz)
+        wait_for(squares_x.at[three], recv_sx)
+        spreads[v] = jnp.sqrt(jnp.sum(squares_x[...], axis=0) / (SHARDS * ROWS) + TINY)
+        for k in range(1, VARS):
+            to_variant(k, spreads.at[v], spreads.at[v], send_sp.at[k], recv_sp.at[k]).start()
+        wait_for(peaks_z.at[seven], recv_pz)
+        line_peaks[...] = jnp.max(peaks_z[...], axis=0)
+        share(along_x, 4, row_x, line_peaks, peaks_x, send_px, recv_px)
+        wait_for(peaks_x.at[three], recv_px)
+        for k in range(1, VARS):
+            there = spreads.at[lax.rem(v + VARS - k, VARS)]
+            to_variant(k, there, there, send_sp.at[k], recv_sp.at[k]).wait()
+        peak = jnp.max(peaks_x[...], axis=0)
+        for w in range(VARS):
+            rows = slice(w * CUT_TILES, (w + 1) * CUT_TILES)
+            answer[rows, :] = peak[rows, :] / spreads[w, :CUT_TILES, :]
+        answer_over.start()
+        wait_for(squares_z.at[seven], send_sz)
+        wait_for(squares_x.at[three], send_sx)
+        wait_for(peaks_z.at[seven], send_pz)
+        wait_for(peaks_x.at[three], send_px)
+        answer_over.wait_send()
+
+    @pl.when(core == 0)
+    def _():
+        squares_over.wait_send()
+        peaks_over.wait_send()
+        answer_over.wait_recv()
+
+    effect[...] = answer[...]
     save.wait()
-    wait_for(squares_z.at[seven], send_sz)
-    wait_for(squares_x.at[seven], send_sx)
-    wait_for(peaks_z.at[seven], send_pz)
-    wait_for(peaks_x.at[seven], send_px)
     others = pl.ds(0, CHIPS - 1)
     wait_for(chip_totals.at[others], send_ct)
     wait_for(chip_ends.at[others], send_ce)
     wait_for(leaving.at[others], send_in)
+
+    swap_start.wait_send()
 
 
 SMEM = pl.BlockSpec(memory_space=pltpu.SMEM)
@@ -634,10 +689,13 @@
 ):
     rims = pl.pallas_call(
         halo_kernel,
-        out_shape=jax.ShapeDtypeStruct((2, 8, INNER), BF16),
+        out_shape=jax.ShapeDtypeStruct((8, INNER), BF16),
         in_specs=[HBM, HBM],
         out_specs=HBM,
-        scratch_shapes=[DMA((2,)), DMA((2,))],
+        scratch_shapes=[
+            pltpu.VMEM((2, 8, INNER), BF16), pltpu.VMEM((8, INNER), F32),
+            pltpu.VMEM((8, INNER), BF16), DMA((2,)), DMA, DMA,
+        ],
         compiler_params=pltpu.CompilerParams(
             collective_id=1, has_side_effects=True, vmem_limit_bytes=67_043_328
         ),
@@ -659,7 +717,7 @@
             pltpu.VMEM((ROWS, INNER), BF16),
             pltpu.VMEM((ROWS, INNER), BF16),
             pltpu.VMEM((ROWS, INNER), BF16),
-            pltpu.VMEM((2, 8, INNER), BF16),
+            pltpu.VMEM((8, INNER), BF16),
             pltpu.VMEM((TAPS, INNER), F32),
             pltpu.VMEM((1, INNER), F32),
             pltpu.VMEM((RANK + 2 * STATE, INNER), BF16),
@@ -698,18 +756,23 @@
             pltpu.VMEM((TILES, LANES), F32),
             pltpu.VMEM((8, STATE, LANES), F32),
             pltpu.VMEM((STATE, LANES), F32),
-            pltpu.VMEM((8, STATE, LANES), F32),
+            pltpu.VMEM((4, STATE, LANES), F32),
             pltpu.VMEM((VARS, STATE, LANES), F32),
             pltpu.VMEM((8, TILES, LANES), F32),
             pltpu.VMEM((TILES, LANES), F32),
-            pltpu.VMEM((8, TILES, LANES), F32),
+            pltpu.VMEM((4, TILES, LANES), F32),
+            pltpu.VMEM((STATE, LANES), F32),
+            pltpu.VMEM((STATE, LANES), F32),
+            pltpu.VMEM((TILES, LANES), F32),
+            pltpu.VMEM((TILES, LANES), F32),
+            pltpu.VMEM((TILES, LANES), F32),
             DMA((12,)),
         ]
         + [DMA] * 12
-        + [DMA((6,)), DMA((6,))]
+        + [DMA((VARS,)), DMA((VARS,))]
         + [DMA] * 4
         + [DMA((VARS,)), DMA((VARS,))]
-        + [DMA] * 4,
+        + [DMA] * 10,
         compiler_params=pltpu.CompilerParams(
             collective_id=0, has_side_effects=True, vmem_limit_bytes=67_043_328
         ),

time: 62.9 us -> 58.7 us (0.933)
  Pallas kernels: 61.5 us -> 57.3 us
    pallas_call x1, Pallas kernels: 10.4 us -> 5.24 us  [shards(): pl.pallas_call(halo_kernel, out_shape=jax.ShapeDtypeStruct((8, INNER), BF...]
    pallas_call x1, Pallas kernels: 49.3 us -> 50.3 us  [shards(): pl.pallas_call(kernel, out_shape=(jax.ShapeDtypeStruct((ROWS, INNER), BF1...]
where the time goes in v5:
time: 58.7 us; the launch traced here: 58.6 us
  Pallas kernels  57.3 us (98%)
  between operations  1.29 us (2%)
    pallas_call x1, Pallas kernels, shards(): pl.pallas_call(kernel, out_shape=(jax.ShapeDtypeStruct((ROWS, INNER), BF1...  50.3 us
    pallas_call x1, Pallas kernels, shards(): pl.pallas_call(halo_kernel, out_shape=jax.ShapeDtypeStruct((8, INNER), BF...  5.24 us
    pallas_call x1, Pallas kernels, shards(): pl.pallas_call(emit_kernel, out_shape=(jax.ShapeDtypeStruct((ROWS, INNER)...  1.71 us

profile of v5, /device:TPU:1, one launch (start us, length us, event | category | flops | bytes accessed | tf_op | source)
XLA Modules:
  0.0 58.6 jit_solution(9104438660839456827)
XLA Ops:
  1.3 5.2 %halo.1.rims_in = bf16[8,5120]{1,0:T(8,128)(2,1)} custom-call(bf16[32,10240]{1,0:T(8,128)(2,1)} %clean_in.1, bf16[32,10240]{1,0:T(8,128)(2,1)} %corrupt_in.1), custom_call_target="tpu_custom_call" | custom-call | tf_op jit(solution)/shard_map/halo/pallas_call | solution.py:690
  6.5 50.3 %mixer.1 = (bf16[32,5120]{1,0:T(8,128)(2,1)}, f32[40,128]{1,0:T(8,128)}) custom-call(s32[1,16]{1,0:T(1,128)} %pos.1, s32[1]{0:T(128)S(6)} %copy.13.mode, bf16[32,10240]{1,0:T(8,128)(2,1)} %clean_in.1, bf16[32,10240]{1,0:T(8,128)(2,1)} %corrupt_in.1, bf16[8,5120]{1,0:T(8,128)(2,1)} %halo.1.rims_in, f32[4,5120]{1,0:T(4,128)} %conv_w_in.1, f32[1,5120]{1,0:T(1,128)} %bitcast.7, ...), custom_call_target="tpu_custom_call" | custom-call | tf_op jit(solution)/shard_map/mixer/pallas_call | solution.py:706
  56.8 1.7 %emit.1 = (bf16[32,5120]{1,0:T(8,128)(2,1)}, f32[40,128]{1,0:T(8,128)}) custom-call(bf16[32,5120]{1,0:T(8,128)(2,1)} %get-tuple-element.6.patched_in, f32[40,128]{1,0:T(8,128)} %get-tuple-element.7.effect_in), custom_call_target="tpu_custom_call" | custom-call | tf_op jit(solution)/shard_map/emit/pallas_call | solution.py:784

commit v6 on v5

--- a/solution.py
+++ b/solution.py
@@ -105,18 +105,30 @@
     pltpu.make_async_copy(ref, ref, sem).wait()
 
 
-def halo_kernel(clean, corrupt, rims, ends, wide, packed, load_sem, send_sem, recv_sem):
+def front_kernel(
+    pos, mode, clean_in, corrupt_in, conv_w_in, conv_b_in, x_w_in, dt_w_in, dt_b_in, a_log_in,
+    acts, x_w, dt_w, dt_b, a_log,
+    rims, ends, wide, packed, clean, corrupt, conv_w, conv_b, pad, load_sem, send_sem, recv_sem,
+):
     me = lax.axis_index("seq")
     v = lax.axis_index("var")
     after = lax.min(me + 1, SHARDS - 1)
+    has_next, has_last = me < SHARDS - 1, me > 0
     barrier = pltpu.get_barrier_semaphore()
     loads = [
-        pltpu.make_async_copy(src.at[ROWS - 8 :, :INNER], ends.at[i], load_sem.at[i])
-        for i, src in enumerate((clean, corrupt))
+        pltpu.make_async_copy(src, dst, load_sem.at[i])
+        for i, (src, dst) in enumerate(
+            (
+                (clean_in.at[ROWS - 8 :, :INNER], ends.at[0]),
+                (corrupt_in.at[ROWS - 8 :, :INNER], ends.at[1]),
+                (clean_in.at[:, :INNER], clean), (corrupt_in.at[:, :INNER], corrupt),
+                (conv_w_in, conv_w), (conv_b_in, conv_b), (x_w_in, x_w), (dt_w_in, dt_w),
+                (dt_b_in, dt_b), (a_log_in, a_log),
+            )
+        )
     ]
     for load in loads:
         load.start()
-    has_next, has_last = me < SHARDS - 1, me > 0
 
     def signal(peer):
         pl.semaphore_signal(barrier, inc=1, device_id=(peer, v), device_id_type=MESH)
@@ -129,14 +141,16 @@
     def _():
         signal(me - 1)
 
-    for load in loads:
+    for load in loads[:2]:
         load.wait()
     margin = TAPS - 1
     wide[...] = jnp.zeros_like(wide)
     for i in range(2):
         wide[i * margin : (i + 1) * margin, :] = ends[i].astype(F32)[8 - margin :, :]
     packed[...] = wide[...].astype(BF16)
-
+    first = me * ROWS
+    take = hit_rows(pos, first, ROWS)[:, :1] & (mode[0] != 1)
+    take_rim = hit_rows(pos, first - margin, margin)[:, :1] & (mode[0] != 1)
     pl.semaphore_wait(barrier, lax.min(me, 1) + lax.min(SHARDS - 1 - me, 1))
     copy = pltpu.make_async_remote_copy(
         src_ref=packed, dst_ref=rims, send_sem=send_sem, recv_sem=recv_sem,
@@ -146,47 +160,88 @@
     @pl.when(has_next)
     def _():
         copy.start()
+
+    for load in loads[2:6]:
+        load.wait()
+    width = 512
+    span = 8 + ROWS
+    per = width // LANES
+
+    def columns(i):
+        return pl.ds(pl.multiple_of(i * width, width), width)
+
+    def fill(i, _):
+        sig_clean = clean[:, columns(i)].astype(F32)
+        sig_corrupt = corrupt[:, columns(i)].astype(F32)
+        pieces = (sig_clean, sig_corrupt, jnp.where(take, sig_clean, sig_corrupt))
+        for run, sig in enumerate(pieces):
+            for k in range(per):
+                at = pl.multiple_of((run * TILES + i * per + k) * span, 8)
+                pad[pl.ds(at, 8), :] = jnp.zeros((8, LANES), F32)
+                pad[pl.ds(at + 8, ROWS), :] = sig[:, k * LANES : (k + 1) * LANES]
+        return 0
+
+    def convolve(rows):
+        def body(tile, _):
+            cols = pl.ds(pl.multiple_of(tile * LANES, LANES), LANES)
+            bias = conv_b[:, cols]
+            for run in range(3):
+                at = (run * TILES + tile) * span + 8 - margin
+                total = bias + conv_w[0:1, cols] * pad[pl.ds(at, rows), :]
+                for k in range(1, TAPS):
+                    total = total + conv_w[k : k + 1, cols] * pad[pl.ds(at + k, rows), :]
+                acts[run * ROWS : run * ROWS + rows, cols] = silu(total).astype(BF16)
+            return 0
+
+        lax.fori_loop(0, TILES, body, 0, unroll=4)
+
+    def fill_rim(i, _):
+        rim = rims[:, columns(i)].astype(F32)
+        rim_clean, rim_corrupt = rim[:margin], rim[margin : 2 * margin]
+        pieces = (rim_clean, rim_corrupt, jnp.where(take_rim, rim_clean, rim_corrupt))
+        for run, part in enumerate(pieces):
+            for k in range(per):
+                at = (run * TILES + i * per + k) * span + 8 - margin
+                pad[pl.ds(at, margin), :] = part[:, k * LANES : (k + 1) * LANES]
+        return 0
+
+    lax.fori_loop(0, INNER // width, fill, 0)
+    convolve(ROWS)
+
+    @pl.when(has_last)
+    def _():
+        copy.wait_recv()
+        lax.fori_loop(0, INNER // width, fill_rim, 0)
+        convolve(8)
+
+    for load in loads[6:]:
+        load.wait()
+
+    @pl.when(has_next)
+    def _():
         copy.wait_send()
 
-    @pl.when(has_last)
-    def _():
-        copy.wait_recv()
-
-
-def emit_kernel(patched_in, effect_in, patched_out, effect_out, patched, effect, sems_in, sems_out):
-    cut = ROWS // 2
-    pieces = [
-        (patched_in.at[i * cut : (i + 1) * cut], patched.at[i * cut : (i + 1) * cut],
-         patched_out.at[i * cut : (i + 1) * cut])
-        for i in range(2)
+
+def emit_kernel(patched, effect, patched_out, effect_out, sems):
+    copies = [
+        pltpu.make_async_copy(patched, patched_out, sems.at[0]),
+        pltpu.make_async_copy(effect, effect_out, sems.at[1]),
     ]
-    pieces.append((effect_in, effect, effect_out))
-    arrivals = [
-        pltpu.make_async_copy(src, here, sems_in.at[i]) for i, (src, here, _) in enumerate(pieces)
-    ]
-    departures = [
-        pltpu.make_async_copy(here, dst, sems_out.at[i]) for i, (_, here, dst) in enumerate(pieces)
-    ]
-    for arrival in arrivals:
-        arrival.start()
-    for arrival, departure in zip(arrivals, departures):
-        arrival.wait()
-        departure.start()
-    for departure in departures:
-        departure.wait()
+    for copy in copies:
+        copy.start()
+    for copy in copies:
+        copy.wait()
 
 
 def kernel(
-    pos, mode, clean_in, corrupt_in, rims_in, conv_w_in, conv_b_in, x_w_in, dt_w_in, dt_b_in,
-    a_log_in, d_skip_in,
-    patched_out, effect,
-    patched, clean, corrupt, clean_gate, corrupt_gate, rims, conv_w, conv_b, x_w, dt_w, dt_b, a_log, d_skip,
-    pad, acts, low, maps, weights, base, gates, dts, us, bs, cs, rates, ends, totals,
-    pair_ends, pair_totals, chip_ends, chip_totals, got_ends, got_totals,
+    pos, mode, acts, x_w, dt_w, dt_b, a_log, clean_in, corrupt_in, d_skip_in,
+    patched, effect,
+    clean_gate, corrupt_gate, d_skip, low, maps, weights, base, gates, dts, us, bs, cs, rates, ends, totals,
+    pair_ends, pair_totals, chip_ends, got_ends,
     leaving, landed, across, start, ys,
     cut, squares, whole, peaks, squares_z, line_squares, squares_x, spreads,
     peaks_z, line_peaks, peaks_x, pair_squares, chip_squares, pair_peaks, chip_peaks, answer,
-    load_sem, send_pt, recv_pt, send_pe, recv_pe, send_ct, recv_ct, send_ce, recv_ce,
+    load_sem, send_pt, recv_pt, send_pe, recv_pe, send_ce, recv_ce,
     send_in, recv_in, send_st, recv_st,
     send_cut, recv_cut, send_sz, recv_sz, send_sx, recv_sx, send_sp, recv_sp,
     send_pz, recv_pz, send_px, recv_px, send_qq, recv_qq, send_pp, recv_pp, send_an, recv_an,
@@ -204,11 +259,8 @@
         pltpu.make_async_copy(src, dst, load_sem.at[i])
         for i, (src, dst) in enumerate(
             (
-                (clean_in.at[:, :INNER], clean), (corrupt_in.at[:, :INNER], corrupt),
-                (rims_in, rims), (conv_w_in, conv_w),
-                (conv_b_in, conv_b), (x_w_in, x_w), (dt_w_in, dt_w), (dt_b_in, dt_b),
-                (a_log_in, a_log), (d_skip_in, d_skip),
-                (clean_in.at[:, INNER:], clean_gate), (corrupt_in.at[:, INNER:], corrupt_gate),
+                (d_skip_in, d_skip), (clean_in.at[:, INNER:], clean_gate),
+                (corrupt_in.at[:, INNER:], corrupt_gate),
             )
         )
     ]
@@ -218,11 +270,10 @@
     def signal(peer, variant):
         pl.semaphore_signal(barrier, inc=1, device_id=(peer, variant), device_id_type=MESH)
 
-    def greet(k, _):
-        signal(2 * lax.rem(chip + k, CHIPS) + core, v)
-        return 0
-
-    lax.fori_loop(1, CHIPS, greet, 0)
+    row_x, line_z = lax.div(chip, 8), lax.rem(chip, 8)
+    peers = [8 * lax.rem(row_x + dx, 4) + lax.rem(line_z + dz, 8) for dx, dz in STEPS]
+    for peer in peers:
+        signal(2 * peer + core, v)
     signal(mate, v)
     for k in range(1, VARS):
         signal(me, lax.rem(v + k, VARS))
@@ -239,59 +290,8 @@
             device_id=(peer, v), device_id_type=MESH,
         )
 
-    first = me * ROWS
-    margin = TAPS - 1
-    inside = me > 0
-    hits = hit_rows(pos, first, ROWS)[:, :1]
-    take = hits & (mode[0] != 1)
-    take_gate = hits & (mode[0] != 0)
-    take_rim = hit_rows(pos, first - margin, margin)[:, :1] & (mode[0] != 1)
-
-    for load in loads[:5]:
-        load.wait()
-    width = 512
-
-    width = 512
-    span = 8 + ROWS
-
-    def fill(i, _):
-        cols = pl.ds(pl.multiple_of(i * width, width), width)
-        sig_clean = clean[:, cols].astype(F32)
-        sig_corrupt = corrupt[:, cols].astype(F32)
-        rim = jnp.where(inside, rims[:, cols].astype(F32), 0.0)
-        rim_clean, rim_corrupt = rim[:margin], rim[margin : 2 * margin]
-        pieces = (
-            (rim_clean, sig_clean),
-            (rim_corrupt, sig_corrupt),
-            (
-                jnp.where(take_rim, rim_clean, rim_corrupt),
-                jnp.where(take, sig_clean, sig_corrupt),
-            ),
-        )
-        for run, (rim, sig) in enumerate(pieces):
-            for k in range(width // LANES):
-                part = slice(k * LANES, (k + 1) * LANES)
-                at = pl.multiple_of((run * TILES + i * (width // LANES) + k) * span, 8)
-                pad[pl.ds(at + 8 - margin, margin), :] = rim[:, part]
-                pad[pl.ds(at + 8, ROWS), :] = sig[:, part]
-        return 0
-
-    lax.fori_loop(0, INNER // width, fill, 0)
-
-    def conv(tile, _):
-        cols = pl.ds(pl.multiple_of(tile * LANES, LANES), LANES)
-        bias = conv_b[:, cols]
-        for run in range(3):
-            at = (run * TILES + tile) * span + 8 - (TAPS - 1)
-            total = bias + conv_w[0:1, cols] * pad[pl.ds(at, ROWS), :]
-            for k in range(1, TAPS):
-                total = total + conv_w[k : k + 1, cols] * pad[pl.ds(at + k, ROWS), :]
-            acts[run * ROWS : (run + 1) * ROWS, cols] = silu(total).astype(BF16)
-        return 0
-
-    lax.fori_loop(0, TILES, conv, 0, unroll=4)
-
-    loads[5].wait()
+    take_gate = hit_rows(pos, me * ROWS, ROWS)[:, :1] & (mode[0] != 0)
+
     projected = lax.dot_general(
         acts[...], x_w[...], (((1,), (1,)), ((), ())), preferred_element_type=F32
     )
@@ -305,8 +305,6 @@
                 part[:, RANK + n : RANK + n + 1], (ROWS, LANES)
             )
 
-    for load in loads[6:9]:
-        load.wait()
 
     def rate_at(slot):
         return pl.ds(lax.div(slot, 8) * (STATE * 8) + lax.rem(slot, 8), STATE, stride=8)
@@ -346,11 +344,6 @@
     for slot in range(60, CHUNKS):
         place(slot, blank, blank, jnp.zeros((STATE, LANES), F32))
 
-    pl.semaphore_wait(barrier, CHIPS - 1 + 1 + VARS - 1)
-    theirs_3 = pl.ds(theirs, HALF)
-    swap_totals = to_shard(mate, totals.at[theirs_3], pair_totals, send_pt, recv_pt)
-    swap_totals.start()
-
     zero = jnp.zeros((8, LANES), F32)
 
     def rates_of(group):
@@ -384,23 +377,17 @@
         lax.fori_loop(0, GROUPS // 2, body, 0)
 
     local_pass(lax.div(theirs, 8))
+    pl.semaphore_wait(barrier, CHIPS - 1 + 1 + VARS - 1)
+    theirs_3 = pl.ds(theirs, HALF)
+    swap_totals = to_shard(mate, totals.at[theirs_3], pair_totals, send_pt, recv_pt)
+    swap_totals.start()
+
     theirs_2 = pl.ds(pl.multiple_of(theirs * STATE, 8), HALF * STATE)
     swap_ends = to_shard(mate, ends.at[theirs_2], pair_ends, send_pe, recv_pe)
     swap_ends.start()
+    local_pass(lax.div(mine, 8))
     swap_totals.wait()
 
-    def chip_total(k, _):
-        chip_totals[k] = totals[mine + k] + pair_totals[k]
-        return 0
-
-    lax.fori_loop(0, HALF, chip_total, 0, unroll=4)
-    row_x, line_z = lax.div(chip, 8), lax.rem(chip, 8)
-    peers = [8 * lax.rem(row_x + dx, 4) + lax.rem(line_z + dz, 8) for dx, dz in STEPS]
-    pltpu.make_async_copy(chip_totals.at[chip], got_totals.at[chip], recv_ct).start()
-    for peer in peers:
-        target = 2 * peer + core
-        to_shard(target, chip_totals.at[peer], got_totals.at[chip], send_ct, recv_ct).start()
-    local_pass(lax.div(mine, 8))
     leads = core == 0
 
     def my_summary(k):
@@ -420,7 +407,8 @@
 
     def chip_end(k, _):
         end_a, total_a, end_b, total_b = pair_of(k)
-        chip_ends[k] = jnp.exp2(rates[rate_at(mine + k), :] * total_b) * end_a + end_b
+        chip_ends[k, :STATE] = jnp.exp2(rates[rate_at(mine + k), :] * total_b) * end_a + end_b
+        chip_ends[k, STATE:] = total_a + total_b
         return 0
 
     lax.fori_loop(0, HALF, chip_end, 0, unroll=4)
@@ -446,12 +434,11 @@
 
     lax.fori_loop(0, GROUPS - 1, plain_readout, 0)
     local_readout(GROUPS - 1, mixed_reader(bs), mixed_reader(cs))
-    wait_for(got_totals, recv_ct)
     wait_for(got_ends, recv_ce)
 
     def chain(s, state):
         leaving[s] = state
-        return jnp.exp2(my_rate * got_totals[s]) * state + got_ends[s]
+        return jnp.exp2(my_rate * got_ends[s, STATE:]) * state + got_ends[s, :STATE]
 
     lax.fori_loop(0, CHIPS, chain, jnp.zeros((STATE, LANES), F32), unroll=4)
     pltpu.make_async_copy(leaving.at[chip], landed.at[chip], recv_in).start()
@@ -479,7 +466,7 @@
 
     lax.fori_loop(0, GROUPS - 1, plain_weights, 0)
     entry_weights(GROUPS - 1, mixed_reader(cs))
-    for load in loads[9:]:
+    for load in loads:
         load.wait()
 
     def prepare(slot, act, skip, gate):
@@ -602,8 +589,6 @@
 
     lax.fori_loop(0, TILES, patched_tile, 0, unroll=4)
 
-    save = pltpu.make_async_copy(patched, patched_out, load_sem.at[0])
-    save.start()
 
     @pl.when(core == 1)
     def _():
@@ -668,9 +653,7 @@
         answer_over.wait_recv()
 
     effect[...] = answer[...]
-    save.wait()
     others = pl.ds(0, CHIPS - 1)
-    wait_for(chip_totals.at[others], send_ct)
     wait_for(chip_ends.at[others], send_ce)
     wait_for(leaving.at[others], send_in)
 
@@ -687,46 +670,58 @@
     clean_proj, corrupt_proj, patch_pos, patch_mode, a_log, dt_bias,
     conv_weight, conv_bias, x_weight, dt_weight, d_skip,
 ):
-    rims = pl.pallas_call(
-        halo_kernel,
-        out_shape=jax.ShapeDtypeStruct((8, INNER), BF16),
-        in_specs=[HBM, HBM],
-        out_specs=HBM,
+    hold = functools.partial(pltpu.with_memory_space_constraint, memory_space=pltpu.HBM)
+    keep = functools.partial(pltpu.with_memory_space_constraint, memory_space=pltpu.VMEM)
+    front = pl.pallas_call(
+        front_kernel,
+        out_shape=(
+            pltpu.VMEM((3 * ROWS, INNER), BF16),
+            pltpu.VMEM((RANK + 2 * STATE, INNER), BF16),
+            pltpu.VMEM((RANK, INNER), BF16),
+            pltpu.VMEM((1, INNER), F32),
+            pltpu.VMEM((STATE, INNER), F32),
+        ),
+        in_specs=[SMEM, SMEM] + [HBM] * 8,
+        out_specs=(VMEM,) * 5,
         scratch_shapes=[
-            pltpu.VMEM((2, 8, INNER), BF16), pltpu.VMEM((8, INNER), F32),
-            pltpu.VMEM((8, INNER), BF16), DMA((2,)), DMA, DMA,
+            pltpu.VMEM((8, INNER), BF16),
+            pltpu.VMEM((2, 8, INNER), BF16),
+            pltpu.VMEM((8, INNER), F32),
+            pltpu.VMEM((8, INNER), BF16),
+            pltpu.VMEM((ROWS, INNER), BF16),
+            pltpu.VMEM((ROWS, INNER), BF16),
+            pltpu.VMEM((TAPS, INNER), F32),
+            pltpu.VMEM((1, INNER), F32),
+            pltpu.VMEM((3 * TILES * (8 + ROWS), LANES), F32),
+            DMA((10,)),
+            DMA,
+            DMA,
         ],
         compiler_params=pltpu.CompilerParams(
-            collective_id=1, has_side_effects=True, vmem_limit_bytes=67_043_328
+            collective_id=1, has_side_effects=True, vmem_limit_bytes=40_000_000
         ),
-        name="halo",
-    )(clean_proj, corrupt_proj)
+        name="front",
+    )(
+        hold(patch_pos), patch_mode,
+        *map(
+            hold,
+            (
+                clean_proj, corrupt_proj, conv_weight, conv_bias[None], x_weight.T, dt_weight,
+                dt_bias[None], a_log,
+            ),
+        ),
+    )
     row = (1, LANES)
     tile = (STATE, LANES)
     patched, effect = pl.pallas_call(
         kernel,
-        out_shape=(
-            jax.ShapeDtypeStruct((ROWS, INNER), BF16),
-            jax.ShapeDtypeStruct((TILES, LANES), F32),
-        ),
-        in_specs=[SMEM, SMEM] + [HBM] * 10,
-        out_specs=(HBM, VMEM),
+        out_shape=(pltpu.VMEM((ROWS, INNER), BF16), pltpu.VMEM((TILES, LANES), F32)),
+        in_specs=[SMEM, SMEM] + [VMEM] * 5 + [HBM] * 3,
+        out_specs=(VMEM, VMEM),
         scratch_shapes=[
             pltpu.VMEM((ROWS, INNER), BF16),
             pltpu.VMEM((ROWS, INNER), BF16),
-            pltpu.VMEM((ROWS, INNER), BF16),
-            pltpu.VMEM((ROWS, INNER), BF16),
-            pltpu.VMEM((ROWS, INNER), BF16),
-            pltpu.VMEM((8, INNER), BF16),
-            pltpu.VMEM((TAPS, INNER), F32),
             pltpu.VMEM((1, INNER), F32),
-            pltpu.VMEM((RANK + 2 * STATE, INNER), BF16),
-            pltpu.VMEM((RANK, INNER), BF16),
-            pltpu.VMEM((1, INNER), F32),
-            pltpu.VMEM((STATE, INNER), F32),
-            pltpu.VMEM((1, INNER), F32),
-            pltpu.VMEM((3 * TILES * (8 + ROWS), LANES), F32),
-            pltpu.VMEM((3 * ROWS, INNER), BF16),
             pltpu.VMEM((3 * ROWS, RANK), BF16),
             pltpu.VMEM((3 * ROWS, STATE), F32),
             pltpu.VMEM((GROUPS * ROWS * STATE * 8, LANES), F32),
@@ -741,10 +736,8 @@
             pltpu.VMEM((CHUNKS, *row), F32),
             pltpu.VMEM((HALF * STATE, LANES), F32),
             pltpu.VMEM((HALF, *row), F32),
-            pltpu.VMEM((HALF, *tile), F32),
-            pltpu.VMEM((HALF, *row), F32),
-            pltpu.VMEM((CHIPS, *tile), F32),
-            pltpu.VMEM((CHIPS, *row), F32),
+            pltpu.VMEM((HALF, STATE + 1, LANES), F32),
+            pltpu.VMEM((CHIPS, STATE + 1, LANES), F32),
             pltpu.VMEM((CHIPS, *tile), F32),
             pltpu.VMEM((HALF, *tile), F32),
             pltpu.VMEM((HALF * STATE, LANES), F32),
@@ -766,20 +759,20 @@
             pltpu.VMEM((TILES, LANES), F32),
             pltpu.VMEM((TILES, LANES), F32),
             pltpu.VMEM((TILES, LANES), F32),
-            DMA((12,)),
+            DMA((3,)),
         ]
-        + [DMA] * 12
+        + [DMA] * 10
         + [DMA((VARS,)), DMA((VARS,))]
         + [DMA] * 4
         + [DMA((VARS,)), DMA((VARS,))]
         + [DMA] * 10,
         compiler_params=pltpu.CompilerParams(
-            collective_id=0, has_side_effects=True, vmem_limit_bytes=67_043_328
+            collective_id=0, has_side_effects=True, vmem_limit_bytes=54_000_000
         ),
         name="mixer",
     )(
-        patch_pos, patch_mode, clean_proj, corrupt_proj, rims, conv_weight, conv_bias[None],
-        x_weight.T, dt_weight, dt_bias[None], a_log, d_skip[None],
+        hold(patch_pos), patch_mode, *map(keep, front),
+        *map(hold, (clean_proj, corrupt_proj, d_skip[None])),
     )
     patched, effect = pl.pallas_call(
         emit_kernel,
@@ -787,14 +780,14 @@
             jax.ShapeDtypeStruct((ROWS, INNER), BF16),
             jax.ShapeDtypeStruct((TILES, LANES), F32),
         ),
-        in_specs=[HBM, HBM],
+        in_specs=[VMEM, VMEM],
         out_specs=(HBM, HBM),
-        scratch_shapes=[
-            pltpu.VMEM((ROWS, INNER), BF16), pltpu.VMEM((TILES, LANES), F32), DMA((3,)), DMA((3,)),
-        ],
-        compiler_params=pltpu.CompilerParams(vmem_limit_bytes=67_043_328),
+        scratch_shapes=[DMA((2,))],
+        compiler_params=pltpu.CompilerParams(vmem_limit_bytes=16_000_000),
         name="emit",
-    )(patched, effect)
+    )(
+        keep(patched), keep(effect),
+    )
     return (patched[None], effect.reshape(1, INNER))
 
 

time: 58.7 us -> 57.4 us (0.978)
  Pallas kernels: 57.3 us -> 56 us
    pallas_call x1, Pallas kernels: 1.71 us -> 0.75 us  [shards(): pl.pallas_call(emit_kernel, out_shape=(jax.ShapeDtypeStruct((ROWS, INNER)...]
where the time goes in v6:
time: 57.4 us; the launch traced here: 57.3 us
  Pallas kernels  56 us (98%)
  between operations  1.29 us (2%)
    pallas_call x1, Pallas kernels, shards(): pl.pallas_call(kernel, out_shape=(pltpu.VMEM((ROWS, INNER), BF16), pltpu....  48.8 us
    pallas_call x1, Pallas kernels, shards(): pl.pallas_call(front_kernel, out_shape=(pltpu.VMEM((3 * ROWS, INNER), BF1...  6.4 us

profile of v6, /device:TPU:1, one launch (start us, length us, event | category | flops | bytes accessed | tf_op | source)
XLA Modules:
  0.0 57.3 jit_solution(7407702703551253500)
XLA Ops:
  1.3 6.4 %front.1 = (bf16[96,5120]{1,0:T(8,128)(2,1)S(1)}, bf16[192,5120]{1,0:T(8,128)(2,1)S(1)}, bf16[160,5120]{1,0:T(8,128)(2,1)S(1)}, f32[1,5120]{1,0:T(1,128)S(1)}, f32[16,5120]{1,0:T(8,128)S(1)}) custom-call(s32[1,16]{1,0:T(1,128)} %pos.3, s32[1]{0:T(128)S(6)} %copy.13.mode, bf16[32,10240]{1,0:T(8,128)(2,1)} %clean_in.3, bf16[32,10240]{1,0:T(8,128)(2,1)} %corrupt_in.3, ...), custom_call_target="tpu_custom_call" | custom-call | tf_op jit(solution)/shard_map/front/pallas_call | solution.py:675
  7.7 48.8 %mixer.1 = (bf16[32,5120]{1,0:T(8,128)(2,1)S(1)}, f32[40,128]{1,0:T(8,128)S(1)}) custom-call(s32[1,16]{1,0:T(1,128)} %pos.3, s32[1]{0:T(128)S(6)} %copy.13.mode, bf16[96,5120]{1,0:T(8,128)(2,1)S(1)} %get-tuple-element.11.acts, bf16[192,5120]{1,0:T(8,128)(2,1)S(1)} %get-tuple-element.12.x_w, bf16[160,5120]{1,0:T(8,128)(2,1)S(1)} %get-tuple-element.13.dt_w, ...), custom_call_target="tpu_custom_call" | custom-call | tf_op jit(solution)/shard_map/mixer/pallas_call | solution.py:716
  56.5 0.7 %emit.1 = (bf16[32,5120]{1,0:T(8,128)(2,1)}, f32[40,128]{1,0:T(8,128)}) custom-call(bf16[32,5120]{1,0:T(8,128)(2,1)S(1)} %get-tuple-element.16.patched, f32[40,128]{1,0:T(8,128)S(1)} %get-tuple-element.17.effect), custom_call_target="tpu_custom_call" | custom-call | tf_op jit(solution)/shard_map/emit/pallas_call | solution.py:777

commit v7 on v6

--- a/solution.py
+++ b/solution.py
@@ -20,6 +20,7 @@
 TILES = INNER // LANES
 CUT_TILES = SPAN // LANES
 GROUPS = CHUNKS // 8
+BUSY = 28
 HALF = CHUNKS // 2
 CHIPS = SHARDS // 2
 PITCH = 72
@@ -41,6 +42,10 @@
     if tile < 8:
         return TILES + 8 * run + tile
     return 56 + 2 * run + (tile - 8)
+
+
+def rate_at(slot):
+    return pl.ds(lax.div(slot, 8) * (STATE * 8) + lax.rem(slot, 8), STATE, stride=8)
 
 
 def hit_rows(pos_ref, first, count):
@@ -107,8 +112,8 @@
 
 def front_kernel(
     pos, mode, clean_in, corrupt_in, conv_w_in, conv_b_in, x_w_in, dt_w_in, dt_b_in, a_log_in,
-    acts, x_w, dt_w, dt_b, a_log,
-    rims, ends, wide, packed, clean, corrupt, conv_w, conv_b, pad, load_sem, send_sem, recv_sem,
+    acts, x_w, dt_w, dt_b, rates,
+    rims, a_log, ends, wide, packed, clean, corrupt, conv_w, conv_b, pad, load_sem, send_sem, recv_sem,
 ):
     me = lax.axis_index("seq")
     v = lax.axis_index("var")
@@ -207,15 +212,29 @@
 
     lax.fori_loop(0, INNER // width, fill, 0)
     convolve(ROWS)
+    for load in loads[6:]:
+        load.wait()
+
+    def rate_of(slot, cols):
+        rates[rate_at(slot), :] = jnp.exp(a_log[:, cols]) * (-LOG2E)
+
+    def patched_rate(tile, _):
+        rate_of(tile, pl.ds(pl.multiple_of(tile * LANES, LANES), LANES))
+        return 0
+
+    lax.fori_loop(0, TILES, patched_rate, 0, unroll=4)
+    for tile in range(CUT_TILES):
+        for run in (CLEAN, CORRUPT):
+            cols = pl.ds(pl.multiple_of(v * SPAN + tile * LANES, LANES), LANES)
+            rate_of(cut_slot(run, tile), cols)
+    for slot in range(60, CHUNKS):
+        rates[rate_at(slot), :] = jnp.zeros((STATE, LANES), F32)
 
     @pl.when(has_last)
     def _():
         copy.wait_recv()
         lax.fori_loop(0, INNER // width, fill_rim, 0)
         convolve(8)
-
-    for load in loads[6:]:
-        load.wait()
 
     @pl.when(has_next)
     def _():
@@ -234,13 +253,13 @@
 
 
 def kernel(
-    pos, mode, acts, x_w, dt_w, dt_b, a_log, clean_in, corrupt_in, d_skip_in,
+    pos, mode, acts, x_w, dt_w, dt_b, rates, clean_in, corrupt_in, d_skip_in,
     patched, effect,
-    clean_gate, corrupt_gate, d_skip, low, maps, weights, base, gates, dts, us, bs, cs, rates, ends, totals,
+    clean_gate, corrupt_gate, d_skip, low, maps, weights, base, gates, dts, us, bs, cs, ends, totals,
     pair_ends, pair_totals, chip_ends, got_ends,
     leaving, landed, across, start, ys,
     cut, squares, whole, peaks, squares_z, line_squares, squares_x, spreads,
-    peaks_z, line_peaks, peaks_x, pair_squares, chip_squares, pair_peaks, chip_peaks, answer,
+    peaks_z, line_peaks, peaks_x, pair_squares, chip_squares, pair_peaks, chip_peaks, sent_peaks, answer,
     load_sem, send_pt, recv_pt, send_pe, recv_pe, send_ce, recv_ce,
     send_in, recv_in, send_st, recv_st,
     send_cut, recv_cut, send_sz, recv_sz, send_sx, recv_sx, send_sp, recv_sp,
@@ -306,26 +325,21 @@
             )
 
 
-    def rate_at(slot):
-        return pl.ds(lax.div(slot, 8) * (STATE * 8) + lax.rem(slot, 8), STATE, stride=8)
-
-    def place(slot, steps, act, log_rate):
+    def place(slot, steps, act):
         dts[pl.ds(slot, ROWS, stride=PITCH), :] = steps
         us[pl.ds(slot, ROWS, stride=PITCH), :] = steps * act
         totals[slot] = jnp.sum(steps, axis=0, keepdims=True)
-        rates[rate_at(slot), :] = jnp.exp(log_rate) * (-LOG2E)
-
-    wide = 1280
+
+    wide = 2560
 
     def patched_steps(i, _):
         cols = pl.ds(pl.multiple_of(i * wide, wide), wide)
         raw = jnp.dot(low[2 * ROWS :, :], dt_w[:, cols], preferred_element_type=F32)
         steps = softplus(raw + dt_b[:, cols])
         act = acts[2 * ROWS :, cols].astype(F32)
-        logs = a_log[:, cols]
         for k in range(wide // LANES):
             part = slice(k * LANES, (k + 1) * LANES)
-            place(i * (wide // LANES) + k, steps[:, part], act[:, part], logs[:, part])
+            place(i * (wide // LANES) + k, steps[:, part], act[:, part])
         return 0
 
     lax.fori_loop(0, INNER // wide, patched_steps, 0)
@@ -334,15 +348,14 @@
     raw = jnp.dot(low[: 2 * ROWS, :], dt_w[:, cols], preferred_element_type=F32)
     steps = softplus(raw + dt_b[:, cols])
     act = acts[: 2 * ROWS, cols].astype(F32)
-    logs = a_log[:, cols]
     for run in (CLEAN, CORRUPT):
         rows = slice(run * ROWS, (run + 1) * ROWS)
         for tile in range(CUT_TILES):
             part = slice(tile * LANES, (tile + 1) * LANES)
-            place(cut_slot(run, tile), steps[rows, part], act[rows, part], logs[:, part])
+            place(cut_slot(run, tile), steps[rows, part], act[rows, part])
     blank = jnp.zeros((ROWS, LANES), F32)
     for slot in range(60, CHUNKS):
-        place(slot, blank, blank, jnp.zeros((STATE, LANES), F32))
+        place(slot, blank, blank)
 
     zero = jnp.zeros((8, LANES), F32)
 
@@ -412,11 +425,19 @@
         return 0
 
     lax.fori_loop(0, HALF, chip_end, 0, unroll=4)
-    pltpu.make_async_copy(chip_ends.at[chip], got_ends.at[chip], recv_ce).start()
+    owns = (core == 0) | (chip < BUSY)
+    others = pl.ds(0, CHIPS - 1)
+
+    @pl.when(owns)
+    def _():
+        pltpu.make_async_copy(chip_ends.at[chip], got_ends.at[chip], recv_ce).start()
 
     for peer in peers:
-        target = 2 * peer + core
-        to_shard(target, chip_ends.at[peer], got_ends.at[chip], send_ce, recv_ce).start()
+        @pl.when((core == 0) | (peer < BUSY))
+        def _():
+            target = 2 * peer + core
+            to_shard(target, chip_ends.at[peer], got_ends.at[chip], send_ce, recv_ce).start()
+
     my_rate = rates[rate_at(mine + chip), :]
     for run in range(3):
         for n in range(STATE):
@@ -434,17 +455,18 @@
 
     lax.fori_loop(0, GROUPS - 1, plain_readout, 0)
     local_readout(GROUPS - 1, mixed_reader(bs), mixed_reader(cs))
-    wait_for(got_ends, recv_ce)
-
     def chain(s, state):
         leaving[s] = state
         return jnp.exp2(my_rate * got_ends[s, STATE:]) * state + got_ends[s, :STATE]
 
-    lax.fori_loop(0, CHIPS, chain, jnp.zeros((STATE, LANES), F32), unroll=4)
-    pltpu.make_async_copy(leaving.at[chip], landed.at[chip], recv_in).start()
-
-    for peer in peers:
-        to_shard(2 * peer + core, leaving.at[peer], landed.at[chip], send_in, recv_in).start()
+    @pl.when(owns)
+    def _():
+        wait_for(got_ends, recv_ce)
+        lax.fori_loop(0, CHIPS, chain, jnp.zeros((STATE, LANES), F32), unroll=4)
+        pltpu.make_async_copy(leaving.at[chip], landed.at[chip], recv_in).start()
+        for peer in peers:
+            to_shard(2 * peer + core, leaving.at[peer], landed.at[chip], send_in, recv_in).start()
+
     def entry_weights(group, read):
         rate = rates_of(group)
 
@@ -503,14 +525,14 @@
         send_st, recv_st,
     )
 
-    def enter_half():
-        wait_for(landed, recv_in)
+    def enter_half(sources):
+        wait_for(landed.at[pl.ds(0, sources)], recv_in)
         lax.fori_loop(0, HALF, enter, 0, unroll=4)
         swap_start.start()
 
     @pl.when(core == 1)
     def _():
-        enter_half()
+        enter_half(BUSY)
 
     @pl.when(core == 0)
     def _():
@@ -548,7 +570,7 @@
         direct.start()
     @pl.when(core == 0)
     def _():
-        enter_half()
+        enter_half(CHIPS)
 
     @pl.when(core == 1)
     def _():
@@ -609,7 +631,8 @@
 
         lax.fori_loop(0, CUT_TILES, peak_tile, 0, unroll=2)
 
-    peaks_over = to_shard(mate, peaks, pair_peaks, send_pp, recv_pp)
+    sent_peaks[...] = peaks[...].astype(BF16)
+    peaks_over = to_shard(mate, sent_peaks, pair_peaks, send_pp, recv_pp)
     answer_over = to_shard(mate, answer, answer, send_an, recv_an)
 
     @pl.when(core == 0)
@@ -622,20 +645,21 @@
         line_squares[...] = jnp.sum(squares_z[...], axis=0)
         share(along_x, 4, row_x, line_squares, squares_x, send_sx, recv_sx)
         peaks_over.wait_recv()
-        chip_peaks[...] = jnp.maximum(peaks[...], pair_peaks[...])
+        both = jnp.maximum(sent_peaks[...].astype(F32), pair_peaks[...].astype(F32))
+        chip_peaks[...] = both.astype(BF16)
         share(along_z, 8, line_z, chip_peaks, peaks_z, send_pz, recv_pz)
         wait_for(squares_x.at[three], recv_sx)
         spreads[v] = jnp.sqrt(jnp.sum(squares_x[...], axis=0) / (SHARDS * ROWS) + TINY)
         for k in range(1, VARS):
             to_variant(k, spreads.at[v], spreads.at[v], send_sp.at[k], recv_sp.at[k]).start()
         wait_for(peaks_z.at[seven], recv_pz)
-        line_peaks[...] = jnp.max(peaks_z[...], axis=0)
+        line_peaks[...] = jnp.max(peaks_z[...].astype(F32), axis=0).astype(BF16)
         share(along_x, 4, row_x, line_peaks, peaks_x, send_px, recv_px)
         wait_for(peaks_x.at[three], recv_px)
         for k in range(1, VARS):
             there = spreads.at[lax.rem(v + VARS - k, VARS)]
             to_variant(k, there, there, send_sp.at[k], recv_sp.at[k]).wait()
-        peak = jnp.max(peaks_x[...], axis=0)
+        peak = jnp.max(peaks_x[...].astype(F32), axis=0)
         for w in range(VARS):
             rows = slice(w * CUT_TILES, (w + 1) * CUT_TILES)
             answer[rows, :] = peak[rows, :] / spreads[w, :CUT_TILES, :]
@@ -653,9 +677,21 @@
         answer_over.wait_recv()
 
     effect[...] = answer[...]
-    others = pl.ds(0, CHIPS - 1)
-    wait_for(chip_ends.at[others], send_ce)
-    wait_for(leaving.at[others], send_in)
+    @pl.when(core == 0)
+    def _():
+        wait_for(chip_ends.at[others], send_ce)
+
+    @pl.when((core == 1) & (chip < BUSY))
+    def _():
+        wait_for(chip_ends.at[pl.ds(0, BUSY - 1)], send_ce)
+
+    @pl.when((core == 1) & (chip >= BUSY))
+    def _():
+        wait_for(chip_ends.at[pl.ds(0, BUSY)], send_ce)
+
+    @pl.when(owns)
+    def _():
+        wait_for(leaving.at[others], send_in)
 
     swap_start.wait_send()
 
@@ -679,12 +715,13 @@
             pltpu.VMEM((RANK + 2 * STATE, INNER), BF16),
             pltpu.VMEM((RANK, INNER), BF16),
             pltpu.VMEM((1, INNER), F32),
-            pltpu.VMEM((STATE, INNER), F32),
+            pltpu.VMEM((CHUNKS * STATE, LANES), F32),
         ),
         in_specs=[SMEM, SMEM] + [HBM] * 8,
         out_specs=(VMEM,) * 5,
         scratch_shapes=[
             pltpu.VMEM((8, INNER), BF16),
+            pltpu.VMEM((STATE, INNER), F32),
             pltpu.VMEM((2, 8, INNER), BF16),
             pltpu.VMEM((8, INNER), F32),
             pltpu.VMEM((8, INNER), BF16),
@@ -732,7 +769,6 @@
             pltpu.VMEM((3 * ROWS * SPLAT + 8, LANES), F32),
             pltpu.VMEM((3 * ROWS * SPLAT + 8, LANES), F32),
             pltpu.VMEM((CHUNKS * STATE, LANES), F32),
-            pltpu.VMEM((CHUNKS * STATE, LANES), F32),
             pltpu.VMEM((CHUNKS, *row), F32),
             pltpu.VMEM((HALF * STATE, LANES), F32),
             pltpu.VMEM((HALF, *row), F32),
@@ -751,13 +787,14 @@
             pltpu.VMEM((STATE, LANES), F32),
             pltpu.VMEM((4, STATE, LANES), F32),
             pltpu.VMEM((VARS, STATE, LANES), F32),
-            pltpu.VMEM((8, TILES, LANES), F32),
-            pltpu.VMEM((TILES, LANES), F32),
-            pltpu.VMEM((4, TILES, LANES), F32),
+            pltpu.VMEM((8, TILES, LANES), BF16),
+            pltpu.VMEM((TILES, LANES), BF16),
+            pltpu.VMEM((4, TILES, LANES), BF16),
             pltpu.VMEM((STATE, LANES), F32),
             pltpu.VMEM((STATE, LANES), F32),
-            pltpu.VMEM((TILES, LANES), F32),
-            pltpu.VMEM((TILES, LANES), F32),
+            pltpu.VMEM((TILES, LANES), BF16),
+            pltpu.VMEM((TILES, LANES), BF16),
+            pltpu.VMEM((TILES, LANES), BF16),
             pltpu.VMEM((TILES, LANES), F32),
             DMA((3,)),
         ]

time: 57.4 us -> 56.5 us (0.984)
  Pallas kernels: 56 us -> 55.1 us
    pallas_call x1, Pallas kernels: 48.8 us -> 48 us  [shards(): pl.pallas_call(kernel, out_shape=(pltpu.VMEM((ROWS, INNER), BF16), pltpu....]
where the time goes in v7:
time: 56.5 us; the launch traced here: 56.4 us
  Pallas kernels  55.1 us (98%)
  between operations  1.29 us (2%)
    pallas_call x1, Pallas kernels, shards(): pl.pallas_call(kernel, out_shape=(pltpu.VMEM((ROWS, INNER), BF16), pltpu....  48 us
    pallas_call x1, Pallas kernels, shards(): pl.pallas_call(front_kernel, out_shape=(pltpu.VMEM((3 * ROWS, INNER), BF1...  6.4 us

profile of v7, /device:TPU:1, one launch (start us, length us, event | category | flops | bytes accessed | tf_op | source)
XLA Modules:
  0.0 56.4 jit_solution(15397449548979927932)
XLA Ops:
  1.3 6.4 %front.1 = (bf16[96,5120]{1,0:T(8,128)(2,1)S(1)}, bf16[192,5120]{1,0:T(8,128)(2,1)S(1)}, bf16[160,5120]{1,0:T(8,128)(2,1)S(1)}, f32[1,5120]{1,0:T(1,128)S(1)}, f32[1024,128]{1,0:T(8,128)S(1)}) custom-call(s32[1,16]{1,0:T(1,128)} %pos.3, s32[1]{0:T(128)S(6)} %copy.13.mode, bf16[32,10240]{1,0:T(8,128)(2,1)} %clean_in.3, bf16[32,10240]{1,0:T(8,128)(2,1)} %corrupt_in.3, ...), custom_call_target="tpu_custom_call" | custom-call | tf_op jit(solution)/shard_map/front/pallas_call | solution.py:711
  7.7 48.0 %mixer.1 = (bf16[32,5120]{1,0:T(8,128)(2,1)S(1)}, f32[40,128]{1,0:T(8,128)S(1)}) custom-call(s32[1,16]{1,0:T(1,128)} %pos.3, s32[1]{0:T(128)S(6)} %copy.13.mode, bf16[96,5120]{1,0:T(8,128)(2,1)S(1)} %get-tuple-element.11.acts, bf16[192,5120]{1,0:T(8,128)(2,1)S(1)} %get-tuple-element.12.x_w, bf16[160,5120]{1,0:T(8,128)(2,1)S(1)} %get-tuple-element.13.dt_w, ...), custom_call_target="tpu_custom_call" | custom-call | tf_op jit(solution)/shard_map/mixer/pallas_call | solution.py:753
  55.7 0.7 %emit.1 = (bf16[32,5120]{1,0:T(8,128)(2,1)}, f32[40,128]{1,0:T(8,128)}) custom-call(bf16[32,5120]{1,0:T(8,128)(2,1)S(1)} %get-tuple-element.16.patched, f32[40,128]{1,0:T(8,128)S(1)} %get-tuple-element.17.effect), custom_call_target="tpu_custom_call" | custom-call | tf_op jit(solution)/shard_map/emit/pallas_call | solution.py:814

commit v8 on v7

--- a/solution.py
+++ b/solution.py
@@ -198,7 +198,7 @@
                 acts[run * ROWS : run * ROWS + rows, cols] = silu(total).astype(BF16)
             return 0
 
-        lax.fori_loop(0, TILES, body, 0, unroll=4)
+        lax.fori_loop(0, TILES, body, 0, unroll=4 if rows == ROWS else 10)
 
     def fill_rim(i, _):
         rim = rims[:, columns(i)].astype(F32)
@@ -233,7 +233,7 @@
     @pl.when(has_last)
     def _():
         copy.wait_recv()
-        lax.fori_loop(0, INNER // width, fill_rim, 0)
+        lax.fori_loop(0, INNER // width, fill_rim, 0, unroll=5)
         convolve(8)
 
     @pl.when(has_next)
@@ -330,7 +330,7 @@
         us[pl.ds(slot, ROWS, stride=PITCH), :] = steps * act
         totals[slot] = jnp.sum(steps, axis=0, keepdims=True)
 
-    wide = 2560
+    wide = 5120
 
     def patched_steps(i, _):
         cols = pl.ds(pl.multiple_of(i * wide, wide), wide)
@@ -424,7 +424,7 @@
         chip_ends[k, STATE:] = total_a + total_b
         return 0
 
-    lax.fori_loop(0, HALF, chip_end, 0, unroll=4)
+    lax.fori_loop(0, HALF, chip_end, 0, unroll=8)
     owns = (core == 0) | (chip < BUSY)
     others = pl.ds(0, CHIPS - 1)
 
@@ -527,7 +527,7 @@
 
     def enter_half(sources):
         wait_for(landed.at[pl.ds(0, sources)], recv_in)
-        lax.fori_loop(0, HALF, enter, 0, unroll=4)
+        lax.fori_loop(0, HALF, enter, 0, unroll=8)
         swap_start.start()
 
     @pl.when(core == 1)

time: 56.5 us -> 56.3 us (level)
  no operation moved by 1% of the time
where the time goes in v8:
time: 56.3 us; the launch traced here: 56.2 us
  Pallas kernels  54.9 us (98%)
  between operations  1.29 us (2%)
    pallas_call x1, Pallas kernels, shards(): pl.pallas_call(kernel, out_shape=(pltpu.VMEM((ROWS, INNER), BF16), pltpu....  47.9 us
    pallas_call x1, Pallas kernels, shards(): pl.pallas_call(front_kernel, out_shape=(pltpu.VMEM((3 * ROWS, INNER), BF1...  6.26 us

profile of v8, /device:TPU:1, one launch (start us, length us, event | category | flops | bytes accessed | tf_op | source)
XLA Modules:
  0.0 56.2 jit_solution(6711102103519606199)
XLA Ops:
  1.3 6.3 %front.1 = (bf16[96,5120]{1,0:T(8,128)(2,1)S(1)}, bf16[192,5120]{1,0:T(8,128)(2,1)S(1)}, bf16[160,5120]{1,0:T(8,128)(2,1)S(1)}, f32[1,5120]{1,0:T(1,128)S(1)}, f32[1024,128]{1,0:T(8,128)S(1)}) custom-call(s32[1,16]{1,0:T(1,128)} %pos.3, s32[1]{0:T(128)S(6)} %copy.13.mode, bf16[32,10240]{1,0:T(8,128)(2,1)} %clean_in.3, bf16[32,10240]{1,0:T(8,128)(2,1)} %corrupt_in.3, ...), custom_call_target="tpu_custom_call" | custom-call | tf_op jit(solution)/shard_map/front/pallas_call | solution.py:711
  7.5 47.9 %mixer.1 = (bf16[32,5120]{1,0:T(8,128)(2,1)S(1)}, f32[40,128]{1,0:T(8,128)S(1)}) custom-call(s32[1,16]{1,0:T(1,128)} %pos.3, s32[1]{0:T(128)S(6)} %copy.13.mode, bf16[96,5120]{1,0:T(8,128)(2,1)S(1)} %get-tuple-element.11.acts, bf16[192,5120]{1,0:T(8,128)(2,1)S(1)} %get-tuple-element.12.x_w, bf16[160,5120]{1,0:T(8,128)(2,1)S(1)} %get-tuple-element.13.dt_w, ...), custom_call_target="tpu_custom_call" | custom-call | tf_op jit(solution)/shard_map/mixer/pallas_call | solution.py:753
  55.4 0.7 %emit.1 = (bf16[32,5120]{1,0:T(8,128)(2,1)}, f32[40,128]{1,0:T(8,128)}) custom-call(bf16[32,5120]{1,0:T(8,128)(2,1)S(1)} %get-tuple-element.16.patched, f32[40,128]{1,0:T(8,128)S(1)} %get-tuple-element.17.effect), custom_call_target="tpu_custom_call" | custom-call | tf_op jit(solution)/shard_map/emit/pallas_call | solution.py:814

commit v9 on v8

--- a/solution.py
+++ b/solution.py
@@ -590,7 +590,7 @@
         return 16 * lax.rem(row_x + k, 4) + 2 * line_z + 1
 
     def share(peer_of, count, slot, src, dst, send_sem, recv_sem):
-        for k in range(1, count):
+        for k in sorted(range(1, count), key=lambda k: -min(k, count - k)):
             to_shard(peer_of(k), src, dst.at[slot], send_sem, recv_sem).start()
         dst[slot] = src[...]
 

time: 56.3 us -> 55.7 us (0.989)
  Pallas kernels: 54.9 us -> 54.3 us
    pallas_call x1, Pallas kernels: 47.9 us -> 47.2 us  [shards(): pl.pallas_call(kernel, out_shape=(pltpu.VMEM((ROWS, INNER), BF16), pltpu....]
where the time goes in v9:
time: 55.7 us; the launch traced here: 55.5 us
  Pallas kernels  54.3 us (97%)
  between operations  1.29 us (2%)
    pallas_call x1, Pallas kernels, shards(): pl.pallas_call(kernel, out_shape=(pltpu.VMEM((ROWS, INNER), BF16), pltpu....  47.2 us
    pallas_call x1, Pallas kernels, shards(): pl.pallas_call(front_kernel, out_shape=(pltpu.VMEM((3 * ROWS, INNER), BF1...  6.26 us

profile of v9, /device:TPU:1, one launch (start us, length us, event | category | flops | bytes accessed | tf_op | source)
XLA Modules:
  0.0 55.5 jit_solution(10302769343930809970)
XLA Ops:
  1.3 6.3 %front.1 = (bf16[96,5120]{1,0:T(8,128)(2,1)S(1)}, bf16[192,5120]{1,0:T(8,128)(2,1)S(1)}, bf16[160,5120]{1,0:T(8,128)(2,1)S(1)}, f32[1,5120]{1,0:T(1,128)S(1)}, f32[1024,128]{1,0:T(8,128)S(1)}) custom-call(s32[1,16]{1,0:T(1,128)} %pos.3, s32[1]{0:T(128)S(6)} %copy.13.mode, bf16[32,10240]{1,0:T(8,128)(2,1)} %clean_in.3, bf16[32,10240]{1,0:T(8,128)(2,1)} %corrupt_in.3, ...), custom_call_target="tpu_custom_call" | custom-call | tf_op jit(solution)/shard_map/front/pallas_call | solution.py:711
  7.5 47.2 %mixer.1 = (bf16[32,5120]{1,0:T(8,128)(2,1)S(1)}, f32[40,128]{1,0:T(8,128)S(1)}) custom-call(s32[1,16]{1,0:T(1,128)} %pos.3, s32[1]{0:T(128)S(6)} %copy.13.mode, bf16[96,5120]{1,0:T(8,128)(2,1)S(1)} %get-tuple-element.11.acts, bf16[192,5120]{1,0:T(8,128)(2,1)S(1)} %get-tuple-element.12.x_w, bf16[160,5120]{1,0:T(8,128)(2,1)S(1)} %get-tuple-element.13.dt_w, ...), custom_call_target="tpu_custom_call" | custom-call | tf_op jit(solution)/shard_map/mixer/pallas_call | solution.py:753
  54.8 0.7 %emit.1 = (bf16[32,5120]{1,0:T(8,128)(2,1)}, f32[40,128]{1,0:T(8,128)}) custom-call(bf16[32,5120]{1,0:T(8,128)(2,1)S(1)} %get-tuple-element.16.patched, f32[40,128]{1,0:T(8,128)S(1)} %get-tuple-element.17.effect), custom_call_target="tpu_custom_call" | custom-call | tf_op jit(solution)/shard_map/emit/pallas_call | solution.py:814

commit v10 on v9

--- a/solution.py
+++ b/solution.py
@@ -399,7 +399,7 @@
     swap_ends = to_shard(mate, ends.at[theirs_2], pair_ends, send_pe, recv_pe)
     swap_ends.start()
     local_pass(lax.div(mine, 8))
-    swap_totals.wait()
+    swap_totals.wait_recv()
 
     leads = core == 0
 
@@ -416,7 +416,7 @@
             jnp.where(leads, other_end, own_end), jnp.where(leads, other_total, own_total),
         )
 
-    swap_ends.wait()
+    swap_ends.wait_recv()
 
     def chip_end(k, _):
         end_a, total_a, end_b, total_b = pair_of(k)
@@ -619,7 +619,7 @@
         share(along_z, 8, line_z, chip_squares, squares_z, send_sz, recv_sz)
 
     for direct in directs:
-        direct.wait()
+        direct.wait_recv()
 
     for w in range(VARS):
         def peak_tile(i, _):
@@ -694,6 +694,8 @@
         wait_for(leaving.at[others], send_in)
 
     swap_start.wait_send()
+    for sent in (swap_ends, swap_totals, *directs):
+        sent.wait_send()
 
 
 SMEM = pl.BlockSpec(memory_space=pltpu.SMEM)

time: 55.7 us -> 55.6 us (level)
  no operation moved by 1% of the time
where the time goes in v10:
time: 55.6 us; the launch traced here: 55.5 us
  Pallas kernels  54.2 us (97%)
  between operations  1.29 us (2%)
    pallas_call x1, Pallas kernels, shards(): pl.pallas_call(kernel, out_shape=(pltpu.VMEM((ROWS, INNER), BF16), pltpu....  47.2 us
    pallas_call x1, Pallas kernels, shards(): pl.pallas_call(front_kernel, out_shape=(pltpu.VMEM((3 * ROWS, INNER), BF1...  6.26 us

profile of v10, /device:TPU:1, one launch (start us, length us, event | category | flops | bytes accessed | tf_op | source)
XLA Modules:
  0.0 55.5 jit_solution(9075017794879460372)
XLA Ops:
  1.3 6.3 %front.1 = (bf16[96,5120]{1,0:T(8,128)(2,1)S(1)}, bf16[192,5120]{1,0:T(8,128)(2,1)S(1)}, bf16[160,5120]{1,0:T(8,128)(2,1)S(1)}, f32[1,5120]{1,0:T(1,128)S(1)}, f32[1024,128]{1,0:T(8,128)S(1)}) custom-call(s32[1,16]{1,0:T(1,128)} %pos.3, s32[1]{0:T(128)S(6)} %copy.13.mode, bf16[32,10240]{1,0:T(8,128)(2,1)} %clean_in.3, bf16[32,10240]{1,0:T(8,128)(2,1)} %corrupt_in.3, ...), custom_call_target="tpu_custom_call" | custom-call | tf_op jit(solution)/shard_map/front/pallas_call | solution.py:713
  7.5 47.2 %mixer.1 = (bf16[32,5120]{1,0:T(8,128)(2,1)S(1)}, f32[40,128]{1,0:T(8,128)S(1)}) custom-call(s32[1,16]{1,0:T(1,128)} %pos.3, s32[1]{0:T(128)S(6)} %copy.13.mode, bf16[96,5120]{1,0:T(8,128)(2,1)S(1)} %get-tuple-element.11.acts, bf16[192,5120]{1,0:T(8,128)(2,1)S(1)} %get-tuple-element.12.x_w, bf16[160,5120]{1,0:T(8,128)(2,1)S(1)} %get-tuple-element.13.dt_w, ...), custom_call_target="tpu_custom_call" | custom-call | tf_op jit(solution)/shard_map/mixer/pallas_call | solution.py:755
  54.8 0.7 %emit.1 = (bf16[32,5120]{1,0:T(8,128)(2,1)}, f32[40,128]{1,0:T(8,128)}) custom-call(bf16[32,5120]{1,0:T(8,128)(2,1)S(1)} %get-tuple-element.16.patched, f32[40,128]{1,0:T(8,128)S(1)} %get-tuple-element.17.effect), custom_call_target="tpu_custom_call" | custom-call | tf_op jit(solution)/shard_map/emit/pallas_call | solution.py:816

commit v11 on v9

--- a/solution.py
+++ b/solution.py
@@ -30,7 +30,7 @@
 TINY = 1e-06
 F32 = jnp.float32
 BF16 = jnp.bfloat16
-UNROLL = 8
+UNROLL = 16
 CLEAN, CORRUPT, PATCHED = 0, 1, 2
 STEPS = sorted(
     ((dx, dz) for dx in range(4) for dz in range(8) if dx or dz),

time: 55.7 us -> 55.6 us (level)
  no operation moved by 1% of the time
where the time goes in v11:
time: 55.6 us; the launch traced here: 55.4 us
  Pallas kernels  54.2 us (97%)
  between operations  1.29 us (2%)
    pallas_call x1, Pallas kernels, shards(): pl.pallas_call(kernel, out_shape=(pltpu.VMEM((ROWS, INNER), BF16), pltpu....  47.1 us
    pallas_call x1, Pallas kernels, shards(): pl.pallas_call(front_kernel, out_shape=(pltpu.VMEM((3 * ROWS, INNER), BF1...  6.26 us

profile of v11, /device:TPU:1, one launch (start us, length us, event | category | flops | bytes accessed | tf_op | source)
XLA Modules:
  0.0 55.4 jit_solution(2442878330136773294)
XLA Ops:
  1.3 6.3 %front.1 = (bf16[96,5120]{1,0:T(8,128)(2,1)S(1)}, bf16[192,5120]{1,0:T(8,128)(2,1)S(1)}, bf16[160,5120]{1,0:T(8,128)(2,1)S(1)}, f32[1,5120]{1,0:T(1,128)S(1)}, f32[1024,128]{1,0:T(8,128)S(1)}) custom-call(s32[1,16]{1,0:T(1,128)} %pos.3, s32[1]{0:T(128)S(6)} %copy.13.mode, bf16[32,10240]{1,0:T(8,128)(2,1)} %clean_in.3, bf16[32,10240]{1,0:T(8,128)(2,1)} %corrupt_in.3, ...), custom_call_target="tpu_custom_call" | custom-call | tf_op jit(solution)/shard_map/front/pallas_call | solution.py:711
  7.5 47.1 %mixer.1 = (bf16[32,5120]{1,0:T(8,128)(2,1)S(1)}, f32[40,128]{1,0:T(8,128)S(1)}) custom-call(s32[1,16]{1,0:T(1,128)} %pos.3, s32[1]{0:T(128)S(6)} %copy.13.mode, bf16[96,5120]{1,0:T(8,128)(2,1)S(1)} %get-tuple-element.11.acts, bf16[192,5120]{1,0:T(8,128)(2,1)S(1)} %get-tuple-element.12.x_w, bf16[160,5120]{1,0:T(8,128)(2,1)S(1)} %get-tuple-element.13.dt_w, ...), custom_call_target="tpu_custom_call" | custom-call | tf_op jit(solution)/shard_map/mixer/pallas_call | solution.py:753
  54.7 0.7 %emit.1 = (bf16[32,5120]{1,0:T(8,128)(2,1)}, f32[40,128]{1,0:T(8,128)}) custom-call(bf16[32,5120]{1,0:T(8,128)(2,1)S(1)} %get-tuple-element.16.patched, f32[40,128]{1,0:T(8,128)S(1)} %get-tuple-element.17.effect), custom_call_target="tpu_custom_call" | custom-call | tf_op jit(solution)/shard_map/emit/pallas_call | solution.py:814
